TPU v7x, 256 devices: a whole 4x4x8 slice. The times are simulated.
256 devices in a mesh: dp: 32 (over z, x), mp: 8 (over y, core).
Axes of the slice: x: 4, y: 4, z: 8, core: 2. Of those that a mesh axis runs over, the one named last changes fastest.
Arguments:
- activations: bfloat16 [16384, 3072], P('dp', 'mp'), may hold values from -6 to 6
- out_grads: bfloat16 [16384, 6144], P('dp', 'mp'), may hold values from -0.25 to 0.25
- error: bfloat16 [32, 3072, 6144], P('dp', 'mp'), may hold values from -8 to 8
- sketch: bfloat16 [6144, 64], replicated, may hold values from -0.078125 to 0.078125
- momentum: float32 [3072, 6144], P('mp', 'dp'), may hold values from -6 to 6
Outputs:
- error_new: bfloat16 [32, 3072, 6144], P('dp', 'mp')
- momentum_new: float32 [3072, 6144], P('mp', 'dp')
- next_sketch: bfloat16 [6144, 64], replicated
All inputs are finite; a program needn't handle non-finite values.
Results may differ from a plain program's by a relative error of at most 0.0057.
Values may be sent and summed in bfloat16 or wider, within the bound.
No kernel may reach another device: no remote copies, remote signals or barrier semaphores. Data moves between devices by JAX's collectives and lax.ppermute only.
A program may use at most 64 MiB of HBM per device.

v0:
```python
import jax
import jax.numpy as jnp
from jax import lax
from jax.sharding import Mesh
from jax.sharding import PartitionSpec as P

MP = ("mp_0", "mp_1")
DP = ("dp_0", "dp_1")


beta_decay = 0.9


def cut_along(shard, dim, peers):
    before, after = (shard.shape[:dim], shard.shape[dim + 1 :])
    return jnp.moveaxis(shard.reshape(*before, peers, -1, *after), dim, 0)


def summed_on_arrival(shard, axis, dim):
    blocks = cut_along(shard, dim, lax.axis_size(axis))
    arrived = lax.all_to_all(blocks, axis, split_axis=0, concat_axis=0, tiled=True)
    return arrived.sum(axis=0)


def filled_up(lines, peers):
    spare = -lines.shape[0] % peers
    if not spare:
        return lines
    return jnp.concatenate([lines, jnp.zeros((spare, *lines.shape[1:]), lines.dtype)])


def in_order(blocks, dim):
    blocks = jnp.moveaxis(blocks, 0, dim)
    dims = blocks.shape
    return blocks.reshape(*dims[:dim], dims[dim] * dims[dim + 1], *dims[dim + 2 :])


def copy_for_each(shard, axis):
    copies = jnp.broadcast_to(shard, (lax.axis_size(axis), *shard.shape))
    return lax.all_to_all(copies, axis, split_axis=0, concat_axis=0, tiled=True)


def collect(shard, axis, dim):
    return in_order(copy_for_each(shard, axis), dim)


def nested_sum(shard, axes):
    lines = shard.reshape(-1, shard.shape[-1])
    own = summed_on_arrival(filled_up(lines, lax.axis_size(axes)), axes, 0)
    whole = collect(own, axes, 0)
    return whole[: len(lines)].reshape(shard.shape)


def over_copies(shard, axis):
    return copy_for_each(shard, axis).sum(axis=0)


def gathered_by_axis(shard, axes, dim):
    far, near = axes
    blocks = copy_for_each(copy_for_each(shard, far), near)
    return in_order(blocks.swapaxes(0, 1).reshape(-1, *shard.shape), dim)


def sum_in_two_steps(shard, axes, dim):
    far, near = axes
    own = summed_on_arrival(cut_along(shard, dim, lax.axis_size(far)), near, dim + 1)
    return jnp.sum(lax.all_to_all(own, far, 0, 0, tiled=True), axis=0)


def total_of(shard, axes):
    lines = shard.reshape(-1, shard.shape[-1])
    padded = filled_up(lines, lax.axis_size(axes[0]) * lax.axis_size(axes[1]))
    whole = gathered_by_axis(sum_in_two_steps(padded, axes, 0), axes, 0)
    return lax.slice_in_dim(whole, 0, len(lines)).reshape(shard.shape)


def update_momentum(momentum, basis_rows, sketch_block):
    product = lax.dot_general(
        basis_rows, sketch_block, (((1,), (1,)), ((), ())), preferred_element_type=jnp.float32
    )
    return beta_decay * momentum + product


def local(activations, out_grads, error, sketch, momentum):
    own_error = error[0]
    product = lax.dot_general(
        activations,
        lax.all_gather(out_grads, MP, axis=1, tiled=True),
        (((0,), (0,)), ((), ())),
        preferred_element_type=jnp.float32,
    )
    accumulated = (product + own_error.astype(jnp.float32)).astype(jnp.bfloat16)
    local_left = jnp.dot(accumulated, sketch, preferred_element_type=jnp.float32)
    left_sketch = nested_sum(local_left, DP)
    gram_local = jnp.dot(
        left_sketch.T,
        left_sketch,
        precision=lax.Precision.HIGHEST,
        preferred_element_type=jnp.float32,
    )
    gram_matrix = over_copies(gram_local, MP)
    factor = jnp.linalg.cholesky(gram_matrix)
    basis_rows = jax.scipy.linalg.solve_triangular(factor, left_sketch.T, lower=True).T.astype(
        jnp.bfloat16
    )
    block_width = momentum.shape[1]
    local_right = lax.dot_general(
        accumulated, basis_rows, (((0,), (0,)), ((), ())), preferred_element_type=jnp.float32
    )
    right_sketch = total_of(local_right, (("dp_0", "dp_1"), ("mp_0", "mp_1")))
    next_sketch = right_sketch.astype(jnp.bfloat16)
    sketch_part = lax.dynamic_slice_in_dim(
        next_sketch, lax.axis_index(DP) * block_width, block_width, 0
    )
    momentum_new = update_momentum(momentum, basis_rows, sketch_part)
    decoded = lax.dot_general(
        basis_rows, next_sketch, (((1,), (1,)), ((), ())), preferred_element_type=jnp.float32
    )
    error_new = (accumulated.astype(jnp.float32) - decoded / lax.axis_size(DP)).astype(jnp.bfloat16)
    return (error_new[None], momentum_new, next_sketch)


def solution(mesh):
    split = Mesh(mesh.devices.reshape(8, 4, 4, 2), ("dp_0", "dp_1", "mp_0", "mp_1"))
    placed = (P(DP, MP), P(DP, MP), P(DP, MP, None), P(), P(MP, DP))
    return jax.shard_map(
        local,
        mesh=split,
        in_specs=placed,
        out_specs=(P(DP, MP, None), P(MP, DP), P()),
        check_vma=False,
    )
```

profile of v0, /device:TPU:1, one launch (start us, length us, event | category | flops | bytes accessed | tf_op | source)
XLA Modules:
  0.0 240.9 jit_solution(73632805947021888)
XLA Ops:
  7.2 0.7 all-gather.2.cloned.1.call-update
  7.9 49.6 %all-gather.2.cloned.1.call-done = bf16[512,6144]{1,0:T(8,128)(2,1)} async-done(((bf16[512,768]{1,0:T(8,128)(2,1)}), bf16[512,6144]{1,0:T(8,128)(2,1)}) %all-gather.2.cloned.1.call-update) | async-done | bytes 6291472 | tf_op jit(solution)/shard_map/all_gather | solution.py:88
  57.5 6.9 %fusion = bf16[384,6144]{1,0:T(8,128)(2,1)S(1)} fusion(bf16[512,384]{1,0:T(8,128)(2,1)} %param.5, bf16[512,6144]{1,0:T(8,128)(2,1)} %all-gather.2.cloned.1.call-done, bf16[1,384,6144]{2,1,0:T(8,128)(2,1)} %param.7), kind=kOutput, calls=%fused_computation.1 | convolution fusion | flops 2422996992 | bytes 16121856 | tf_op jit(solution)/shard_map/dot_general | solution.py:86
  64.4 2.2 copy-done.1
  66.6 1.4 fusion.8
  68.0 0.2 reshape.29
  68.2 18.4 %all_to_all.35 = f32[32,1,768]{2,1,0:T(1,128)S(1)} all-to-all(f32[32,1,768]{2,1,0:T(1,128)S(1)} %reshape.29), channel_id=1, replica_groups=mesh['dp_0'=8,'dp_1'=4,'mp_0'=4,'mp_1'=2] {'dp_0','dp_1'}, dimensions={0} | all-to-all | bytes 196608 | tf_op jit(solution)/shard_map/all_to_all | solution.py:21
  86.6 0.5 broadcast.54
  87.1 0.9 reduce.6
  88.0 0.1 reshape.30
  88.2 0.2 reshape.31
  88.3 12.3 %all_to_all.36 = f32[32,1,768]{2,1,0:T(1,128)S(1)} all-to-all(f32[32,1,768]{2,1,0:T(1,128)S(1)} %reshape.31), channel_id=1, replica_groups=mesh['dp_0'=8,'dp_1'=4,'mp_0'=4,'mp_1'=2] {'dp_0','dp_1'}, dimensions={0} | all-to-all | bytes 196608 | tf_op jit(solution)/shard_map/all_to_all | solution.py:40
  100.6 0.9 reduce.7
  101.5 0.1 reshape.32
  101.6 0.5 convolution_bitcast_fusion
  102.2 0.8 reshape.33
  103.0 6.2 %all-to-all-start.2 = ((f32[8,1,4096]{2,1,0:T(1,128)}), f32[8,1,4096]{2,1,0:T(1,128)S(1)}, u32[]{:S(2)}, u32[]{:S(2)}) async-start(f32[8,1,4096]{2,1,0:T(1,128)} %reshape.33), calls=%async_computation.2 | async-start | bytes 262144 | tf_op jit(solution)/shard_map/all_to_all | solution.py:40
  109.2 5.2 %all-to-all-done.2 = f32[8,1,4096]{2,1,0:T(1,128)S(1)} async-done(((f32[8,1,4096]{2,1,0:T(1,128)}), f32[8,1,4096]{2,1,0:T(1,128)S(1)}, u32[]{:S(2)}, u32[]{:S(2)}) %all-to-all-start.2) | async-done | bytes 131104 | tf_op jit(solution)/shard_map/all_to_all | solution.py:40
  114.5 1.0 reduce.8
  115.4 0.1 reshape.34
  115.6 5.8 %cholesky.16 = f32[64,64]{1,0:T(8,128)S(1)} custom-call(f32[64,64]{1,0:T(8,128)S(1)} %fusion.6), custom_call_target="Cholesky" | custom-call | tf_op jit(solution)/shard_map/jit(cholesky)/cholesky | solution.py:102
  121.5 0.6 compare_reduce_fusion
  122.2 0.7 fusion.4
  122.8 4.9 %custom-call.7 = f32[1,64,64]{1,2,0:T(8,128)S(1)} custom-call(f32[1,64,64]{2,1,0:T(8,128)S(1)} %fusion.4), custom_call_target="InvertDiagBlocksLowerTriangular" | custom-call | tf_op jit(solution)/shard_map/jit(_solve_triangular)/triangular_solve | solution.py:103
  127.7 0.4 convolution_convert_fusion
  128.2 3.8 %fusion.9 = f32[6144,64]{1,0:T(8,128)S(1)} fusion(bf16[384,6144]{1,0:T(8,128)(2,1)} %copy-done.1, bf16[384,64]{0,1:T(8,128)(2,1)S(1)} %convolution_convert_fusion), kind=kOutput, calls=%fused_computation.21 | convolution fusion | flops 301989888 | bytes 6340608 | tf_op jit(solution)/shard_map/dot_general | solution.py:107
  132.0 1.9 copy.27
  133.9 3.8 %reshape.35 = f32[8,1,49152]{2,1,0:T(1,128)S(1)} reshape(f32[8,32,24,64]{3,2,1,0:T(8,128)} %copy.27) | data formatting | bytes 3145728
  137.7 24.6 %all_to_all.37 = f32[8,1,49152]{2,1,0:T(1,128)} all-to-all(f32[8,1,49152]{2,1,0:T(1,128)S(1)} %reshape.35), channel_id=1, replica_groups=mesh['dp_0'=8,'dp_1'=4,'mp_0'=4,'mp_1'=2] {'mp_0','mp_1'}, dimensions={0} | all-to-all | bytes 3145728 | tf_op jit(solution)/shard_map/all_to_all | solution.py:21
  162.2 5.8 %reduce.9 = f32[8,49152]{1,0:T(8,128)S(1)} reduce(f32[8,1,49152]{2,1,0:T(1,128)} %all_to_all.37, f32[]{:T(128)} %broadcast.54), dimensions={1}, to_apply=%all_to_all.24.reduce_sub_computation | reduce | bytes 3145732 | tf_op jit(solution)/shard_map/all_to_all | solution.py:21
  168.0 2.9 %reshape.36 = f32[8,32,24,64]{3,2,1,0:T(8,128)} reshape(f32[8,49152]{1,0:T(8,128)S(1)} %reduce.9) | data formatting | bytes 3145728
  171.0 2.1 reduce_sum.38
  173.1 0.2 reshape.37
  173.3 13.0 %all_to_all.38 = f32[32,1,1536]{2,1,0:T(1,128)S(1)} all-to-all(f32[32,1,1536]{2,1,0:T(1,128)S(1)} %reshape.37), channel_id=1, replica_groups=mesh['dp_0'=8,'dp_1'=4,'mp_0'=4,'mp_1'=2] {'dp_0','dp_1'}, dimensions={0} | all-to-all | bytes 393216 | tf_op jit(solution)/shard_map/all_to_all | solution.py:67
  186.3 1.1 reduce.10
  187.4 0.1 reshape.38
  187.6 0.1 reshape.39
  187.8 12.9 %all_to_all.39 = bf16[32,2,768]{2,1,0:T(2,128)(2,1)S(1)} all-to-all(bf16[32,2,768]{2,1,0:T(2,128)(2,1)S(1)} %reshape.39), channel_id=1, replica_groups=mesh['dp_0'=8,'dp_1'=4,'mp_0'=4,'mp_1'=2] {'dp_0','dp_1'}, dimensions={0} | all-to-all | bytes 196608 | tf_op jit(solution)/shard_map/all_to_all | solution.py:40
  200.7 0.2 reshape.40
  200.9 0.2 broadcast_in_dim.20
  201.1 1.9 reshape.41
  203.0 6.9 %all-to-all-start.6 = ((bf16[8,2,24576]{2,1,0:T(2,128)(2,1)}), bf16[8,2,24576]{2,1,0:T(2,128)(2,1)S(1)}, u32[]{:S(2)}, u32[]{:S(2)}) async-start(bf16[8,2,24576]{2,1,0:T(2,128)(2,1)} %reshape.41), calls=%async_computation.6 | async-start | bytes 1572864 | tf_op jit(solution)/shard_map/all_to_all | solution.py:40
  209.9 12.2 %all-to-all-done.6 = bf16[8,2,24576]{2,1,0:T(2,128)(2,1)S(1)} async-done(((bf16[8,2,24576]{2,1,0:T(2,128)(2,1)}), bf16[8,2,24576]{2,1,0:T(2,128)(2,1)S(1)}, u32[]{:S(2)}, u32[]{:S(2)}) %all-to-all-start.6) | async-done | bytes 786464 | tf_op jit(solution)/shard_map/all_to_all | solution.py:40
  222.1 1.9 reshape.42
  224.0 1.8 copy.28
  225.8 6.0 %fusion.1 = bf16[1,384,6144]{2,1,0:T(8,128)(2,1)} fusion(bf16[384,64]{0,1:T(8,128)(2,1)S(1)} %convolution_convert_fusion, bf16[6144,64]{1,0:T(8,128)(2,1)S(1)} %bitcast.33, bf16[384,6144]{1,0:T(8,128)(2,1)} %copy-done.1), kind=kOutput, calls=%fused_computation.3 | convolution fusion | flops 311427072 | bytes 10272768 | tf_op jit(solution)/shard_map/dot_general | solution.py:116
  231.8 1.4 copy.29
  233.2 0.9 convolution_add_fusion
  (17 shorter events, 0.4 us)
Async XLA Ops:
  7.2 59.5 %copy-start = (bf16[6144,64]{0,1:T(8,128)(2,1)S(1)}, bf16[6144,64]{0,1:T(8,128)(2,1)}, u32[]{:S(2)}) copy-start(bf16[6144,64]{0,1:T(8,128)(2,1)} %param.8) | copy-start | bytes 2359300
  7.2 50.3 %all-gather.2.cloned.1.call-start = ((), (), s32[]{:S(2)}) async-start(), calls=%async_computation.7 | async-start | bytes 7077888 | tf_op jit(solution)/shard_map/all_gather | solution.py:88
  64.4 2.2 copy-start.1
  103.0 11.5 %all-to-all-start.2 = ((f32[8,1,4096]{2,1,0:T(1,128)}), f32[8,1,4096]{2,1,0:T(1,128)S(1)}, u32[]{:S(2)}, u32[]{:S(2)}) async-start(f32[8,1,4096]{2,1,0:T(1,128)} %reshape.33), calls=%async_computation.2 | async-start | bytes 262144 | tf_op jit(solution)/shard_map/all_to_all | solution.py:40
  203.0 19.1 %all-to-all-start.6 = ((bf16[8,2,24576]{2,1,0:T(2,128)(2,1)}), bf16[8,2,24576]{2,1,0:T(2,128)(2,1)S(1)}, u32[]{:S(2)}, u32[]{:S(2)}) async-start(bf16[8,2,24576]{2,1,0:T(2,128)(2,1)} %reshape.41), calls=%async_computation.6 | async-start | bytes 1572864 | tf_op jit(solution)/shard_map/all_to_all | solution.py:40
  225.8 7.4 %copy-start.2 = (f32[384,192]{0,1:T(8,128)S(1)}, f32[384,192]{0,1:T(8,128)}, u32[]{:S(2)}) copy-start(f32[384,192]{0,1:T(8,128)} %param.9) | copy-start | bytes 884740
Sparse Core Ops, SparseCore 0:
  9.8 47.6 all-gather.1
where the time goes:
time: 242 us; the launch traced here: 241 us
  blocking collectives  81.1 us (34%)
  waiting for transfers between devices  67.7 us (28%)
  other arithmetic  23.9 us (10%)
  local copies, waits for them, and re-layouts  20.9 us (9%)
  matrix products  20 us (8%)
  between operations  14.3 us (6%)
  starting transfers between devices  13.1 us (5%)
    all_gather x1, waiting for transfers between devices, local(): lax.all_gather(out_grads, MP, axis=1, tiled=True)  49.6 us
    all_to_all x2, blocking collectives, summed_on_arrival(): lax.all_to_all(blocks, axis, split_axis=0, concat_axis=0, tiled=True)  43 us
    all_to_all x2, blocking collectives, copy_for_each(): return lax.all_to_all(copies, axis, split_axis=0, concat_axis=0, tiled=True)  25.2 us
    all_to_all x2, waiting for transfers between devices, copy_for_each(): return lax.all_to_all(copies, axis, split_axis=0, concat_axis=0, tiled=True)  17.4 us
    unnamed x21, local copies, waits for them, and re-layouts  16.3 us
    all_to_all x2, starting transfers between devices, copy_for_each(): return lax.all_to_all(copies, axis, split_axis=0, concat_axis=0, tiled=True)  13.1 us
    all_to_all x1, blocking collectives, sum_in_two_steps(): return jnp.sum(lax.all_to_all(own, far, 0, 0, tiled=True), axis=0)  13 us
    dot_general x1, matrix products, local(): lax.dot_general(activations, lax.all_gather(out_grads, MP, axis=1, tiled=...  6.95 us
  transfers between devices with their start and end apart: 3, of which 3 were waited for; matrix products, arithmetic and copies ran while one was open for 0% of the time, Pallas kernels for 0%

commit v1 on v0

v1 whole, which is shorter than its diff:
```python
import jax
import jax.numpy as jnp
from jax import lax
from jax.experimental import pallas as pl
from jax.experimental.pallas import tpu as pltpu
from jax.sharding import Mesh
from jax.sharding import PartitionSpec as P

DP = ("dp_0", "dp_1")
YY = "mp_0"
CC = "mp_1"
F32 = jnp.float32
BF16 = jnp.bfloat16
HIGHEST = lax.Precision.HIGHEST
D, RANK, ROWS, TOK, COLS, WORKERS = 6144, 64, 384, 512, 768, 32
INTERPRET = False
BETA = 0.9

NN = (((1,), (0,)), ((), ()))
NT = (((1,), (1,)), ((), ()))


def dot(a, b, dims=NN, precision=None):
    return lax.dot_general(a, b, dims, precision=precision, preferred_element_type=F32)


def two_terms(x):
    high = x.astype(BF16)
    low = (x - high.astype(F32)).astype(BF16)
    return jnp.concatenate([high, low], axis=0)


def halves_added(x):
    return x[: x.shape[0] // 2] + x[x.shape[0] // 2 :]


def call(body, out_shape, name, flops, **kw):
    return pl.pallas_call(
        body,
        out_shape=out_shape,
        name=name,
        interpret=INTERPRET,
        cost_estimate=pl.CostEstimate(flops=flops, bytes_accessed=1 << 20, transcendentals=0),
        **kw,
    )


def sds(shape, dtype):
    return jax.ShapeDtypeStruct(shape, dtype)


def grads_sketch_body(ids, grads, sketch, out):
    out[...] = dot(grads[...], sketch[...]).T


def grads_sketch(ids, grads, sketch):
    spec = pltpu.PrefetchScalarGridSpec(
        num_scalar_prefetch=1,
        grid=(1,),
        in_specs=[
            pl.BlockSpec((TOK, COLS), lambda i, s: (0, 0)),
            pl.BlockSpec((COLS, RANK), lambda i, s: (s[0], 0)),
        ],
        out_specs=pl.BlockSpec((RANK, TOK), lambda i, s: (0, 0)),
    )
    return call(grads_sketch_body, sds((RANK, TOK), F32), "grads_sketch", 10**8, grid_spec=spec)(
        ids, grads, sketch
    )


def error_sketch_body(error, sketch, out, acc):
    step = pl.program_id(0)

    @pl.when(step == 0)
    def _():
        acc[...] = jnp.zeros_like(acc)

    acc[...] += dot(error[...], sketch[...])

    @pl.when(step == pl.num_programs(0) - 1)
    def _():
        out[...] = acc[...].T


def error_sketch(error, sketch):
    width = 1536
    return call(
        error_sketch_body,
        sds((RANK, ROWS), F32),
        "error_sketch",
        3 * 10**9,
        grid=(D // width,),
        in_specs=[
            pl.BlockSpec((ROWS, width), lambda i: (0, i)),
            pl.BlockSpec((width, RANK), lambda i: (i, 0)),
        ],
        out_specs=pl.BlockSpec((RANK, ROWS), lambda i: (0, 0)),
        scratch_shapes=[pltpu.VMEM((ROWS, RANK), F32)],
    )(error, sketch)


def left_term_body(own, one, two, three, acts, from_error, out):
    total = own[...] + one[...].astype(F32) + two[...].astype(F32) + three[...].astype(F32)
    left = halves_added(dot(two_terms(total), acts[...])) + from_error[...]
    for r in range(8):
        for j in range(3):
            out[4 * r + j] = left[8 * r : 8 * r + 8, 128 * j : 128 * j + 128]
        out[4 * r + 3] = jnp.zeros((8, 128), F32)


def left_term(own, parts, acts, from_error):
    return call(left_term_body, sds((WORKERS, 8, 128), F32), "left_term", 10**8)(
        own, *parts, acts, from_error
    )


def sum_and_copy_body(arrived, out):
    total = jnp.sum(arrived[...].astype(F32), axis=0).astype(out.dtype)
    out[...] = jnp.broadcast_to(total[None], out.shape)


def sum_and_copy(arrived, dtype, name):
    return call(sum_and_copy_body, sds(arrived.shape, dtype), name, 10**7)(arrived)


def left_products_body(tiles, acts, left_out, left_terms, acts_left_terms, gram):
    rows = [
        jnp.concatenate([tiles[4 * r + j] for j in range(3)], axis=1) for r in range(8)
    ]
    left = jnp.concatenate(rows, axis=0)
    left_out[...] = left
    terms = two_terms(left)
    left_terms[...] = terms
    acts_left_terms[...] = two_terms(halves_added(dot(terms, acts[...], NT)))
    gram[...] = dot(left, left, NT, HIGHEST)


def left_products(tiles, acts):
    return call(
        left_products_body,
        (
            sds((RANK, ROWS), F32),
            sds((2 * RANK, ROWS), BF16),
            sds((2 * RANK, TOK), BF16),
            sds((RANK, RANK), F32),
        ),
        "left_products",
        10**8,
    )(tiles, acts)


def columns(block):
    return pl.ds(pl.multiple_of(block * COLS, COLS), COLS)


def copies_of_grads(pieces, place, sems, first):
    own, up, half_a, half_b, down = pieces
    h = TOK // 2
    return [
        [pltpu.make_async_copy(own, place.at[0], sems.at[first])],
        [pltpu.make_async_copy(up, place.at[1], sems.at[first + 1])],
        [
            pltpu.make_async_copy(half_a, place.at[2, pl.ds(0, h)], sems.at[first + 2]),
            pltpu.make_async_copy(half_b, place.at[2, pl.ds(h, h)], sems.at[first + 3]),
        ],
        [pltpu.make_async_copy(down, place.at[3], sems.at[first + 4])],
    ]


def right_terms_body(
    ids, left_terms, acts_left_terms, error, g0, g1, g2a, g2b, g3, out, held_g, held_e, sems
):
    grads = copies_of_grads((g0, g1, g2a, g2b, g3), held_g, sems, 0)
    errors = [
        pltpu.make_async_copy(error.at[:, columns(ids[k])], held_e.at[k], sems.at[5 + k])
        for k in range(4)
    ]
    for k in range(4):
        errors[k].start()
        for c in grads[k]:
            c.start()
    for k in (0, 1, 3, 2):
        errors[k].wait()
        term = dot(left_terms[...], held_e[k])
        for c in grads[k]:
            c.wait()
        out[k] = halves_added(term + dot(acts_left_terms[...], held_g[k]))


def right_terms(ids, left_terms, acts_left_terms, error, grads, name):
    any_ = pl.BlockSpec(memory_space=pl.ANY)
    vmem = pl.BlockSpec(memory_space=pltpu.VMEM)
    return call(
        right_terms_body,
        sds((4, RANK, COLS), F32),
        name,
        3 * 10**9,
        in_specs=[pl.BlockSpec(memory_space=pltpu.SMEM), vmem, vmem, any_] + [any_] * 5,
        out_specs=vmem,
        scratch_shapes=[
            pltpu.VMEM((4, TOK, COLS), BF16),
            pltpu.VMEM((4, ROWS, COLS), BF16),
            pltpu.SemaphoreType.DMA((9,)),
        ],
    )(ids, left_terms, acts_left_terms, error, *grads)


def add_blocks_body(a, b, o0, o1, o2, o3):
    for k, o in enumerate((o0, o1, o2, o3)):
        o[...] = a[k] + b[k]


def add_blocks(a, b):
    return call(add_blocks_body, (sds((RANK, COLS), F32),) * 4, "add_blocks", 10**8)(a, b)


def factor_body(own, one, two, three, left, inverse_out, basis_out):
    gram = own[...] + one[...] + two[...] + three[...]
    lanes = lax.broadcasted_iota(jnp.int32, (RANK, RANK), 1)
    subs = lax.broadcasted_iota(jnp.int32, (RANK, RANK), 0)
    eye = jnp.where(lanes == subs, 1.0, 0.0).astype(F32)
    work = jnp.concatenate([gram, eye], axis=1)
    rows = lax.broadcasted_iota(jnp.int32, (RANK, 2 * RANK), 0)
    for j in range(RANK - 1):
        row = work[j : j + 1, :]
        ratio = work[:, j : j + 1] / work[j : j + 1, j : j + 1]
        work = work - jnp.where(rows > j, ratio * row, 0.0)
    pivots = jnp.sum(jnp.where(lanes == subs, work[:, :RANK], 0.0), axis=1, keepdims=True)
    inverse = work[:, RANK:] / jnp.sqrt(pivots)
    inverse_out[...] = inverse
    basis_out[...] = dot(inverse, left[...], NN, HIGHEST).T.astype(BF16)


def factor(own, parts, left):
    return call(
        factor_body, (sds((RANK, RANK), F32), sds((ROWS, RANK), BF16)), "factor", 6 * 10**9
    )(own, *parts, left)


def right_term_body(inverse, own, one, two, three, out):
    total = own[...] + one[...] + two[...] + three[...]
    right = dot(inverse[...], total, NN, HIGHEST)
    for j in range(6):
        for r in range(4):
            out[4 * j + r] = right[16 * r : 16 * r + 16, 128 * j : 128 * j + 128].astype(out.dtype)
    out[24:] = jnp.zeros((8, 16, 128), out.dtype)


def right_term(inverse, own, parts):
    return call(right_term_body, sds((WORKERS, 16, 128), F32), "right_term", 10**8)(
        inverse, own, *parts
    )


def fed_body(ids, acts, error, *rest):
    grads, out = rest[:10], rest[10]
    held_g, held_e, held_o, sems, out_sems = rest[11:]
    copies = copies_of_grads(grads[:5], held_g.at[pl.ds(0, 4)], sems, 0) + copies_of_grads(
        grads[5:], held_g.at[pl.ds(4, 4)], sems, 5
    )
    errors = [
        pltpu.make_async_copy(error.at[:, columns(ids[k])], held_e.at[k], sems.at[10 + k])
        for k in range(8)
    ]
    for k in range(8):
        errors[k].start()
        for c in copies[k]:
            c.start()
    turned = acts[...].T
    stores = []
    for k in range(8):
        errors[k].wait()
        for c in copies[k]:
            c.wait()
        held_o[k] = (dot(turned, held_g[k]) + held_e[k].astype(F32)).astype(BF16)
        store = pltpu.make_async_copy(held_o.at[k], out.at[:, columns(ids[k])], out_sems.at[k])
        store.start()
        stores.append(store)
    for store in stores:
        store.wait()


def fed_of(ids, acts, error, grads):
    any_ = pl.BlockSpec(memory_space=pl.ANY)
    vmem = pl.BlockSpec(memory_space=pltpu.VMEM)
    return call(
        fed_body,
        sds((ROWS, D), BF16),
        "fed",
        6 * 10**9,
        in_specs=[pl.BlockSpec(memory_space=pltpu.SMEM), vmem, any_] + [any_] * 10,
        out_specs=any_,
        scratch_shapes=[
            pltpu.VMEM((8, TOK, COLS), BF16),
            pltpu.VMEM((8, ROWS, COLS), BF16),
            pltpu.VMEM((8, ROWS, COLS), BF16),
            pltpu.SemaphoreType.DMA((18,)),
            pltpu.SemaphoreType.DMA((8,)),
        ],
    )(ids, acts, error, *grads)


def outputs_body(ids, fed, basis, *rest):
    blocks, momentum = rest[:8], rest[8]
    error_new, momentum_new, next_sketch, turned = rest[9:]
    step = pl.program_id(0)
    for k in range(8):

        @pl.when(step == k)
        def _():
            for j in range(6):
                for r in range(4):
                    turned[16 * r : 16 * r + 16, 128 * j : 128 * j + 128] = blocks[k][4 * j + r]

    decoded = dot(basis[...], turned[...])
    error_new[0] = (fed[...].astype(F32) - decoded / WORKERS).astype(BF16)
    next_sketch[...] = turned[...].astype(F32).T.astype(BF16)

    @pl.when(ids[step] == ids[8])
    def _():
        first = pl.multiple_of(ids[9] * 192, 64)
        part = next_sketch[pl.ds(first, 192), :]
        momentum_new[...] = BETA * momentum[...] + dot(basis[...], part, NT)


def outputs(ids, fed, basis, blocks, momentum):
    spec = pltpu.PrefetchScalarGridSpec(
        num_scalar_prefetch=1,
        grid=(8,),
        in_specs=[
            pl.BlockSpec((ROWS, COLS), lambda i, s: (0, s[i])),
            pl.BlockSpec((ROWS, RANK), lambda i, s: (0, 0)),
        ]
        + [pl.BlockSpec((24, 16, 128), lambda i, s: (0, 0, 0))] * 8
        + [pl.BlockSpec((ROWS, 192), lambda i, s: (0, 0))],
        out_specs=[
            pl.BlockSpec((1, ROWS, COLS), lambda i, s: (0, 0, s[i])),
            pl.BlockSpec((ROWS, 192), lambda i, s: (0, 0)),
            pl.BlockSpec((COLS, RANK), lambda i, s: (s[i], 0)),
        ],
        scratch_shapes=[pltpu.VMEM((RANK, COLS), BF16)],
    )
    return call(
        outputs_body,
        (sds((1, ROWS, D), BF16), sds((ROWS, 192), F32), sds((D, RANK), BF16)),
        "outputs",
        10**9,
        grid_spec=spec,
    )(ids, fed, basis, *blocks, momentum)


def along_y(x, k):
    return lax.ppermute(x, YY, [(i, (i + k) % 4) for i in range(4)])


def other_core(x):
    return lax.ppermute(x, CC, [(0, 1), (1, 0)])


def to_workers(x):
    return lax.all_to_all(x, DP, split_axis=0, concat_axis=0, tiled=True)


def three_along_y(x):
    return [along_y(x, k) for k in (1, 2, 3)]


def after(x, *others):
    return lax.optimization_barrier((x, *others))[0]


def local(activations, out_grads, error, sketch, momentum):
    own_error = error[0]
    y, c = lax.axis_index(YY), lax.axis_index(CC)
    w = lax.axis_index(DP)
    near = [2 * ((y + k) % 4) + c for k in range(4)]
    far = [2 * ((y + k) % 4) + 1 - c for k in range(4)]
    ids = jnp.stack(near + far + [w // 4, w % 4]).astype(jnp.int32)

    with jax.named_scope("grads_sketch"):
        mine = grads_sketch(ids, out_grads, sketch)
        pair = mine + other_core(mine)
        others = three_along_y(pair.astype(BF16))
    from_error = error_sketch(own_error, sketch)
    tiles = left_term(pair, others, activations, from_error)

    with jax.named_scope("gather_one"):
        held = after(out_grads, *others)
        g3 = along_y(held, 1)
        g1 = along_y(held, -1)
        p0 = other_core(held)

    with jax.named_scope("left_sum"):
        arrived = to_workers(tiles)
    copies = sum_and_copy(arrived, F32, "left_sum")
    with jax.named_scope("gather_two"):
        g1, g3 = lax.optimization_barrier((g1, g3, copies))[:2]
        half = TOK // 2
        g2a = along_y(g1[:half], -1)
        g2b = along_y(g3[half:], 1)
        p1 = other_core(g1)
        p3 = other_core(g3)
    with jax.named_scope("left_copies"):
        tiles = to_workers(copies)
    with jax.named_scope("gather_three"):
        p2a = other_core(g2a)
        p2b = other_core(g2b)

    left, left_terms, acts_left_terms, gram = left_products(tiles, activations)
    with jax.named_scope("gram"):
        gram_pair = gram + other_core(gram)
        gram_parts = three_along_y(gram_pair)
    near_g = (out_grads, g1, g2a, g2b, g3)
    far_g = (p0, p1, p2a, p2b, p3)
    send = right_terms(ids[4:8], left_terms, acts_left_terms, own_error, far_g, "right_far")
    with jax.named_scope("right_core"):
        got = other_core(send)
    keep = right_terms(ids[0:4], left_terms, acts_left_terms, own_error, near_g, "right_near")
    q = add_blocks(keep, got)
    with jax.named_scope("right_y"):
        parts = [along_y(q[k], k) for k in (1, 2, 3)]
    inverse, basis = factor(gram_pair, gram_parts, left)
    fed = fed_of(ids[:8], activations, own_error, near_g + far_g)
    pieces = right_term(inverse, q[0], parts)
    with jax.named_scope("right_sum"):
        arrived = to_workers(pieces)
    copies = sum_and_copy(arrived, BF16, "right_sum")
    with jax.named_scope("right_copies"):
        block = to_workers(copies)[:24]
    with jax.named_scope("spread"):
        n3 = along_y(block, 1)
        n2 = along_y(block, 2)
        n1 = along_y(block, -1)
        near_n = (block, n1, n2, n3)
        far_n = tuple(other_core(n) for n in near_n)
    return outputs(ids, fed, basis, near_n + far_n, momentum)


def solution(mesh):
    split = Mesh(mesh.devices.reshape(8, 4, 4, 2), (*DP, YY, CC))
    mp = (YY, CC)
    return jax.shard_map(
        local,
        mesh=split,
        in_specs=(P(DP, mp), P(DP, mp), P(DP, mp, None), P(), P(mp, DP)),
        out_specs=(P(DP, mp, None), P(mp, DP), P()),
        check_vma=False,
    )
```

time: 242 us -> 187 us (0.77)
  Pallas kernels: 0 us -> 55.7 us
  blocking collectives: 81.1 us -> 28.9 us
  starting transfers between devices: 13.1 us -> 57.2 us
  waiting for transfers between devices: 67.7 us -> 26.4 us
  other arithmetic: 23.9 us -> 2.8 us
  matrix products: 20 us -> 0 us
  between operations: 14.3 us -> 1.06 us
  local copies, waits for them, and re-layouts: 20.9 us -> 14.1 us
    pallas_call x0 -> x13, Pallas kernels: none -> 55.7 us  [the longest x2 10.9 us: right_terms(): call(right_terms_body, sds((4, RANK, COLS), F32), name, 3 * 10 ** 9, in_s...]
    all_to_all x5 -> x2, blocking collectives: 81.1 us -> 28.9 us  [to_workers(): return lax.all_to_all(x, DP, split_axis=0, concat_axis=0, tiled=True)]
    all_gather x1 -> x0, waiting for transfers between devices: 49.6 us -> none  [local(): lax.all_gather(out_grads, MP, axis=1, tiled=True)]
    ppermute x0 -> x28, starting transfers between devices: none -> 41.9 us  [the longest x12 21.2 us: other_core(): return lax.ppermute(x, CC, [(0, 1), (1, 0)])]
    dot_general x6 -> x0, matrix products: 19.5 us -> none  [the longest x1 6.95 us: local(): lax.dot_general(activations, lax.all_gather(out_grads, MP, axis=1, tiled=...]
    another operation x5 -> x2, other arithmetic: 12.1 us -> 1.21 us  [local(): ids = jnp.stack(near + far + [w // 4, w % 4]).astype(jnp.int32)]
    ppermute x0 -> x28, waiting for transfers between devices: none -> 10.3 us  [the longest x16 7.6 us: along_y(): return lax.ppermute(x, YY, [(i, (i + k) % 4) for i in range(4)])]
    all_to_all x5 -> x0, other arithmetic: 9.6 us -> none  [the longest x2 6.67 us: summed_on_arrival(): lax.all_to_all(blocks, axis, split_axis=0, concat_axis=0, tiled=True)]
  transfers between devices with their start and end apart: 3 -> 30, of which waited for: 3 -> 8; matrix products, arithmetic and copies ran while one was open for 0% -> 1% of each run, Pallas kernels for 0% -> 18%
where the time goes in v1:
time: 187 us; the launch traced here: 186 us
  starting transfers between devices  57.2 us (31%)
  Pallas kernels  55.7 us (30%)
  blocking collectives  28.9 us (15%)
  waiting for transfers between devices  26.4 us (14%)
  local copies, waits for them, and re-layouts  14.1 us (8%)
  other arithmetic  2.8 us (1%)
    all_to_all x2, blocking collectives, to_workers(): return lax.all_to_all(x, DP, split_axis=0, concat_axis=0, tiled=True)  28.9 us
    ppermute x12, starting transfers between devices, other_core(): return lax.ppermute(x, CC, [(0, 1), (1, 0)])  21.2 us
    ppermute x16, starting transfers between devices, along_y(): return lax.ppermute(x, YY, [(i, (i + k) % 4) for i in range(4)])  20.6 us
    all_to_all x2, waiting for transfers between devices, to_workers(): return lax.all_to_all(x, DP, split_axis=0, concat_axis=0, tiled=True)  16.1 us
    all_to_all x2, starting transfers between devices, to_workers(): return lax.all_to_all(x, DP, split_axis=0, concat_axis=0, tiled=True)  15.3 us
    pallas_call x2, Pallas kernels, right_terms(): call(right_terms_body, sds((4, RANK, COLS), F32), name, 3 * 10 ** 9, in_s...  10.9 us
    pallas_call x1, Pallas kernels, outputs(): call(outputs_body, (sds((1, ROWS, D), BF16), sds((ROWS, 192), F32), sds((...  9.57 us
    unnamed x56, local copies, waits for them, and re-layouts  8.58 us
  transfers between devices with their start and end apart: 30, of which 8 were waited for; matrix products, arithmetic and copies ran while one was open for 1% of the time, Pallas kernels for 18%

profile of v1, /device:TPU:1, one launch (start us, length us, event | category | flops | bytes accessed | tf_op | source)
XLA Modules:
  0.0 186.2 jit_solution(7459177535761146206)
XLA Ops:
  0.7 2.5 %copy.8.sketch = bf16[6144,64]{1,0:T(8,128)(2,1)} copy(bf16[6144,64]{0,1:T(8,128)(2,1)} %param.8) | data formatting | bytes 1572864 | tf_op args[3]
  3.9 2.9 %grads_sketch.1 = f32[64,512]{1,0:T(8,128)} custom-call(s32[10]{0:T(128)} %stack.49.ids, bf16[512,768]{1,0:T(8,128)(2,1)} %g0.1, bf16[6144,64]{1,0:T(8,128)(2,1)} %copy.8.sketch), custom_call_target="tpu_custom_call" | custom-call | flops 100000000 | bytes 1048576 | tf_op jit(solution)/shard_map/grads_sketch/grads_sketch/pallas_call | solution.py:66
  6.8 3.2 %collective-permute-start = (f32[64,512]{1,0:T(8,128)}, f32[64,512]{1,0:T(8,128)S(1)}, u32[]{:S(2)}, u32[]{:S(2)}) collective-permute-start(f32[64,512]{1,0:T(8,128)} %grads_sketch.1), channel_id=1, source_target_pairs={{0,1},{1,0},{2,3},{3,2},{4,5},{5,4},{6,7},{7,6},{8,9},{9,8},{10,11... | collective-permute-start | bytes 393224 | tf_op jit(solution)/shard_map/grads_sketch/ppermute | solution.py:357
  10.0 1.2 collective-permute-done
  11.2 1.6 fusion
  12.8 1.0 collective-permute-start.3
  14.8 1.0 collective-permute-done.3.three
  15.9 2.6 %collective-permute-done.2.two = bf16[64,512]{1,0:T(8,128)(2,1)S(1)} collective-permute-done((bf16[64,512]{1,0:T(8,128)(2,1)S(1)}, bf16[64,512]{1,0:T(8,128)(2,1)S(1)}, u32[]{:S(2)}, u32[]{:S(2)}) %collective-permute-start.2) | collective-permute-done | bytes 65568 | tf_op jit(solution)/shard_map/grads_sketch/ppermute | solution.py:353
  18.5 1.5 collective-permute-done.1.one
  20.0 2.7 %collective-permute-start.4 = (bf16[512,768]{1,0:T(8,128)(2,1)S(1)}, bf16[512,768]{1,0:T(8,128)(2,1)S(1)}, u32[]{:S(2)}, u32[]{:S(2)}) collective-permute-start(bf16[512,768]{1,0:T(8,128)(2,1)S(1)} %copy-done.1), channel_id=1, source_target_pairs={{0,6},{2,0},{4,2},{6,4},{1,7},{3,1},{5,3},{7,5},{8,14},{10,8},{12,... | collective-permute-start | bytes 2359304 | tf_op jit(solution)/shard_map/gather_one/ppermute | solution.py:353
  22.7 5.1 %error_sketch.1.from_error = f32[64,384]{1,0:T(8,128)} custom-call(bf16[384,6144]{1,0:T(8,128)(2,1)} %bitcast.11, bf16[6144,64]{1,0:T(8,128)(2,1)} %copy.8.sketch), custom_call_target="tpu_custom_call" | custom-call | flops 3000000000 | bytes 1048576 | tf_op jit(solution)/shard_map/error_sketch/pallas_call | solution.py:87
  27.7 2.1 %left_term.1 = f32[32,8,128]{2,1,0:T(8,128)} custom-call(f32[64,512]{1,0:T(8,128)} %get-tuple-element.33.own, bf16[64,512]{1,0:T(8,128)(2,1)} %copy-done.20, bf16[64,512]{1,0:T(8,128)(2,1)} %copy-done.19, bf16[64,512]{1,0:T(8,128)(2,1)} %copy-done.18, bf16[512,384]{1,0:T(8,128)(2,1)} %acts.5, f32[64,384]{1,0:T(8,128)} %error_sketch.1.from_error), custom_call_target="tpu_custom_call" | custom-call | flops 100000000 | bytes 1048576 | tf_op jit(solution)/shard_map/left_term/pallas_call | solution.py:112
  29.8 11.3 %all-to-all-start = ((f32[32,8,128]{2,1,0:T(8,128)}), f32[32,8,128]{2,1,0:T(8,128)S(1)}, u32[]{:S(2)}, u32[]{:S(2)}) async-start(f32[32,8,128]{2,1,0:T(8,128)} %left_term.1), calls=%async_computation | async-start | bytes 262144 | tf_op jit(solution)/shard_map/left_sum/all_to_all | solution.py:361
  41.1 1.9 %collective-permute-start.8 = (bf16[512,768]{1,0:T(8,128)(2,1)S(1)}, bf16[512,768]{1,0:T(8,128)(2,1)S(1)}, u32[]{:S(2)}, u32[]{:S(2)}) collective-permute-start(bf16[512,768]{1,0:T(8,128)(2,1)S(1)} %copy-done.1), channel_id=1, source_target_pairs={{0,1},{1,0},{2,3},{3,2},{4,5},{5,4},{6,7},{7,6},{8,9},{9,8},{10,11... | collective-permute-start | bytes 2359304 | tf_op jit(solution)/shard_map/gather_one/ppermute | solution.py:357
  43.0 7.4 %all-to-all-done.arrived = f32[32,8,128]{2,1,0:T(8,128)S(1)} async-done(((f32[32,8,128]{2,1,0:T(8,128)}), f32[32,8,128]{2,1,0:T(8,128)S(1)}, u32[]{:S(2)}, u32[]{:S(2)}) %all-to-all-start) | async-done | bytes 131104 | tf_op jit(solution)/shard_map/left_sum/all_to_all | solution.py:361
  51.1 1.6 left_sum.1
  52.9 2.7 %collective-permute-start.6 = (bf16[256,768]{1,0:T(8,128)(2,1)S(1)}, bf16[256,768]{1,0:T(8,128)(2,1)}, u32[]{:S(2)}, u32[]{:S(2)}) collective-permute-start(bf16[256,768]{1,0:T(8,128)(2,1)S(1)} %slice.15), channel_id=1, source_target_pairs={{0,6},{2,0},{4,2},{6,4},{1,7},{3,1},{5,3},{7,5},{8,14},{10,8},{12,... | collective-permute-start | bytes 1179656 | tf_op jit(solution)/shard_map/gather_two/ppermute | solution.py:353
  55.6 3.7 %collective-permute-start.9 = (bf16[512,768]{1,0:T(8,128)(2,1)S(1)}, bf16[512,768]{1,0:T(8,128)(2,1)}, u32[]{:S(2)}, u32[]{:S(2)}) collective-permute-start(bf16[512,768]{1,0:T(8,128)(2,1)S(1)} %collective-permute-done.4.rest_1_.g1), channel_id=1, source_target_pairs={{0,1},{1,0},{2,3},{3,2},{4,5},{5,4},{6,7},{7,6},{8,9},{9,8},{10,11... | collective-permute-start | bytes 2359304 | tf_op jit(solution)/shard_map/gather_two/ppermute | solution.py:357
  59.3 2.4 %collective-permute-done.7.rest_3_.g2b = bf16[256,768]{1,0:T(8,128)(2,1)} collective-permute-done((bf16[256,768]{1,0:T(8,128)(2,1)S(1)}, bf16[256,768]{1,0:T(8,128)(2,1)}, u32[]{:S(2)}, u32[]{:S(2)}) %collective-permute-start.7) | collective-permute-done | bytes 393248 | tf_op jit(solution)/shard_map/gather_two/ppermute | solution.py:353
  61.7 4.0 %collective-permute-start.11 = (bf16[256,768]{1,0:T(8,128)(2,1)}, bf16[256,768]{1,0:T(8,128)(2,1)}, u32[]{:S(2)}, u32[]{:S(2)}) collective-permute-start(bf16[256,768]{1,0:T(8,128)(2,1)} %collective-permute-done.7.rest_3_.g2b), channel_id=1, source_target_pairs={{0,1},{1,0},{2,3},{3,2},{4,5},{5,4},{6,7},{7,6},{8,9},{9,8},{10,11... | collective-permute-start | bytes 1179656 | tf_op jit(solution)/shard_map/gather_three/ppermute | solution.py:357
  65.7 4.0 %all-to-all-start.1 = ((f32[32,8,128]{2,1,0:T(8,128)}), f32[32,8,128]{2,1,0:T(8,128)S(1)}, u32[]{:S(2)}, u32[]{:S(2)}) async-start(f32[32,8,128]{2,1,0:T(8,128)} %left_sum.1), calls=%async_computation.1 | async-start | bytes 262144 | tf_op jit(solution)/shard_map/left_copies/all_to_all | solution.py:361
  70.4 8.6 %all-to-all-done.1.tiles = f32[32,8,128]{2,1,0:T(8,128)S(1)} async-done(((f32[32,8,128]{2,1,0:T(8,128)}), f32[32,8,128]{2,1,0:T(8,128)S(1)}, u32[]{:S(2)}, u32[]{:S(2)}) %all-to-all-start.1) | async-done | bytes 131104 | tf_op jit(solution)/shard_map/left_copies/all_to_all | solution.py:361
  79.7 2.0 %left_products.1 = (f32[64,384]{1,0:T(8,128)}, bf16[128,384]{1,0:T(8,128)(2,1)}, bf16[128,512]{1,0:T(8,128)(2,1)}, f32[64,64]{1,0:T(8,128)}) custom-call(f32[32,8,128]{2,1,0:T(8,128)} %copy-done.3, bf16[512,384]{1,0:T(8,128)(2,1)} %acts.5), custom_call_target="tpu_custom_call" | custom-call | flops 100000000 | bytes 1048576 | tf_op jit(solution)/shard_map/left_products/pallas_call | solution.py:139
  81.7 0.8 copy-done.23
  82.6 5.4 %right_far.1 = f32[4,64,768]{2,1,0:T(8,128)} custom-call(s32[4]{0:T(128)} %pad_add_fusion.1.ids, bf16[128,384]{1,0:T(8,128)(2,1)} %get-tuple-element.23.left_terms, bf16[128,512]{1,0:T(8,128)(2,1)} %get-tuple-element.24.acts_left_terms, bf16[384,6144]{1,0:T(8,128)(2,1)} %bitcast.12, bf16[512,768]{1,0:T(8,128)(2,1)} %copy-done.23, ...), custom_call_target="tpu_custom_call" | custom-call | flops 3000000000 | bytes 1048576 | tf_op jit(solution)/shard_map/right_far/pallas_call | solution.py:193
  88.0 2.1 %collective-permute-start.17 = (f32[4,64,768]{2,1,0:T(8,128)}, f32[4,64,768]{2,1,0:T(8,128)S(1)}, u32[]{:S(2)}, u32[]{:S(2)}) collective-permute-start(f32[4,64,768]{2,1,0:T(8,128)} %right_far.1), channel_id=1, source_target_pairs={{0,1},{1,0},{2,3},{3,2},{4,5},{5,4},{6,7},{7,6},{8,9},{9,8},{10,11... | collective-permute-start | bytes 2359304 | tf_op jit(solution)/shard_map/right_core/ppermute | solution.py:357
  90.9 1.5 collective-permute-done.13
  92.4 2.7 %collective-permute-start.16 = (f32[64,64]{1,0:T(8,128)S(1)}, f32[64,64]{1,0:T(8,128)S(1)}, u32[]{:S(2)}, u32[]{:S(2)}) collective-permute-start(f32[64,64]{1,0:T(8,128)S(1)} %add.84.own), channel_id=1, source_target_pairs={{0,6},{2,0},{4,2},{6,4},{1,7},{3,1},{5,3},{7,5},{8,14},{10,8},{12,... | collective-permute-start | bytes 49160 | tf_op jit(solution)/shard_map/gram/ppermute | solution.py:353
  95.8 5.5 %right_near.1.a = f32[4,64,768]{2,1,0:T(8,128)} custom-call(s32[4]{0:T(128)} %pad_add_fusion.ids, bf16[128,384]{1,0:T(8,128)(2,1)} %get-tuple-element.23.left_terms, bf16[128,512]{1,0:T(8,128)(2,1)} %get-tuple-element.24.acts_left_terms, bf16[384,6144]{1,0:T(8,128)(2,1)} %bitcast.13, bf16[512,768]{1,0:T(8,128)(2,1)} %g0.1, bf16[512,768]{1,0:T(8,128)(2,1)} %copy-done.7, ...), custom_call_target="tpu_custom_call" | custom-call | flops 3000000000 | bytes 1048576 | tf_op jit(solution)/shard_map/right_near/pallas_call | solution.py:193
  101.3 0.9 copy-done
  102.2 2.3 %add_blocks.1 = (f32[64,768]{1,0:T(8,128)}, f32[64,768]{1,0:T(8,128)}, f32[64,768]{1,0:T(8,128)}, f32[64,768]{1,0:T(8,128)}) custom-call(f32[4,64,768]{2,1,0:T(8,128)} %right_near.1.a, f32[4,64,768]{2,1,0:T(8,128)} %copy-done), custom_call_target="tpu_custom_call" | custom-call | flops 100000000 | bytes 1048576 | tf_op jit(solution)/shard_map/add_blocks/pallas_call | solution.py:214
  104.4 2.0 %collective-permute-start.18 = (f32[64,768]{1,0:T(8,128)}, f32[64,768]{1,0:T(8,128)S(1)}, u32[]{:S(2)}, u32[]{:S(2)}) collective-permute-start(f32[64,768]{1,0:T(8,128)} %get-tuple-element.26), channel_id=1, source_target_pairs={{0,2},{2,4},{4,6},{6,0},{1,3},{3,5},{5,7},{7,1},{8,10},{10,12},{12... | collective-permute-start | bytes 589832 | tf_op jit(solution)/shard_map/right_y/ppermute | solution.py:353
  106.4 1.2 collective-permute-start.19
  107.6 1.2 collective-permute-start.20
  109.4 7.4 %factor.1 = (f32[64,64]{1,0:T(8,128)}, bf16[384,64]{1,0:T(8,128)(2,1)}) custom-call(f32[64,64]{1,0:T(8,128)} %copy-done.21, f32[64,64]{1,0:T(8,128)} %copy-done.26, f32[64,64]{1,0:T(8,128)} %copy-done.25, f32[64,64]{1,0:T(8,128)} %copy-done.24, f32[64,384]{1,0:T(8,128)} %get-tuple-element.20.left), custom_call_target="tpu_custom_call" | custom-call | flops 6000000000 | bytes 1048576 | tf_op jit(solution)/shard_map/factor/pallas_call | solution.py:235
  117.7 2.2 %right_term.1 = f32[32,16,128]{2,1,0:T(8,128)} custom-call(f32[64,64]{1,0:T(8,128)} %get-tuple-element.22.inverse, f32[64,768]{1,0:T(8,128)} %get-tuple-element.25.own, f32[64,768]{1,0:T(8,128)} %copy-done.8, f32[64,768]{1,0:T(8,128)} %copy-done.9, f32[64,768]{1,0:T(8,128)} %copy-done.10), custom_call_target="tpu_custom_call" | custom-call | flops 100000000 | bytes 1048576 | tf_op jit(solution)/shard_map/right_term/pallas_call | solution.py:250
  119.9 15.1 %all_to_all.20.arrived = f32[32,16,128]{2,1,0:T(8,128)} all-to-all(f32[32,16,128]{2,1,0:T(8,128)} %right_term.1), channel_id=1, replica_groups=mesh['dp_0'=8,'dp_1'=4,'mp_0'=4,'mp_1'=2] {'dp_0','dp_1'}, dimensions={0} | all-to-all | bytes 524288 | tf_op jit(solution)/shard_map/right_sum/all_to_all | solution.py:361
  135.0 1.6 right_sum.1
  136.7 13.8 %all_to_all.21 = bf16[32,16,128]{2,1,0:T(8,128)(2,1)S(1)} all-to-all(bf16[32,16,128]{2,1,0:T(8,128)(2,1)} %right_sum.1), channel_id=1, replica_groups=mesh['dp_0'=8,'dp_1'=4,'mp_0'=4,'mp_1'=2] {'dp_0','dp_1'}, dimensions={0} | all-to-all | bytes 262144 | tf_op jit(solution)/shard_map/right_copies/all_to_all | solution.py:361
  150.5 2.8 %collective-permute-start.23 = (bf16[24,16,128]{2,1,0:T(8,128)(2,1)S(1)}, bf16[24,16,128]{2,1,0:T(8,128)(2,1)S(1)}, u32[]{:S(2)}, u32[]{:S(2)}) collective-permute-start(bf16[24,16,128]{2,1,0:T(8,128)(2,1)S(1)} %slice.18.rest_0_), channel_id=1, source_target_pairs={{0,2},{2,4},{4,6},{6,0},{1,3},{3,5},{5,7},{7,1},{8,10},{10,12},{12... | collective-permute-start | bytes 294920 | tf_op jit(solution)/shard_map/spread/ppermute | solution.py:353
  153.3 1.9 %collective-permute-start.22 = (bf16[24,16,128]{2,1,0:T(8,128)(2,1)S(1)}, bf16[24,16,128]{2,1,0:T(8,128)(2,1)S(1)}, u32[]{:S(2)}, u32[]{:S(2)}) collective-permute-start(bf16[24,16,128]{2,1,0:T(8,128)(2,1)S(1)} %slice.18.rest_0_), channel_id=1, source_target_pairs={{0,4},{2,6},{4,0},{6,2},{1,5},{3,7},{5,1},{7,3},{8,12},{10,14},{12... | collective-permute-start | bytes 294920 | tf_op jit(solution)/shard_map/spread/ppermute | solution.py:353
  156.4 0.9 copy.10.rest_8_
  157.3 3.7 %collective-permute-start.24 = (bf16[24,16,128]{2,1,0:T(8,128)(2,1)S(1)}, bf16[24,16,128]{2,1,0:T(8,128)(2,1)S(1)}, u32[]{:S(2)}, u32[]{:S(2)}) collective-permute-start(bf16[24,16,128]{2,1,0:T(8,128)(2,1)S(1)} %slice.18.rest_0_), channel_id=1, source_target_pairs={{0,1},{1,0},{2,3},{3,2},{4,5},{5,4},{6,7},{7,6},{8,9},{9,8},{10,11... | collective-permute-start | bytes 294920 | tf_op jit(solution)/shard_map/spread/ppermute | solution.py:357
  161.1 1.7 collective-permute-start.26
  163.6 8.0 %fed.1 = bf16[384,6144]{1,0:T(8,128)(2,1)} custom-call(s32[8]{0:T(128)} %stack.50.ids, bf16[512,384]{1,0:T(8,128)(2,1)} %acts.5, bf16[384,6144]{1,0:T(8,128)(2,1)} %bitcast.14, bf16[512,768]{1,0:T(8,128)(2,1)} %g0.1, bf16[512,768]{1,0:T(8,128)(2,1)} %copy-done.7, bf16[256,768]{1,0:T(8,128)(2,1)} %collective-permute-done.6.rest_2_.g2a, ...), custom_call_target="tpu_custom_call" | custom-call | flops 6000000000 | bytes 1048576 | tf_op jit(solution)/shard_map/fed/pallas_call | solution.py:286
  172.3 9.6 %outputs.1 = (bf16[1,384,6144]{2,1,0:T(8,128)(2,1)}, f32[384,192]{1,0:T(8,128)}, bf16[6144,64]{1,0:T(8,128)(2,1)}) custom-call(s32[10]{0:T(128)} %stack.49.ids, bf16[384,6144]{1,0:T(8,128)(2,1)} %fed.1, bf16[384,64]{1,0:T(8,128)(2,1)} %get-tuple-element.21.basis, bf16[24,16,128]{2,1,0:T(8,128)(2,1)} %copy-done.4, bf16[24,16,128]{2,1,0:T(8,128)(2,1)} %copy-done.13, ...), custom_call_target="tpu_custom_call" | custom-call | flops 1000000000 | bytes 1048576 | tf_op jit(solution)/shard_map/outputs/pallas_call | solution.py:343
  181.9 1.9 copy.11
  183.8 2.4 %copy.12 = bf16[6144,64]{0,1:T(8,128)(2,1)} copy(bf16[6144,64]{1,0:T(8,128)(2,1)} %get-tuple-element.31) | data formatting | bytes 1572864 | tf_op jit(solution)/shard_map/outputs/pallas_call | solution.py:343
  (94 shorter events, 9.4 us)
Async XLA Ops:
  0.6 19.3 %copy-start.1 = (bf16[512,768]{1,0:T(8,128)(2,1)S(1)}, bf16[512,768]{1,0:T(8,128)(2,1)}, u32[]{:S(2)}) copy-start(bf16[512,768]{1,0:T(8,128)(2,1)} %g0.1) | copy-start | bytes 2359300
  6.8 4.4 %collective-permute-start = (f32[64,512]{1,0:T(8,128)}, f32[64,512]{1,0:T(8,128)S(1)}, u32[]{:S(2)}, u32[]{:S(2)}) collective-permute-start(f32[64,512]{1,0:T(8,128)} %grads_sketch.1), channel_id=1, source_target_pairs={{0,1},{1,0},{2,3},{3,2},{4,5},{5,4},{6,7},{7,6},{8,9},{9,8},{10,11... | collective-permute-start | bytes 393224 | tf_op jit(solution)/shard_map/grads_sketch/ppermute | solution.py:357
  12.8 3.1 %collective-permute-start.3 = (bf16[64,512]{1,0:T(8,128)(2,1)S(1)}, bf16[64,512]{1,0:T(8,128)(2,1)S(1)}, u32[]{:S(2)}, u32[]{:S(2)}) collective-permute-start(bf16[64,512]{1,0:T(8,128)(2,1)S(1)} %get-tuple-element.32), channel_id=1, source_target_pairs={{0,6},{2,0},{4,2},{6,4},{1,7},{3,1},{5,3},{7,5},{8,14},{10,8},{12,... | collective-permute-start | bytes 196616 | tf_op jit(solution)/shard_map/grads_sketch/ppermute | solution.py:353
  13.8 4.7 %collective-permute-start.2 = (bf16[64,512]{1,0:T(8,128)(2,1)S(1)}, bf16[64,512]{1,0:T(8,128)(2,1)S(1)}, u32[]{:S(2)}, u32[]{:S(2)}) collective-permute-start(bf16[64,512]{1,0:T(8,128)(2,1)S(1)} %get-tuple-element.32), channel_id=1, source_target_pairs={{0,4},{2,6},{4,0},{6,2},{1,5},{3,7},{5,1},{7,3},{8,12},{10,14},{12... | collective-permute-start | bytes 196616 | tf_op jit(solution)/shard_map/grads_sketch/ppermute | solution.py:353
  14.1 5.8 %collective-permute-start.1 = (bf16[64,512]{1,0:T(8,128)(2,1)S(1)}, bf16[64,512]{1,0:T(8,128)(2,1)S(1)}, u32[]{:S(2)}, u32[]{:S(2)}) collective-permute-start(bf16[64,512]{1,0:T(8,128)(2,1)S(1)} %get-tuple-element.32), channel_id=1, source_target_pairs={{0,2},{2,4},{4,6},{6,0},{1,3},{3,5},{5,7},{7,1},{8,10},{10,12},{12... | collective-permute-start | bytes 196616 | tf_op jit(solution)/shard_map/grads_sketch/ppermute | solution.py:353
  15.9 11.8 %copy-start.18 = (bf16[64,512]{1,0:T(8,128)(2,1)}, bf16[64,512]{1,0:T(8,128)(2,1)S(1)}, u32[]{:S(2)}) copy-start(bf16[64,512]{1,0:T(8,128)(2,1)S(1)} %collective-permute-done.3.three) | copy-start | bytes 196612
  18.5 9.2 %copy-start.19 = (bf16[64,512]{1,0:T(8,128)(2,1)}, bf16[64,512]{1,0:T(8,128)(2,1)S(1)}, u32[]{:S(2)}) copy-start(bf16[64,512]{1,0:T(8,128)(2,1)S(1)} %collective-permute-done.2.two) | copy-start | bytes 196612
  20.0 7.7 %copy-start.20 = (bf16[64,512]{1,0:T(8,128)(2,1)}, bf16[64,512]{1,0:T(8,128)(2,1)S(1)}, u32[]{:S(2)}) copy-start(bf16[64,512]{1,0:T(8,128)(2,1)S(1)} %collective-permute-done.1.one) | copy-start | bytes 196612
  20.0 32.7 %collective-permute-start.5 = (bf16[512,768]{1,0:T(8,128)(2,1)S(1)}, bf16[512,768]{1,0:T(8,128)(2,1)S(1)}, u32[]{:S(2)}, u32[]{:S(2)}) collective-permute-start(bf16[512,768]{1,0:T(8,128)(2,1)S(1)} %copy-done.1), channel_id=1, source_target_pairs={{0,2},{2,4},{4,6},{6,0},{1,3},{3,5},{5,7},{7,1},{8,10},{10,12},{12... | collective-permute-start | bytes 2359304 | tf_op jit(solution)/shard_map/gather_one/ppermute | solution.py:353
  20.0 32.7 %collective-permute-start.4 = (bf16[512,768]{1,0:T(8,128)(2,1)S(1)}, bf16[512,768]{1,0:T(8,128)(2,1)S(1)}, u32[]{:S(2)}, u32[]{:S(2)}) collective-permute-start(bf16[512,768]{1,0:T(8,128)(2,1)S(1)} %copy-done.1), channel_id=1, source_target_pairs={{0,6},{2,0},{4,2},{6,4},{1,7},{3,1},{5,3},{7,5},{8,14},{10,8},{12,... | collective-permute-start | bytes 2359304 | tf_op jit(solution)/shard_map/gather_one/ppermute | solution.py:353
  29.8 20.7 %all-to-all-start = ((f32[32,8,128]{2,1,0:T(8,128)}), f32[32,8,128]{2,1,0:T(8,128)S(1)}, u32[]{:S(2)}, u32[]{:S(2)}) async-start(f32[32,8,128]{2,1,0:T(8,128)} %left_term.1), calls=%async_computation | async-start | bytes 262144 | tf_op jit(solution)/shard_map/left_sum/all_to_all | solution.py:361
  41.1 40.6 %collective-permute-start.8 = (bf16[512,768]{1,0:T(8,128)(2,1)S(1)}, bf16[512,768]{1,0:T(8,128)(2,1)S(1)}, u32[]{:S(2)}, u32[]{:S(2)}) collective-permute-start(bf16[512,768]{1,0:T(8,128)(2,1)S(1)} %copy-done.1), channel_id=1, source_target_pairs={{0,1},{1,0},{2,3},{3,2},{4,5},{5,4},{6,7},{7,6},{8,9},{9,8},{10,11... | collective-permute-start | bytes 2359304 | tf_op jit(solution)/shard_map/gather_one/ppermute | solution.py:357
  52.7 35.3 %copy-start.6 = (bf16[512,768]{1,0:T(8,128)(2,1)}, bf16[512,768]{1,0:T(8,128)(2,1)S(1)}, u32[]{:S(2)}) copy-start(bf16[512,768]{1,0:T(8,128)(2,1)S(1)} %collective-permute-done.5.rest_4_.g3) | copy-start | bytes 2359300
  52.7 35.3 %copy-start.7 = (bf16[512,768]{1,0:T(8,128)(2,1)}, bf16[512,768]{1,0:T(8,128)(2,1)S(1)}, u32[]{:S(2)}) copy-start(bf16[512,768]{1,0:T(8,128)(2,1)S(1)} %collective-permute-done.4.rest_1_.g1) | copy-start | bytes 2359300
  52.8 9.0 %collective-permute-start.7 = (bf16[256,768]{1,0:T(8,128)(2,1)S(1)}, bf16[256,768]{1,0:T(8,128)(2,1)}, u32[]{:S(2)}, u32[]{:S(2)}) collective-permute-start(bf16[256,768]{1,0:T(8,128)(2,1)S(1)} %slice.16), channel_id=1, source_target_pairs={{0,2},{2,4},{4,6},{6,0},{1,3},{3,5},{5,7},{7,1},{8,10},{10,12},{12... | collective-permute-start | bytes 1179656 | tf_op jit(solution)/shard_map/gather_two/ppermute | solution.py:353
  52.9 12.8 %collective-permute-start.6 = (bf16[256,768]{1,0:T(8,128)(2,1)S(1)}, bf16[256,768]{1,0:T(8,128)(2,1)}, u32[]{:S(2)}, u32[]{:S(2)}) collective-permute-start(bf16[256,768]{1,0:T(8,128)(2,1)S(1)} %slice.15), channel_id=1, source_target_pairs={{0,6},{2,0},{4,2},{6,4},{1,7},{3,1},{5,3},{7,5},{8,14},{10,8},{12,... | collective-permute-start | bytes 1179656 | tf_op jit(solution)/shard_map/gather_two/ppermute | solution.py:353
  55.6 26.1 %collective-permute-start.9 = (bf16[512,768]{1,0:T(8,128)(2,1)S(1)}, bf16[512,768]{1,0:T(8,128)(2,1)}, u32[]{:S(2)}, u32[]{:S(2)}) collective-permute-start(bf16[512,768]{1,0:T(8,128)(2,1)S(1)} %collective-permute-done.4.rest_1_.g1), channel_id=1, source_target_pairs={{0,1},{1,0},{2,3},{3,2},{4,5},{5,4},{6,7},{7,6},{8,9},{9,8},{10,11... | collective-permute-start | bytes 2359304 | tf_op jit(solution)/shard_map/gather_two/ppermute | solution.py:357
  59.3 22.4 %collective-permute-start.12 = (bf16[512,768]{1,0:T(8,128)(2,1)S(1)}, bf16[512,768]{1,0:T(8,128)(2,1)}, u32[]{:S(2)}, u32[]{:S(2)}) collective-permute-start(bf16[512,768]{1,0:T(8,128)(2,1)S(1)} %collective-permute-done.5.rest_4_.g3), channel_id=1, source_target_pairs={{0,1},{1,0},{2,3},{3,2},{4,5},{5,4},{6,7},{7,6},{8,9},{9,8},{10,11... | collective-permute-start | bytes 2359304 | tf_op jit(solution)/shard_map/gather_two/ppermute | solution.py:357
  61.7 20.0 %collective-permute-start.11 = (bf16[256,768]{1,0:T(8,128)(2,1)}, bf16[256,768]{1,0:T(8,128)(2,1)}, u32[]{:S(2)}, u32[]{:S(2)}) collective-permute-start(bf16[256,768]{1,0:T(8,128)(2,1)} %collective-permute-done.7.rest_3_.g2b), channel_id=1, source_target_pairs={{0,1},{1,0},{2,3},{3,2},{4,5},{5,4},{6,7},{7,6},{8,9},{9,8},{10,11... | collective-permute-start | bytes 1179656 | tf_op jit(solution)/shard_map/gather_three/ppermute | solution.py:357
  65.7 16.0 %collective-permute-start.10 = (bf16[256,768]{1,0:T(8,128)(2,1)}, bf16[256,768]{1,0:T(8,128)(2,1)}, u32[]{:S(2)}, u32[]{:S(2)}) collective-permute-start(bf16[256,768]{1,0:T(8,128)(2,1)} %collective-permute-done.6.rest_2_.g2a), channel_id=1, source_target_pairs={{0,1},{1,0},{2,3},{3,2},{4,5},{5,4},{6,7},{7,6},{8,9},{9,8},{10,11... | collective-permute-start | bytes 1179656 | tf_op jit(solution)/shard_map/gather_three/ppermute | solution.py:357
  65.7 13.3 %all-to-all-start.1 = ((f32[32,8,128]{2,1,0:T(8,128)}), f32[32,8,128]{2,1,0:T(8,128)S(1)}, u32[]{:S(2)}, u32[]{:S(2)}) async-start(f32[32,8,128]{2,1,0:T(8,128)} %left_sum.1), calls=%async_computation.1 | async-start | bytes 262144 | tf_op jit(solution)/shard_map/left_copies/all_to_all | solution.py:361
  81.7 0.9 copy-start.23
  82.6 7.6 %copy-start.22 = (f32[64,64]{1,0:T(8,128)S(1)}, f32[64,64]{1,0:T(8,128)}, u32[]{:S(2)}) copy-start(f32[64,64]{1,0:T(8,128)} %get-tuple-element.19) | copy-start | bytes 49156
  88.0 13.2 %collective-permute-start.17 = (f32[4,64,768]{2,1,0:T(8,128)}, f32[4,64,768]{2,1,0:T(8,128)S(1)}, u32[]{:S(2)}, u32[]{:S(2)}) collective-permute-start(f32[4,64,768]{2,1,0:T(8,128)} %right_far.1), channel_id=1, source_target_pairs={{0,1},{1,0},{2,3},{3,2},{4,5},{5,4},{6,7},{7,6},{8,9},{9,8},{10,11... | collective-permute-start | bytes 2359304 | tf_op jit(solution)/shard_map/right_core/ppermute | solution.py:357
  90.2 2.2 %collective-permute-start.13 = (f32[64,64]{1,0:T(8,128)S(1)}, f32[64,64]{1,0:T(8,128)S(1)}, u32[]{:S(2)}, u32[]{:S(2)}) collective-permute-start(f32[64,64]{1,0:T(8,128)S(1)} %copy-done.22), channel_id=1, source_target_pairs={{0,1},{1,0},{2,3},{3,2},{4,5},{5,4},{6,7},{7,6},{8,9},{9,8},{10,11... | collective-permute-start | bytes 49160 | tf_op jit(solution)/shard_map/gram/ppermute | solution.py:357
  92.4 8.9 %copy-start.21 = (f32[64,64]{1,0:T(8,128)}, f32[64,64]{1,0:T(8,128)S(1)}, u32[]{:S(2)}) copy-start(f32[64,64]{1,0:T(8,128)S(1)} %add.84.own) | copy-start | bytes 49156
  92.4 15.2 %collective-permute-start.16 = (f32[64,64]{1,0:T(8,128)S(1)}, f32[64,64]{1,0:T(8,128)S(1)}, u32[]{:S(2)}, u32[]{:S(2)}) collective-permute-start(f32[64,64]{1,0:T(8,128)S(1)} %add.84.own), channel_id=1, source_target_pairs={{0,6},{2,0},{4,2},{6,4},{1,7},{3,1},{5,3},{7,5},{8,14},{10,8},{12,... | collective-permute-start | bytes 49160 | tf_op jit(solution)/shard_map/gram/ppermute | solution.py:353
  95.1 13.7 %collective-permute-start.15 = (f32[64,64]{1,0:T(8,128)S(1)}, f32[64,64]{1,0:T(8,128)S(1)}, u32[]{:S(2)}, u32[]{:S(2)}) collective-permute-start(f32[64,64]{1,0:T(8,128)S(1)} %add.84.own), channel_id=1, source_target_pairs={{0,4},{2,6},{4,0},{6,2},{1,5},{3,7},{5,1},{7,3},{8,12},{10,14},{12... | collective-permute-start | bytes 49160 | tf_op jit(solution)/shard_map/gram/ppermute | solution.py:353
  95.1 13.7 %collective-permute-start.14 = (f32[64,64]{1,0:T(8,128)S(1)}, f32[64,64]{1,0:T(8,128)S(1)}, u32[]{:S(2)}, u32[]{:S(2)}) collective-permute-start(f32[64,64]{1,0:T(8,128)S(1)} %add.84.own), channel_id=1, source_target_pairs={{0,2},{2,4},{4,6},{6,0},{1,3},{3,5},{5,7},{7,1},{8,10},{10,12},{12... | collective-permute-start | bytes 49160 | tf_op jit(solution)/shard_map/gram/ppermute | solution.py:353
  101.3 0.9 copy-start
  104.4 12.4 %collective-permute-start.18 = (f32[64,768]{1,0:T(8,128)}, f32[64,768]{1,0:T(8,128)S(1)}, u32[]{:S(2)}, u32[]{:S(2)}) collective-permute-start(f32[64,768]{1,0:T(8,128)} %get-tuple-element.26), channel_id=1, source_target_pairs={{0,2},{2,4},{4,6},{6,0},{1,3},{3,5},{5,7},{7,1},{8,10},{10,12},{12... | collective-permute-start | bytes 589832 | tf_op jit(solution)/shard_map/right_y/ppermute | solution.py:353
  106.4 10.4 %collective-permute-start.19 = (f32[64,768]{1,0:T(8,128)}, f32[64,768]{1,0:T(8,128)S(1)}, u32[]{:S(2)}, u32[]{:S(2)}) collective-permute-start(f32[64,768]{1,0:T(8,128)} %get-tuple-element.27), channel_id=1, source_target_pairs={{0,4},{2,6},{4,0},{6,2},{1,5},{3,7},{5,1},{7,3},{8,12},{10,14},{12... | collective-permute-start | bytes 589832 | tf_op jit(solution)/shard_map/right_y/ppermute | solution.py:353
  107.6 1.2 copy-start.24
  107.6 9.2 %collective-permute-start.20 = (f32[64,768]{1,0:T(8,128)}, f32[64,768]{1,0:T(8,128)S(1)}, u32[]{:S(2)}, u32[]{:S(2)}) collective-permute-start(f32[64,768]{1,0:T(8,128)} %get-tuple-element.28), channel_id=1, source_target_pairs={{0,6},{2,0},{4,2},{6,4},{1,7},{3,1},{5,3},{7,5},{8,14},{10,8},{12,... | collective-permute-start | bytes 589832 | tf_op jit(solution)/shard_map/right_y/ppermute | solution.py:353
  109.4 46.9 %copy-start.5 = (f32[384,192]{0,1:T(8,128)S(1)}, f32[384,192]{0,1:T(8,128)}, u32[]{:S(2)}) copy-start(f32[384,192]{0,1:T(8,128)} %param.9) | copy-start | bytes 884740
  116.8 0.7 copy-start.9
  116.9 0.8 copy-start.10
  150.5 21.0 %copy-start.4 = (bf16[24,16,128]{2,1,0:T(8,128)(2,1)}, bf16[24,16,128]{2,1,0:T(8,128)(2,1)S(1)}, u32[]{:S(2)}) copy-start(bf16[24,16,128]{2,1,0:T(8,128)(2,1)S(1)} %slice.18.rest_0_) | copy-start | bytes 294916
  150.5 10.5 %collective-permute-start.23 = (bf16[24,16,128]{2,1,0:T(8,128)(2,1)S(1)}, bf16[24,16,128]{2,1,0:T(8,128)(2,1)S(1)}, u32[]{:S(2)}, u32[]{:S(2)}) collective-permute-start(bf16[24,16,128]{2,1,0:T(8,128)(2,1)S(1)} %slice.18.rest_0_), channel_id=1, source_target_pairs={{0,2},{2,4},{4,6},{6,0},{1,3},{3,5},{5,7},{7,1},{8,10},{10,12},{12... | collective-permute-start | bytes 294920 | tf_op jit(solution)/shard_map/spread/ppermute | solution.py:353
  153.3 7.8 %collective-permute-start.22 = (bf16[24,16,128]{2,1,0:T(8,128)(2,1)S(1)}, bf16[24,16,128]{2,1,0:T(8,128)(2,1)S(1)}, u32[]{:S(2)}, u32[]{:S(2)}) collective-permute-start(bf16[24,16,128]{2,1,0:T(8,128)(2,1)S(1)} %slice.18.rest_0_), channel_id=1, source_target_pairs={{0,4},{2,6},{4,0},{6,2},{1,5},{3,7},{5,1},{7,3},{8,12},{10,14},{12... | collective-permute-start | bytes 294920 | tf_op jit(solution)/shard_map/spread/ppermute | solution.py:353
  155.2 7.7 %collective-permute-start.21 = (bf16[24,16,128]{2,1,0:T(8,128)(2,1)S(1)}, bf16[24,16,128]{2,1,0:T(8,128)(2,1)S(1)}, u32[]{:S(2)}, u32[]{:S(2)}) collective-permute-start(bf16[24,16,128]{2,1,0:T(8,128)(2,1)S(1)} %slice.18.rest_0_), channel_id=1, source_target_pairs={{0,6},{2,0},{4,2},{6,4},{1,7},{3,1},{5,3},{7,5},{8,14},{10,8},{12,... | collective-permute-start | bytes 294920 | tf_op jit(solution)/shard_map/spread/ppermute | solution.py:353
  157.3 14.3 %collective-permute-start.24 = (bf16[24,16,128]{2,1,0:T(8,128)(2,1)S(1)}, bf16[24,16,128]{2,1,0:T(8,128)(2,1)S(1)}, u32[]{:S(2)}, u32[]{:S(2)}) collective-permute-start(bf16[24,16,128]{2,1,0:T(8,128)(2,1)S(1)} %slice.18.rest_0_), channel_id=1, source_target_pairs={{0,1},{1,0},{2,3},{3,2},{4,5},{5,4},{6,7},{7,6},{8,9},{9,8},{10,11... | collective-permute-start | bytes 294920 | tf_op jit(solution)/shard_map/spread/ppermute | solution.py:357
  161.0 10.6 %copy-start.11 = (bf16[24,16,128]{2,1,0:T(8,128)(2,1)}, bf16[24,16,128]{2,1,0:T(8,128)(2,1)S(1)}, u32[]{:S(2)}) copy-start(bf16[24,16,128]{2,1,0:T(8,128)(2,1)S(1)} %collective-permute-done.23.rest_3_) | copy-start | bytes 294916
  161.0 10.6 %collective-permute-start.27 = (bf16[24,16,128]{2,1,0:T(8,128)(2,1)S(1)}, bf16[24,16,128]{2,1,0:T(8,128)(2,1)S(1)}, u32[]{:S(2)}, u32[]{:S(2)}) collective-permute-start(bf16[24,16,128]{2,1,0:T(8,128)(2,1)S(1)} %collective-permute-done.23.rest_3_), channel_id=1, source_target_pairs={{0,1},{1,0},{2,3},{3,2},{4,5},{5,4},{6,7},{7,6},{8,9},{9,8},{10,11... | collective-permute-start | bytes 294920 | tf_op jit(solution)/shard_map/spread/ppermute | solution.py:357
  161.1 10.5 %copy-start.12 = (bf16[24,16,128]{2,1,0:T(8,128)(2,1)}, bf16[24,16,128]{2,1,0:T(8,128)(2,1)S(1)}, u32[]{:S(2)}) copy-start(bf16[24,16,128]{2,1,0:T(8,128)(2,1)S(1)} %collective-permute-done.22.rest_2_) | copy-start | bytes 294916
  161.1 10.5 %collective-permute-start.26 = (bf16[24,16,128]{2,1,0:T(8,128)(2,1)S(1)}, bf16[24,16,128]{2,1,0:T(8,128)(2,1)S(1)}, u32[]{:S(2)}, u32[]{:S(2)}) collective-permute-start(bf16[24,16,128]{2,1,0:T(8,128)(2,1)S(1)} %collective-permute-done.22.rest_2_), channel_id=1, source_target_pairs={{0,1},{1,0},{2,3},{3,2},{4,5},{5,4},{6,7},{7,6},{8,9},{9,8},{10,11... | collective-permute-start | bytes 294920 | tf_op jit(solution)/shard_map/spread/ppermute | solution.py:357
  162.9 8.7 %copy-start.13 = (bf16[24,16,128]{2,1,0:T(8,128)(2,1)}, bf16[24,16,128]{2,1,0:T(8,128)(2,1)S(1)}, u32[]{:S(2)}) copy-start(bf16[24,16,128]{2,1,0:T(8,128)(2,1)S(1)} %collective-permute-done.21.rest_1_) | copy-start | bytes 294916
  162.9 8.8 %collective-permute-start.25 = (bf16[24,16,128]{2,1,0:T(8,128)(2,1)S(1)}, bf16[24,16,128]{2,1,0:T(8,128)(2,1)S(1)}, u32[]{:S(2)}, u32[]{:S(2)}) collective-permute-start(bf16[24,16,128]{2,1,0:T(8,128)(2,1)S(1)} %collective-permute-done.21.rest_1_), channel_id=1, source_target_pairs={{0,1},{1,0},{2,3},{3,2},{4,5},{5,4},{6,7},{7,6},{8,9},{9,8},{10,11... | collective-permute-start | bytes 294920 | tf_op jit(solution)/shard_map/spread/ppermute | solution.py:357
  (9 other events, 5.8 us)

commit v2 on v0

v2 whole, which is shorter than its diff:
```python
import jax
import jax.numpy as jnp
from jax import lax
from jax.experimental import pallas as pl
from jax.experimental.pallas import tpu as pltpu
from jax.sharding import Mesh
from jax.sharding import PartitionSpec as P


DP = ("dp_0", "dp_1")
YY = "mp_0"
CC = "mp_1"
F32 = jnp.float32
BF16 = jnp.bfloat16
HIGHEST = lax.Precision.HIGHEST
D, RANK, ROWS, TOK, COLS, WORKERS = 6144, 64, 384, 512, 768, 32
INTERPRET = False
BETA = 0.9

NN = (((1,), (0,)), ((), ()))
NT = (((1,), (1,)), ((), ()))


def dot(a, b, dims=NN, precision=None):
    return lax.dot_general(a, b, dims, precision=precision, preferred_element_type=F32)


def two_terms(x):
    high = x.astype(BF16)
    low = (x - high.astype(F32)).astype(BF16)
    return jnp.concatenate([high, low], axis=0)


def halves_added(x):
    return x[: x.shape[0] // 2] + x[x.shape[0] // 2 :]


def call(body, out_shape, flops, **kw):
    return pl.pallas_call(
        body,
        out_shape=out_shape,
        interpret=INTERPRET,
        cost_estimate=pl.CostEstimate(flops=flops, bytes_accessed=1 << 20, transcendentals=0),
        **kw,
    )


def sds(shape, dtype):
    return jax.ShapeDtypeStruct(shape, dtype)


VMEM = pl.BlockSpec(memory_space=pltpu.VMEM)
HBM = pl.BlockSpec(memory_space=pltpu.HBM)


def block_at(ahead, other):
    y, c = lax.axis_index(YY), lax.axis_index(CC)
    return 2 * lax.rem(y + ahead, 4) + (1 - c if other else c)


def columns(block):
    return pl.ds(pl.multiple_of(block * COLS, COLS), COLS)


def grads_sketch_body(grads, sketch_t, out, held, sem):
    cut = pltpu.make_async_copy(sketch_t.at[:, columns(block_at(0, False))], held, sem)
    cut.start()
    cut.wait()
    out[...] = dot(held[...], grads[...], NT)


def grads_sketch(grads, sketch_t):
    return call(
        grads_sketch_body,
        sds((RANK, TOK), F32),
        10**8,
        in_specs=[VMEM, HBM],
        out_specs=VMEM,
        scratch_shapes=[pltpu.VMEM((RANK, COLS), BF16), pltpu.SemaphoreType.DMA(())],
    )(grads, sketch_t)


def pair_body(a, b, out, rounded):
    total = a[...] + b[...]
    out[...] = total
    rounded[...] = total.astype(BF16)


def pair_sum(a, b):
    return call(pair_body, (sds(a.shape, F32), sds(a.shape, BF16)), 10**7)(a, b)


def error_sketch_body(error, sketch_t, out, held, sems):
    parts = 8
    width = D // parts
    copies = [
        pltpu.make_async_copy(error.at[:, pl.ds(k * width, width)], held.at[k], sems.at[k])
        for k in range(parts)
    ]
    for c in copies:
        c.start()
    acc = jnp.zeros((RANK, ROWS), F32)
    for k in range(parts):
        copies[k].wait()
        acc = acc + dot(sketch_t[:, k * width : (k + 1) * width], held[k], NT)
    out[...] = acc


def error_sketch(error, sketch_t):
    return call(
        error_sketch_body,
        sds((RANK, ROWS), F32),
        3 * 10**9,
        in_specs=[HBM, VMEM],
        out_specs=VMEM,
        scratch_shapes=[pltpu.VMEM((8, ROWS, D // 8), BF16), pltpu.SemaphoreType.DMA((8,))],
    )(error, sketch_t)


def left_term_body(own, one, two, three, acts, from_error, out):
    total = own[...] + one[...].astype(F32) + two[...].astype(F32) + three[...].astype(F32)
    left = halves_added(dot(two_terms(total), acts[...])) + from_error[...]
    for r in range(8):
        for j in range(3):
            out[4 * r + j] = left[8 * r : 8 * r + 8, 128 * j : 128 * j + 128]
        out[4 * r + 3] = jnp.zeros((8, 128), F32)


def left_term(own, parts, acts, from_error):
    return call(left_term_body, sds((WORKERS, 8, 128), F32), 10**8)(own, *parts, acts, from_error)


def sum_and_copy_body(arrived, out):
    total = jnp.sum(arrived[...].astype(F32), axis=0).astype(out.dtype)
    out[...] = jnp.broadcast_to(total[None], out.shape)


def sum_and_copy(arrived, dtype):
    return call(sum_and_copy_body, sds(arrived.shape, dtype), 10**7)(arrived)


def left_products_body(tiles, acts, left_out, left_terms, small):
    rows = [jnp.concatenate([tiles[4 * r + j] for j in range(3)], axis=1) for r in range(8)]
    left = jnp.concatenate(rows, axis=0)
    left_out[...] = left
    terms = two_terms(left)
    left_terms[...] = terms
    small[:, :TOK] = halves_added(dot(terms, acts[...], NT))
    gram = dot(left, left, NT, HIGHEST)
    small[:, TOK:] = jnp.concatenate([gram, jnp.zeros_like(gram)], axis=1)


def left_products(tiles, acts):
    return call(
        left_products_body,
        (
            sds((RANK, ROWS), F32),
            sds((2 * RANK, ROWS), BF16),
            sds((RANK, TOK + 128), F32),
        ),
        10**8,
    )(tiles, acts)


def right_blocks(other, left_terms, error, held, sems, store):
    copies = [
        pltpu.make_async_copy(error.at[:, columns(block_at(k, other))], held.at[k], sems.at[k])
        for k in range(4)
    ]
    for c in copies:
        c.start()
    for k in range(4):
        copies[k].wait()
        store(k, halves_added(dot(left_terms[...], held[k])))


def right_far_body(left_terms, error, out, held, sems):
    def store(k, block):
        out[k] = block

    right_blocks(True, left_terms, error, held, sems, store)


def right_near_body(left_terms, error, got, o0, o1, o2, o3, held, sems):
    outs = (o0, o1, o2, o3)

    def store(k, block):
        outs[k][...] = block + got[k]

    right_blocks(False, left_terms, error, held, sems, store)


RIGHT_SCRATCH = [pltpu.VMEM((4, ROWS, COLS), BF16), pltpu.SemaphoreType.DMA((4,))]


def right_far(left_terms, error):
    return call(
        right_far_body,
        sds((4, RANK, COLS), F32),
        10**9,
        in_specs=[VMEM, HBM],
        out_specs=VMEM,
        scratch_shapes=RIGHT_SCRATCH,
    )(left_terms, error)


def right_near(left_terms, error, got):
    return call(
        right_near_body,
        (sds((RANK, COLS), F32),) * 4,
        10**9,
        in_specs=[VMEM, HBM, VMEM],
        out_specs=(VMEM,) * 4,
        scratch_shapes=RIGHT_SCRATCH,
    )(left_terms, error, got)


def factor_body(own, one, two, three, left, inverse_out, basis_out, acts_left):
    small = own[...] + one[...] + two[...] + three[...]
    acts_left[...] = two_terms(small[:, :TOK])
    lanes = lax.broadcasted_iota(jnp.int32, (RANK, RANK), 1)
    subs = lax.broadcasted_iota(jnp.int32, (RANK, RANK), 0)
    eye = jnp.where(lanes == subs, 1.0, 0.0).astype(F32)
    work = jnp.concatenate([small[:, TOK : TOK + RANK], eye], axis=1)
    rows = lax.broadcasted_iota(jnp.int32, (RANK, 2 * RANK), 0)
    for j in range(RANK - 1):
        row = work[j : j + 1, :]
        ratio = work[:, j : j + 1] / work[j : j + 1, j : j + 1]
        work = work - jnp.where(rows > j, ratio * row, 0.0)
    pivots = jnp.sum(jnp.where(lanes == subs, work[:, :RANK], 0.0), axis=1, keepdims=True)
    inverse = work[:, RANK:] / jnp.sqrt(pivots)
    inverse_out[...] = inverse
    basis_out[...] = dot(inverse, left[...], NN, HIGHEST).T.astype(BF16)


def factor(own, parts, left):
    return call(
        factor_body,
        (sds((RANK, RANK), F32), sds((ROWS, RANK), BF16), sds((2 * RANK, TOK), BF16)),
        6 * 10**9,
    )(own, *parts, left)


def right_term_body(inverse, acts_left, grads, own, one, two, three, out):
    total = own[...] + one[...] + two[...] + three[...]
    total = total + halves_added(dot(acts_left[...], grads[...]))
    right = dot(inverse[...], total, NN, HIGHEST)
    for j in range(6):
        for r in range(4):
            out[4 * j + r] = right[16 * r : 16 * r + 16, 128 * j : 128 * j + 128].astype(out.dtype)
    out[24:] = jnp.zeros((8, 16, 128), out.dtype)


def right_term(inverse, acts_left, grads, own, parts):
    return call(right_term_body, sds((WORKERS, 16, 128), BF16), 10**8)(
        inverse, acts_left, grads, own, *parts
    )


def fed_body(acts, error, *rest):
    grads, out = rest[:8], rest[8]
    held_g, held_e, sems = rest[9:]
    loads = [
        pltpu.make_async_copy(grads[k], held_g.at[k], sems.at[k]) for k in range(8)
    ]
    errors = [
        pltpu.make_async_copy(
            error.at[:, columns(block_at(k % 4, k >= 4))], held_e.at[k], sems.at[8 + k]
        )
        for k in range(8)
    ]
    for k in range(8):
        errors[k].start()
        loads[k].start()
    turned = acts[...].T
    for k in range(8):
        errors[k].wait()
        loads[k].wait()
        out[k] = (dot(turned, held_g[k]) + held_e[k].astype(F32)).astype(BF16)


def fed_of(acts, error, grads):
    return call(
        fed_body,
        sds((8, ROWS, COLS), BF16),
        6 * 10**9,
        in_specs=[VMEM, HBM] + [HBM] * 8,
        out_specs=VMEM,
        scratch_shapes=[
            pltpu.VMEM((8, TOK, COLS), BF16),
            pltpu.VMEM((8, ROWS, COLS), BF16),
            pltpu.SemaphoreType.DMA((16,)),
        ],
    )(acts, error, *grads)


def outputs_body(fed, basis, *rest):
    blocks, momentum_t = rest[:8], rest[8]
    error_new, momentum_new_t, sketch_t = rest[9:12]
    held, turned, sems = rest[12:]
    w = lax.axis_index(DP)
    stores = []
    for k in range(8):
        where = block_at(k % 4, k >= 4)
        rows = [
            jnp.concatenate([blocks[k][4 * j + r] for j in range(6)], axis=1) for r in range(4)
        ]
        block = jnp.concatenate(rows, axis=0)
        decoded = dot(basis[...], block)
        held[k] = (fed[k].astype(F32) - decoded / WORKERS).astype(BF16)
        store = pltpu.make_async_copy(held.at[k], error_new.at[0, :, columns(where)], sems.at[k])
        store.start()
        stores.append(store)
        sketch_t[:, columns(where)] = block

        @pl.when(where == w // 4)
        def _():
            turned[...] = block.astype(F32).T
            first = pl.multiple_of(lax.rem(w, 4) * 192, 64)
            part = turned[pl.ds(first, 192), :].astype(BF16)
            momentum_new_t[...] = BETA * momentum_t[...] + dot(part, basis[...], NT)

    for store in stores:
        store.wait()


def outputs(fed, basis, blocks, momentum_t):
    return call(
        outputs_body,
        (sds((1, ROWS, D), BF16), sds((192, ROWS), F32), sds((RANK, D), BF16)),
        10**9,
        in_specs=[VMEM] * 11,
        out_specs=(HBM, VMEM, VMEM),
        scratch_shapes=[
            pltpu.VMEM((8, ROWS, COLS), BF16),
            pltpu.VMEM((COLS, RANK), F32),
            pltpu.SemaphoreType.DMA((8,)),
        ],
    )(fed, basis, *blocks, momentum_t)


def along_y(x, k):
    return lax.ppermute(x, YY, [(i, (i + k) % 4) for i in range(4)])


def other_core(x):
    return lax.ppermute(x, CC, [(0, 1), (1, 0)])


def to_workers(x):
    return lax.all_to_all(x, DP, split_axis=0, concat_axis=0, tiled=True)


def after(x, *others):
    return lax.optimization_barrier((x, *others))[0]


def step(activations, out_grads, error, sketch, momentum):
    own_error = error[0]
    sketch_t = sketch.T

    mine = grads_sketch(out_grads, sketch_t)
    pair, rounded = pair_sum(mine, other_core(mine))
    others = []
    for k in (1, 2, 3):
        others.append(along_y(rounded, k))
    from_error = error_sketch(own_error, sketch_t)
    tiles = left_term(pair, others, activations, from_error)

    held = after(out_grads, *others)
    gathered = []
    for k in (1, 2, 3):
        gathered.append(along_y(held, -k % 4))

    arrived = to_workers(tiles)
    copies = sum_and_copy(arrived, F32)
    tiles = to_workers(copies)

    left, left_terms, small = left_products(tiles, activations)
    small = small + other_core(small)
    small_parts = [along_y(small, k) for k in (1, 2, 3)]
    send = right_far(left_terms, own_error)
    got = other_core(send)
    q = right_near(left_terms, own_error, got)
    parts = [along_y(q[k], k) for k in (1, 2, 3)]
    inverse, basis, acts_left = factor(small, small_parts, left)
    pieces = right_term(inverse, acts_left, out_grads, q[0], parts)

    near_g = (out_grads, *gathered)
    far_g = []
    for k in range(4):
        far_g.append(other_core(after(near_g[k], pieces)))
    arrived = to_workers(pieces)
    copies = sum_and_copy(arrived, BF16)
    fed = fed_of(activations, own_error, (*near_g, *far_g))
    block = to_workers(copies)[:24]
    n3, n2, n1 = along_y(block, 1), along_y(block, 2), along_y(block, -1)
    near_n = (block, n1, n2, n3)
    far_n = tuple(other_core(n) for n in near_n)
    error_new, momentum_t, sketch_t = outputs(fed, basis, near_n + far_n, momentum.T)
    return error_new, momentum_t.T, sketch_t.T


def solution(mesh):
    split = Mesh(mesh.devices.reshape(8, 4, 4, 2), (*DP, YY, CC))
    mp = (YY, CC)
    return jax.shard_map(
        step,
        mesh=split,
        in_specs=(P(DP, mp), P(DP, mp), P(DP, mp, None), P(), P(mp, DP)),
        out_specs=(P(DP, mp, None), P(mp, DP), P()),
        check_vma=False,
    )
```

time: 242 us -> 202 us (0.83)
  Pallas kernels: 0 us -> 52.5 us
  blocking collectives: 81.1 us -> 48 us
  starting transfers between devices: 13.1 us -> 37.4 us
  other arithmetic: 23.9 us -> 0.02 us
  matrix products: 20 us -> 0 us
  local copies, waits for them, and re-layouts: 20.9 us -> 4.3 us
  between operations: 14.3 us -> 1.11 us
  waiting for transfers between devices: 67.7 us -> 58.2 us
    pallas_call x0 -> x13, Pallas kernels: none -> 52.5 us  [the longest x1 9.22 us: fed_of(): call(fed_body, sds((8, ROWS, COLS), BF16), 6 * 10 ** 9, in_specs=[VMEM, H...]
    ppermute x0 -> x26, waiting for transfers between devices: none -> 51.5 us  [the longest x15 48 us: along_y(): return lax.ppermute(x, YY, [(i, (i + k) % 4) for i in range(4)])]
    all_gather x1 -> x0, waiting for transfers between devices: 49.6 us -> none  [local(): lax.all_gather(out_grads, MP, axis=1, tiled=True)]
    ppermute x0 -> x26, starting transfers between devices: none -> 33.6 us  [the longest x11 17.2 us: other_core(): return lax.ppermute(x, CC, [(0, 1), (1, 0)])]
    all_to_all x5 -> x3, blocking collectives: 81.1 us -> 48 us  [to_workers(): return lax.all_to_all(x, DP, split_axis=0, concat_axis=0, tiled=True)]
    dot_general x6 -> x0, matrix products: 19.5 us -> none  [the longest x1 6.95 us: local(): lax.dot_general(activations, lax.all_gather(out_grads, MP, axis=1, tiled=...]
    another operation x5 -> x0, other arithmetic: 12.1 us -> none  [the longest x3 6.52 us: local(): factor = jnp.linalg.cholesky(gram_matrix)]
    unnamed x21 -> x48, local copies, waits for them, and re-layouts: 16.3 us -> 4.29 us
  transfers between devices with their start and end apart: 3 -> 27, of which waited for: 3 -> 8; matrix products, arithmetic and copies ran while one was open for 0% -> 0% of each run, Pallas kernels for 0% -> 15%
where the time goes in v2:
time: 202 us
  waiting for transfers between devices  58.2 us (29%)
  Pallas kernels  52.5 us (26%)
  blocking collectives  48 us (24%)
  starting transfers between devices  37.4 us (19%)
  local copies, waits for them, and re-layouts  4.3 us (2%)
    ppermute x15, waiting for transfers between devices, along_y(): return lax.ppermute(x, YY, [(i, (i + k) % 4) for i in range(4)])  48 us
    all_to_all x3, blocking collectives, to_workers(): return lax.all_to_all(x, DP, split_axis=0, concat_axis=0, tiled=True)  48 us
    ppermute x11, starting transfers between devices, other_core(): return lax.ppermute(x, CC, [(0, 1), (1, 0)])  17.2 us
    ppermute x15, starting transfers between devices, along_y(): return lax.ppermute(x, YY, [(i, (i + k) % 4) for i in range(4)])  16.3 us
    pallas_call x1, Pallas kernels, fed_of(): call(fed_body, sds((8, ROWS, COLS), BF16), 6 * 10 ** 9, in_specs=[VMEM, H...  9.22 us
    pallas_call x1, Pallas kernels, factor(): call(factor_body, (sds((RANK, RANK), F32), sds((ROWS, RANK), BF16), sds((...  7.74 us
    pallas_call x1, Pallas kernels, outputs(): call(outputs_body, (sds((1, ROWS, D), BF16), sds((192, ROWS), F32), sds((...  7.18 us
    all_to_all x1, waiting for transfers between devices, to_workers(): return lax.all_to_all(x, DP, split_axis=0, concat_axis=0, tiled=True)  6.72 us
  transfers between devices with their start and end apart: 27, of which 8 were waited for; matrix products, arithmetic and copies ran while one was open for 0% of the time, Pallas kernels for 15%

profile of v2, /device:TPU:1, one launch (start us, length us, event | category | flops | bytes accessed | tf_op | source)
XLA Modules:
  0.0 201.5 jit_solution(2426950287892385103)
XLA Ops:
  0.6 3.0 %shard_map.76.a = f32[64,512]{1,0:T(8,128)} custom-call(bf16[512,768]{1,0:T(8,128)(2,1)} %rest_0_.1, bf16[64,6144]{1,0:T(8,128)(2,1)} %bitcast.9), custom_call_target="tpu_custom_call" | custom-call | flops 100000000 | bytes 1048576 | tf_op jit(solution)/shard_map/pallas_call | solution.py:73
  3.7 3.3 %collective-permute-start = (f32[64,512]{1,0:T(8,128)}, f32[64,512]{1,0:T(8,128)S(1)}, u32[]{:S(2)}, u32[]{:S(2)}) collective-permute-start(f32[64,512]{1,0:T(8,128)} %shard_map.76.a), channel_id=1, source_target_pairs={{0,1},{1,0},{2,3},{3,2},{4,5},{5,4},{6,7},{7,6},{8,9},{9,8},{10,11... | collective-permute-start | bytes 393224 | tf_op jit(solution)/shard_map/ppermute | solution.py:347
  7.0 1.2 collective-permute-done.b
  8.2 0.7 copy-done.8
  8.8 1.7 shard_map.77
  10.5 1.0 collective-permute-start.3
  11.5 0.3 collective-permute-start.2
  11.9 0.7 collective-permute-start.1
  12.6 5.2 %shard_map.78.from_error = f32[64,384]{1,0:T(8,128)} custom-call(bf16[384,6144]{1,0:T(8,128)(2,1)} %bitcast.5, bf16[64,6144]{1,0:T(8,128)(2,1)} %bitcast.10), custom_call_target="tpu_custom_call" | custom-call | flops 3000000000 | bytes 1048576 | tf_op jit(solution)/shard_map/pallas_call | solution.py:110
  17.9 0.5 copy-done.16
  18.5 2.1 %shard_map.79 = f32[32,8,128]{2,1,0:T(8,128)} custom-call(f32[64,512]{1,0:T(8,128)} %get-tuple-element.25.own, bf16[64,512]{1,0:T(8,128)(2,1)} %copy-done.18, bf16[64,512]{1,0:T(8,128)(2,1)} %copy-done.17, bf16[64,512]{1,0:T(8,128)(2,1)} %copy-done.16, bf16[512,384]{1,0:T(8,128)(2,1)} %acts.5, f32[64,384]{1,0:T(8,128)} %shard_map.78.from_error), custom_call_target="tpu_custom_call" | custom-call | flops 100000000 | bytes 1048576 | tf_op jit(solution)/shard_map/pallas_call | solution.py:130
  20.6 20.8 %all_to_all.20.arrived = f32[32,8,128]{2,1,0:T(8,128)} all-to-all(f32[32,8,128]{2,1,0:T(8,128)} %shard_map.79), channel_id=1, replica_groups=mesh['dp_0'=8,'dp_1'=4,'mp_0'=4,'mp_1'=2] {'dp_0','dp_1'}, dimensions={0} | all-to-all | bytes 262144 | tf_op jit(solution)/shard_map/all_to_all | solution.py:351
  41.4 1.6 shard_map.80
  43.0 13.9 %all_to_all.21.tiles = f32[32,8,128]{2,1,0:T(8,128)} all-to-all(f32[32,8,128]{2,1,0:T(8,128)} %shard_map.80), channel_id=1, replica_groups=mesh['dp_0'=8,'dp_1'=4,'mp_0'=4,'mp_1'=2] {'dp_0','dp_1'}, dimensions={0} | all-to-all | bytes 262144 | tf_op jit(solution)/shard_map/all_to_all | solution.py:351
  57.0 2.1 %shard_map.81 = (f32[64,384]{1,0:T(8,128)}, bf16[128,384]{1,0:T(8,128)(2,1)}, f32[64,640]{1,0:T(8,128)}) custom-call(f32[32,8,128]{2,1,0:T(8,128)} %all_to_all.21.tiles, bf16[512,384]{1,0:T(8,128)(2,1)} %acts.5), custom_call_target="tpu_custom_call" | custom-call | flops 100000000 | bytes 1048576 | tf_op jit(solution)/shard_map/pallas_call | solution.py:154
  59.1 4.1 %shard_map.83 = f32[4,64,768]{2,1,0:T(8,128)} custom-call(bf16[128,384]{1,0:T(8,128)(2,1)} %get-tuple-element.30.left_terms, bf16[384,6144]{1,0:T(8,128)(2,1)} %bitcast.6), custom_call_target="tpu_custom_call" | custom-call | flops 1000000000 | bytes 1048576 | tf_op jit(solution)/shard_map/pallas_call | solution.py:197
  63.2 3.6 %collective-permute-start.11 = (f32[4,64,768]{2,1,0:T(8,128)}, f32[4,64,768]{2,1,0:T(8,128)S(1)}, u32[]{:S(2)}, u32[]{:S(2)}) collective-permute-start(f32[4,64,768]{2,1,0:T(8,128)} %shard_map.83), channel_id=1, source_target_pairs={{0,1},{1,0},{2,3},{3,2},{4,5},{5,4},{6,7},{7,6},{8,9},{9,8},{10,11... | collective-permute-start | bytes 2359304 | tf_op jit(solution)/shard_map/ppermute | solution.py:347
  66.9 2.2 %collective-permute-done.7 = f32[64,640]{1,0:T(8,128)S(1)} collective-permute-done((f32[64,640]{1,0:T(8,128)S(1)}, f32[64,640]{1,0:T(8,128)S(1)}, u32[]{:S(2)}, u32[]{:S(2)}) %collective-permute-start.7) | collective-permute-done | bytes 163872 | tf_op jit(solution)/shard_map/ppermute | solution.py:347
  69.2 2.0 collective-permute-start.10
  71.2 1.4 collective-permute-start.9
  72.6 1.9 collective-permute-start.5
  74.5 0.9 copy-done
  75.4 4.2 %shard_map.84 = (f32[64,768]{1,0:T(8,128)}, f32[64,768]{1,0:T(8,128)}, f32[64,768]{1,0:T(8,128)}, f32[64,768]{1,0:T(8,128)}) custom-call(bf16[128,384]{1,0:T(8,128)(2,1)} %get-tuple-element.30.left_terms, bf16[384,6144]{1,0:T(8,128)(2,1)} %bitcast.7, f32[4,64,768]{2,1,0:T(8,128)} %copy-done), custom_call_target="tpu_custom_call" | custom-call | flops 1000000000 | bytes 1048576 | tf_op jit(solution)/shard_map/pallas_call | solution.py:208
  79.6 1.4 collective-permute-start.12
  81.0 1.3 collective-permute-start.4
  82.5 37.7 %collective-permute-done.8.one = f32[64,640]{1,0:T(8,128)S(1)} collective-permute-done((f32[64,640]{1,0:T(8,128)S(1)}, f32[64,640]{1,0:T(8,128)S(1)}, u32[]{:S(2)}, u32[]{:S(2)}) %collective-permute-start.8) | collective-permute-done | bytes 163872 | tf_op jit(solution)/shard_map/ppermute | solution.py:343
  120.2 1.5 collective-permute-start.13
  121.7 7.7 %shard_map.82 = (f32[64,64]{1,0:T(8,128)}, bf16[384,64]{1,0:T(8,128)(2,1)}, bf16[128,512]{1,0:T(8,128)(2,1)}) custom-call(f32[64,640]{1,0:T(8,128)} %copy-done.6, f32[64,640]{1,0:T(8,128)} %copy-done.23, f32[64,640]{1,0:T(8,128)} %collective-permute-done.9.two, f32[64,640]{1,0:T(8,128)} %copy-done.22, f32[64,384]{1,0:T(8,128)} %get-tuple-element.27.left), custom_call_target="tpu_custom_call" | custom-call | flops 6000000000 | bytes 1048576 | tf_op jit(solution)/shard_map/pallas_call | solution.py:237
  129.5 0.7 copy-done.4
  130.2 2.7 %shard_map.85 = bf16[32,16,128]{2,1,0:T(8,128)(2,1)} custom-call(f32[64,64]{1,0:T(8,128)} %get-tuple-element.28.inverse, bf16[128,512]{1,0:T(8,128)(2,1)} %get-tuple-element.29.acts_left, bf16[512,768]{1,0:T(8,128)(2,1)} %rest_0_.1, f32[64,768]{1,0:T(8,128)} %get-tuple-element.31.own, f32[64,768]{1,0:T(8,128)} %copy-done.3, f32[64,768]{1,0:T(8,128)} %copy-done.4, ...), custom_call_target="tpu_custom_call" | custom-call | flops 100000000 | bytes 1048576 | tf_op jit(solution)/shard_map/pallas_call | solution.py:255
  132.9 3.9 %all-to-all-start.2 = ((bf16[32,16,128]{2,1,0:T(8,128)(2,1)}), bf16[32,16,128]{2,1,0:T(8,128)(2,1)S(1)}, u32[]{:S(2)}, u32[]{:S(2)}) async-start(bf16[32,16,128]{2,1,0:T(8,128)(2,1)} %shard_map.85), calls=%async_computation.2 | async-start | bytes 262144 | tf_op jit(solution)/shard_map/all_to_all | solution.py:351
  136.8 2.0 %collective-permute-start.15 = (bf16[512,768]{1,0:T(8,128)(2,1)}, bf16[512,768]{1,0:T(8,128)(2,1)}, u32[]{:S(2)}, u32[]{:S(2)}) collective-permute-start(bf16[512,768]{1,0:T(8,128)(2,1)} %rest_0_.1), channel_id=1, source_target_pairs={{0,1},{1,0},{2,3},{3,2},{4,5},{5,4},{6,7},{7,6},{8,9},{9,8},{10,11... | collective-permute-start | bytes 2359304 | tf_op jit(solution)/shard_map/ppermute | solution.py:347
  138.9 0.4 collective-permute-start.17
  139.5 6.7 %all-to-all-done.2.arrived = bf16[32,16,128]{2,1,0:T(8,128)(2,1)S(1)} async-done(((bf16[32,16,128]{2,1,0:T(8,128)(2,1)}), bf16[32,16,128]{2,1,0:T(8,128)(2,1)S(1)}, u32[]{:S(2)}, u32[]{:S(2)}) %all-to-all-start.2) | async-done | bytes 131104 | tf_op jit(solution)/shard_map/all_to_all | solution.py:351
  146.2 0.7 copy-done.1
  146.8 1.6 shard_map.87
  148.4 13.2 %all_to_all.22 = bf16[32,16,128]{2,1,0:T(8,128)(2,1)S(1)} all-to-all(bf16[32,16,128]{2,1,0:T(8,128)(2,1)} %shard_map.87), channel_id=1, replica_groups=mesh['dp_0'=8,'dp_1'=4,'mp_0'=4,'mp_1'=2] {'dp_0','dp_1'}, dimensions={0} | all-to-all | bytes 262144 | tf_op jit(solution)/shard_map/all_to_all | solution.py:351
  161.7 2.6 %collective-permute-start.21 = (bf16[24,16,128]{2,1,0:T(8,128)(2,1)S(1)}, bf16[24,16,128]{2,1,0:T(8,128)(2,1)S(1)}, u32[]{:S(2)}, u32[]{:S(2)}) collective-permute-start(bf16[24,16,128]{2,1,0:T(8,128)(2,1)S(1)} %slice.4.rest_0_), channel_id=1, source_target_pairs={{0,2},{2,4},{4,6},{6,0},{1,3},{3,5},{5,7},{7,1},{8,10},{10,12},{12... | collective-permute-start | bytes 294920 | tf_op jit(solution)/shard_map/ppermute | solution.py:343
  164.3 2.2 %collective-permute-done.21.rest_3_ = bf16[24,16,128]{2,1,0:T(8,128)(2,1)S(1)} collective-permute-done((bf16[24,16,128]{2,1,0:T(8,128)(2,1)S(1)}, bf16[24,16,128]{2,1,0:T(8,128)(2,1)S(1)}, u32[]{:S(2)}, u32[]{:S(2)}) %collective-permute-start.21) | collective-permute-done | bytes 98336 | tf_op jit(solution)/shard_map/ppermute | solution.py:343
  166.5 1.6 collective-permute-start.20
  168.1 4.1 %collective-permute-done.20.rest_2_ = bf16[24,16,128]{2,1,0:T(8,128)(2,1)S(1)} collective-permute-done((bf16[24,16,128]{2,1,0:T(8,128)(2,1)S(1)}, bf16[24,16,128]{2,1,0:T(8,128)(2,1)S(1)}, u32[]{:S(2)}, u32[]{:S(2)}) %collective-permute-start.20) | collective-permute-done | bytes 98336 | tf_op jit(solution)/shard_map/ppermute | solution.py:343
  172.2 0.4 collective-permute-start.19
  172.6 3.9 %collective-permute-done.19.rest_1_ = bf16[24,16,128]{2,1,0:T(8,128)(2,1)S(1)} collective-permute-done((bf16[24,16,128]{2,1,0:T(8,128)(2,1)S(1)}, bf16[24,16,128]{2,1,0:T(8,128)(2,1)S(1)}, u32[]{:S(2)}, u32[]{:S(2)}) %collective-permute-start.19) | collective-permute-done | bytes 98336 | tf_op jit(solution)/shard_map/ppermute | solution.py:343
  176.5 6.7 %collective-permute-start.22 = (bf16[24,16,128]{2,1,0:T(8,128)(2,1)S(1)}, bf16[24,16,128]{2,1,0:T(8,128)(2,1)S(1)}, u32[]{:S(2)}, u32[]{:S(2)}) collective-permute-start(bf16[24,16,128]{2,1,0:T(8,128)(2,1)S(1)} %slice.4.rest_0_), channel_id=1, source_target_pairs={{0,1},{1,0},{2,3},{3,2},{4,5},{5,4},{6,7},{7,6},{8,9},{9,8},{10,11... | collective-permute-start | bytes 294920 | tf_op jit(solution)/shard_map/ppermute | solution.py:347
  183.4 0.4 collective-permute-start.24
  184.1 9.2 %shard_map.86.fed = bf16[8,384,768]{2,1,0:T(8,128)(2,1)} custom-call(bf16[512,384]{1,0:T(8,128)(2,1)} %acts.5, bf16[384,6144]{1,0:T(8,128)(2,1)} %bitcast.8, bf16[512,768]{1,0:T(8,128)(2,1)} %rest_0_.1, bf16[512,768]{1,0:T(8,128)(2,1)} %copy-done.21, bf16[512,768]{1,0:T(8,128)(2,1)} %copy-done.20, bf16[512,768]{1,0:T(8,128)(2,1)} %copy-done.19, ...), custom_call_target="tpu_custom_call" | custom-call | flops 6000000000 | bytes 1048576 | tf_op jit(solution)/shard_map/pallas_call | solution.py:283
  193.5 0.6 copy-done.12
  194.2 7.2 %shard_map.88 = (bf16[1,384,6144]{2,1,0:T(8,128)(2,1)}, f32[192,384]{1,0:T(8,128)}, bf16[64,6144]{1,0:T(8,128)(2,1)}) custom-call(bf16[8,384,768]{2,1,0:T(8,128)(2,1)} %shard_map.86.fed, bf16[384,64]{1,0:T(8,128)(2,1)} %get-tuple-element.39.basis, bf16[24,16,128]{2,1,0:T(8,128)(2,1)} %copy-done.2, bf16[24,16,128]{2,1,0:T(8,128)(2,1)} %copy-done.11, ...), custom_call_target="tpu_custom_call" | custom-call | flops 1000000000 | bytes 1048576 | tf_op jit(solution)/shard_map/pallas_call | solution.py:328
  (72 shorter events, 1.4 us)
Async XLA Ops:
  3.7 4.5 %collective-permute-start = (f32[64,512]{1,0:T(8,128)}, f32[64,512]{1,0:T(8,128)S(1)}, u32[]{:S(2)}, u32[]{:S(2)}) collective-permute-start(f32[64,512]{1,0:T(8,128)} %shard_map.76.a), channel_id=1, source_target_pairs={{0,1},{1,0},{2,3},{3,2},{4,5},{5,4},{6,7},{7,6},{8,9},{9,8},{10,11... | collective-permute-start | bytes 393224 | tf_op jit(solution)/shard_map/ppermute | solution.py:347
  8.2 0.7 copy-start.8
  10.5 7.3 %collective-permute-start.3 = (bf16[64,512]{1,0:T(8,128)(2,1)}, bf16[64,512]{1,0:T(8,128)(2,1)S(1)}, u32[]{:S(2)}, u32[]{:S(2)}) collective-permute-start(bf16[64,512]{1,0:T(8,128)(2,1)} %get-tuple-element.23), channel_id=1, source_target_pairs={{0,6},{2,0},{4,2},{6,4},{1,7},{3,1},{5,3},{7,5},{8,14},{10,8},{12,... | collective-permute-start | bytes 196616 | tf_op jit(solution)/shard_map/ppermute | solution.py:343
  11.5 6.3 %collective-permute-start.2 = (bf16[64,512]{1,0:T(8,128)(2,1)}, bf16[64,512]{1,0:T(8,128)(2,1)S(1)}, u32[]{:S(2)}, u32[]{:S(2)}) collective-permute-start(bf16[64,512]{1,0:T(8,128)(2,1)} %get-tuple-element.23), channel_id=1, source_target_pairs={{0,4},{2,6},{4,0},{6,2},{1,5},{3,7},{5,1},{7,3},{8,12},{10,14},{12... | collective-permute-start | bytes 196616 | tf_op jit(solution)/shard_map/ppermute | solution.py:343
  11.9 6.0 %collective-permute-start.1 = (bf16[64,512]{1,0:T(8,128)(2,1)}, bf16[64,512]{1,0:T(8,128)(2,1)S(1)}, u32[]{:S(2)}, u32[]{:S(2)}) collective-permute-start(bf16[64,512]{1,0:T(8,128)(2,1)} %get-tuple-element.23), channel_id=1, source_target_pairs={{0,2},{2,4},{4,6},{6,0},{1,3},{3,5},{5,7},{7,1},{8,10},{10,12},{12... | collective-permute-start | bytes 196616 | tf_op jit(solution)/shard_map/ppermute | solution.py:343
  59.1 7.7 %copy-start.7 = (f32[64,640]{1,0:T(8,128)S(1)}, f32[64,640]{1,0:T(8,128)}, u32[]{:S(2)}) copy-start(f32[64,640]{1,0:T(8,128)} %get-tuple-element.26) | copy-start | bytes 491524
  63.2 11.3 %collective-permute-start.11 = (f32[4,64,768]{2,1,0:T(8,128)}, f32[4,64,768]{2,1,0:T(8,128)S(1)}, u32[]{:S(2)}, u32[]{:S(2)}) collective-permute-start(f32[4,64,768]{2,1,0:T(8,128)} %shard_map.83), channel_id=1, source_target_pairs={{0,1},{1,0},{2,3},{3,2},{4,5},{5,4},{6,7},{7,6},{8,9},{9,8},{10,11... | collective-permute-start | bytes 2359304 | tf_op jit(solution)/shard_map/ppermute | solution.py:347
  66.8 2.4 %collective-permute-start.7 = (f32[64,640]{1,0:T(8,128)S(1)}, f32[64,640]{1,0:T(8,128)S(1)}, u32[]{:S(2)}, u32[]{:S(2)}) collective-permute-start(f32[64,640]{1,0:T(8,128)S(1)} %copy-done.7), channel_id=1, source_target_pairs={{0,1},{1,0},{2,3},{3,2},{4,5},{5,4},{6,7},{7,6},{8,9},{9,8},{10,11... | collective-permute-start | bytes 491528 | tf_op jit(solution)/shard_map/ppermute | solution.py:347
  69.2 52.5 %copy-start.6 = (f32[64,640]{1,0:T(8,128)}, f32[64,640]{1,0:T(8,128)S(1)}, u32[]{:S(2)}) copy-start(f32[64,640]{1,0:T(8,128)S(1)} %add.3.own) | copy-start | bytes 491524
  69.2 11.8 %collective-permute-start.10 = (f32[64,640]{1,0:T(8,128)S(1)}, f32[64,640]{1,0:T(8,128)S(1)}, u32[]{:S(2)}, u32[]{:S(2)}) collective-permute-start(f32[64,640]{1,0:T(8,128)S(1)} %add.3.own), channel_id=1, source_target_pairs={{0,6},{2,0},{4,2},{6,4},{1,7},{3,1},{5,3},{7,5},{8,14},{10,8},{12,... | collective-permute-start | bytes 491528 | tf_op jit(solution)/shard_map/ppermute | solution.py:343
  71.2 11.1 %collective-permute-start.9 = (f32[64,640]{1,0:T(8,128)S(1)}, f32[64,640]{1,0:T(8,128)}, u32[]{:S(2)}, u32[]{:S(2)}) collective-permute-start(f32[64,640]{1,0:T(8,128)S(1)} %add.3.own), channel_id=1, source_target_pairs={{0,4},{2,6},{4,0},{6,2},{1,5},{3,7},{5,1},{7,3},{8,12},{10,14},{12... | collective-permute-start | bytes 491528 | tf_op jit(solution)/shard_map/ppermute | solution.py:343
  72.6 66.2 %collective-permute-start.6 = (bf16[512,768]{1,0:T(8,128)(2,1)}, bf16[512,768]{1,0:T(8,128)(2,1)S(1)}, u32[]{:S(2)}, u32[]{:S(2)}) collective-permute-start(bf16[512,768]{1,0:T(8,128)(2,1)} %rest_0_.1), channel_id=1, source_target_pairs={{0,2},{2,4},{4,6},{6,0},{1,3},{3,5},{5,7},{7,1},{8,10},{10,12},{12... | collective-permute-start | bytes 2359304 | tf_op jit(solution)/shard_map/ppermute | solution.py:343
  72.6 66.3 %collective-permute-start.5 = (bf16[512,768]{1,0:T(8,128)(2,1)}, bf16[512,768]{1,0:T(8,128)(2,1)S(1)}, u32[]{:S(2)}, u32[]{:S(2)}) collective-permute-start(bf16[512,768]{1,0:T(8,128)(2,1)} %rest_0_.1), channel_id=1, source_target_pairs={{0,4},{2,6},{4,0},{6,2},{1,5},{3,7},{5,1},{7,3},{8,12},{10,14},{12... | collective-permute-start | bytes 2359304 | tf_op jit(solution)/shard_map/ppermute | solution.py:343
  74.5 0.9 copy-start
  79.6 42.1 %collective-permute-start.12 = (f32[64,768]{1,0:T(8,128)}, f32[64,768]{1,0:T(8,128)S(1)}, u32[]{:S(2)}, u32[]{:S(2)}) collective-permute-start(f32[64,768]{1,0:T(8,128)} %get-tuple-element.32), channel_id=1, source_target_pairs={{0,2},{2,4},{4,6},{6,0},{1,3},{3,5},{5,7},{7,1},{8,10},{10,12},{12... | collective-permute-start | bytes 589832 | tf_op jit(solution)/shard_map/ppermute | solution.py:343
  81.0 40.7 %copy-start.22 = (f32[64,640]{1,0:T(8,128)}, f32[64,640]{1,0:T(8,128)S(1)}, u32[]{:S(2)}) copy-start(f32[64,640]{1,0:T(8,128)S(1)} %collective-permute-done.10.three) | copy-start | bytes 491524
  81.0 58.3 %collective-permute-start.4 = (bf16[512,768]{1,0:T(8,128)(2,1)}, bf16[512,768]{1,0:T(8,128)(2,1)S(1)}, u32[]{:S(2)}, u32[]{:S(2)}) collective-permute-start(bf16[512,768]{1,0:T(8,128)(2,1)} %rest_0_.1), channel_id=1, source_target_pairs={{0,6},{2,0},{4,2},{6,4},{1,7},{3,1},{5,3},{7,5},{8,14},{10,8},{12,... | collective-permute-start | bytes 2359304 | tf_op jit(solution)/shard_map/ppermute | solution.py:343
  82.3 37.8 %collective-permute-start.8 = (f32[64,640]{1,0:T(8,128)S(1)}, f32[64,640]{1,0:T(8,128)S(1)}, u32[]{:S(2)}, u32[]{:S(2)}) collective-permute-start(f32[64,640]{1,0:T(8,128)S(1)} %add.3.own), channel_id=1, source_target_pairs={{0,2},{2,4},{4,6},{6,0},{1,3},{3,5},{5,7},{7,1},{8,10},{10,12},{12... | collective-permute-start | bytes 491528 | tf_op jit(solution)/shard_map/ppermute | solution.py:343
  120.2 1.5 copy-start.23
  120.2 9.3 %collective-permute-start.13 = (f32[64,768]{1,0:T(8,128)}, f32[64,768]{1,0:T(8,128)S(1)}, u32[]{:S(2)}, u32[]{:S(2)}) collective-permute-start(f32[64,768]{1,0:T(8,128)} %get-tuple-element.33), channel_id=1, source_target_pairs={{0,4},{2,6},{4,0},{6,2},{1,5},{3,7},{5,1},{7,3},{8,12},{10,14},{12... | collective-permute-start | bytes 589832 | tf_op jit(solution)/shard_map/ppermute | solution.py:343
  121.7 7.8 %copy-start.3 = (f32[64,768]{1,0:T(8,128)}, f32[64,768]{1,0:T(8,128)S(1)}, u32[]{:S(2)}) copy-start(f32[64,768]{1,0:T(8,128)S(1)} %collective-permute-done.12.one) | copy-start | bytes 589828
  121.7 7.8 %collective-permute-start.14 = (f32[64,768]{1,0:T(8,128)}, f32[64,768]{1,0:T(8,128)S(1)}, u32[]{:S(2)}, u32[]{:S(2)}) collective-permute-start(f32[64,768]{1,0:T(8,128)} %get-tuple-element.34), channel_id=1, source_target_pairs={{0,6},{2,0},{4,2},{6,4},{1,7},{3,1},{5,3},{7,5},{8,14},{10,8},{12,... | collective-permute-start | bytes 589832 | tf_op jit(solution)/shard_map/ppermute | solution.py:343
  129.4 0.7 copy-start.4
  129.5 0.7 copy-start.5
  132.9 13.3 %all-to-all-start.2 = ((bf16[32,16,128]{2,1,0:T(8,128)(2,1)}), bf16[32,16,128]{2,1,0:T(8,128)(2,1)S(1)}, u32[]{:S(2)}, u32[]{:S(2)}) async-start(bf16[32,16,128]{2,1,0:T(8,128)(2,1)} %shard_map.85), calls=%async_computation.2 | async-start | bytes 262144 | tf_op jit(solution)/shard_map/all_to_all | solution.py:351
  136.8 46.5 %collective-permute-start.15 = (bf16[512,768]{1,0:T(8,128)(2,1)}, bf16[512,768]{1,0:T(8,128)(2,1)}, u32[]{:S(2)}, u32[]{:S(2)}) collective-permute-start(bf16[512,768]{1,0:T(8,128)(2,1)} %rest_0_.1), channel_id=1, source_target_pairs={{0,1},{1,0},{2,3},{3,2},{4,5},{5,4},{6,7},{7,6},{8,9},{9,8},{10,11... | collective-permute-start | bytes 2359304 | tf_op jit(solution)/shard_map/ppermute | solution.py:347
  138.8 45.3 %copy-start.19 = (bf16[512,768]{1,0:T(8,128)(2,1)}, bf16[512,768]{1,0:T(8,128)(2,1)S(1)}, u32[]{:S(2)}) copy-start(bf16[512,768]{1,0:T(8,128)(2,1)S(1)} %collective-permute-done.6.rest_3_) | copy-start | bytes 2359300
  138.8 44.6 %collective-permute-start.18 = (bf16[512,768]{1,0:T(8,128)(2,1)S(1)}, bf16[512,768]{1,0:T(8,128)(2,1)}, u32[]{:S(2)}, u32[]{:S(2)}) collective-permute-start(bf16[512,768]{1,0:T(8,128)(2,1)S(1)} %collective-permute-done.6.rest_3_), channel_id=1, source_target_pairs={{0,1},{1,0},{2,3},{3,2},{4,5},{5,4},{6,7},{7,6},{8,9},{9,8},{10,11... | collective-permute-start | bytes 2359304 | tf_op jit(solution)/shard_map/ppermute | solution.py:347
  138.9 45.2 %copy-start.20 = (bf16[512,768]{1,0:T(8,128)(2,1)}, bf16[512,768]{1,0:T(8,128)(2,1)S(1)}, u32[]{:S(2)}) copy-start(bf16[512,768]{1,0:T(8,128)(2,1)S(1)} %collective-permute-done.5.rest_2_) | copy-start | bytes 2359300
  138.9 44.9 %collective-permute-start.17 = (bf16[512,768]{1,0:T(8,128)(2,1)S(1)}, bf16[512,768]{1,0:T(8,128)(2,1)}, u32[]{:S(2)}, u32[]{:S(2)}) collective-permute-start(bf16[512,768]{1,0:T(8,128)(2,1)S(1)} %collective-permute-done.5.rest_2_), channel_id=1, source_target_pairs={{0,1},{1,0},{2,3},{3,2},{4,5},{5,4},{6,7},{7,6},{8,9},{9,8},{10,11... | collective-permute-start | bytes 2359304 | tf_op jit(solution)/shard_map/ppermute | solution.py:347
  139.3 44.8 %copy-start.21 = (bf16[512,768]{1,0:T(8,128)(2,1)}, bf16[512,768]{1,0:T(8,128)(2,1)S(1)}, u32[]{:S(2)}) copy-start(bf16[512,768]{1,0:T(8,128)(2,1)S(1)} %collective-permute-done.4.rest_1_) | copy-start | bytes 2359300
  139.3 44.8 %collective-permute-start.16 = (bf16[512,768]{1,0:T(8,128)(2,1)S(1)}, bf16[512,768]{1,0:T(8,128)(2,1)}, u32[]{:S(2)}, u32[]{:S(2)}) collective-permute-start(bf16[512,768]{1,0:T(8,128)(2,1)S(1)} %collective-permute-done.4.rest_1_), channel_id=1, source_target_pairs={{0,1},{1,0},{2,3},{3,2},{4,5},{5,4},{6,7},{7,6},{8,9},{9,8},{10,11... | collective-permute-start | bytes 2359304 | tf_op jit(solution)/shard_map/ppermute | solution.py:347
  146.2 0.7 copy-start.1
  161.7 31.7 %copy-start.2 = (bf16[24,16,128]{2,1,0:T(8,128)(2,1)}, bf16[24,16,128]{2,1,0:T(8,128)(2,1)S(1)}, u32[]{:S(2)}) copy-start(bf16[24,16,128]{2,1,0:T(8,128)(2,1)S(1)} %slice.4.rest_0_) | copy-start | bytes 294916
  161.7 4.8 %collective-permute-start.21 = (bf16[24,16,128]{2,1,0:T(8,128)(2,1)S(1)}, bf16[24,16,128]{2,1,0:T(8,128)(2,1)S(1)}, u32[]{:S(2)}, u32[]{:S(2)}) collective-permute-start(bf16[24,16,128]{2,1,0:T(8,128)(2,1)S(1)} %slice.4.rest_0_), channel_id=1, source_target_pairs={{0,2},{2,4},{4,6},{6,0},{1,3},{3,5},{5,7},{7,1},{8,10},{10,12},{12... | collective-permute-start | bytes 294920 | tf_op jit(solution)/shard_map/ppermute | solution.py:343
  166.5 26.9 %copy-start.9 = (bf16[24,16,128]{2,1,0:T(8,128)(2,1)}, bf16[24,16,128]{2,1,0:T(8,128)(2,1)S(1)}, u32[]{:S(2)}) copy-start(bf16[24,16,128]{2,1,0:T(8,128)(2,1)S(1)} %collective-permute-done.21.rest_3_) | copy-start | bytes 294916
  166.5 5.7 %collective-permute-start.20 = (bf16[24,16,128]{2,1,0:T(8,128)(2,1)S(1)}, bf16[24,16,128]{2,1,0:T(8,128)(2,1)S(1)}, u32[]{:S(2)}, u32[]{:S(2)}) collective-permute-start(bf16[24,16,128]{2,1,0:T(8,128)(2,1)S(1)} %slice.4.rest_0_), channel_id=1, source_target_pairs={{0,4},{2,6},{4,0},{6,2},{1,5},{3,7},{5,1},{7,3},{8,12},{10,14},{12... | collective-permute-start | bytes 294920 | tf_op jit(solution)/shard_map/ppermute | solution.py:343
  172.2 21.2 %copy-start.10 = (bf16[24,16,128]{2,1,0:T(8,128)(2,1)}, bf16[24,16,128]{2,1,0:T(8,128)(2,1)S(1)}, u32[]{:S(2)}) copy-start(bf16[24,16,128]{2,1,0:T(8,128)(2,1)S(1)} %collective-permute-done.20.rest_2_) | copy-start | bytes 294916
  172.2 4.4 %collective-permute-start.19 = (bf16[24,16,128]{2,1,0:T(8,128)(2,1)S(1)}, bf16[24,16,128]{2,1,0:T(8,128)(2,1)S(1)}, u32[]{:S(2)}, u32[]{:S(2)}) collective-permute-start(bf16[24,16,128]{2,1,0:T(8,128)(2,1)S(1)} %slice.4.rest_0_), channel_id=1, source_target_pairs={{0,6},{2,0},{4,2},{6,4},{1,7},{3,1},{5,3},{7,5},{8,14},{10,8},{12,... | collective-permute-start | bytes 294920 | tf_op jit(solution)/shard_map/ppermute | solution.py:343
  176.5 16.9 %copy-start.11 = (bf16[24,16,128]{2,1,0:T(8,128)(2,1)}, bf16[24,16,128]{2,1,0:T(8,128)(2,1)S(1)}, u32[]{:S(2)}) copy-start(bf16[24,16,128]{2,1,0:T(8,128)(2,1)S(1)} %collective-permute-done.19.rest_1_) | copy-start | bytes 294916
  176.5 16.9 %collective-permute-start.22 = (bf16[24,16,128]{2,1,0:T(8,128)(2,1)S(1)}, bf16[24,16,128]{2,1,0:T(8,128)(2,1)S(1)}, u32[]{:S(2)}, u32[]{:S(2)}) collective-permute-start(bf16[24,16,128]{2,1,0:T(8,128)(2,1)S(1)} %slice.4.rest_0_), channel_id=1, source_target_pairs={{0,1},{1,0},{2,3},{3,2},{4,5},{5,4},{6,7},{7,6},{8,9},{9,8},{10,11... | collective-permute-start | bytes 294920 | tf_op jit(solution)/shard_map/ppermute | solution.py:347
  183.3 10.1 %collective-permute-start.25 = (bf16[24,16,128]{2,1,0:T(8,128)(2,1)S(1)}, bf16[24,16,128]{2,1,0:T(8,128)(2,1)S(1)}, u32[]{:S(2)}, u32[]{:S(2)}) collective-permute-start(bf16[24,16,128]{2,1,0:T(8,128)(2,1)S(1)} %collective-permute-done.21.rest_3_), channel_id=1, source_target_pairs={{0,1},{1,0},{2,3},{3,2},{4,5},{5,4},{6,7},{7,6},{8,9},{9,8},{10,11... | collective-permute-start | bytes 294920 | tf_op jit(solution)/shard_map/ppermute | solution.py:347
  183.4 10.1 %collective-permute-start.24 = (bf16[24,16,128]{2,1,0:T(8,128)(2,1)S(1)}, bf16[24,16,128]{2,1,0:T(8,128)(2,1)S(1)}, u32[]{:S(2)}, u32[]{:S(2)}) collective-permute-start(bf16[24,16,128]{2,1,0:T(8,128)(2,1)S(1)} %collective-permute-done.20.rest_2_), channel_id=1, source_target_pairs={{0,1},{1,0},{2,3},{3,2},{4,5},{5,4},{6,7},{7,6},{8,9},{9,8},{10,11... | collective-permute-start | bytes 294920 | tf_op jit(solution)/shard_map/ppermute | solution.py:347
  183.8 9.7 %collective-permute-start.23 = (bf16[24,16,128]{2,1,0:T(8,128)(2,1)S(1)}, bf16[24,16,128]{2,1,0:T(8,128)(2,1)S(1)}, u32[]{:S(2)}, u32[]{:S(2)}) collective-permute-start(bf16[24,16,128]{2,1,0:T(8,128)(2,1)S(1)} %collective-permute-done.19.rest_1_), channel_id=1, source_target_pairs={{0,1},{1,0},{2,3},{3,2},{4,5},{5,4},{6,7},{7,6},{8,9},{9,8},{10,11... | collective-permute-start | bytes 294920 | tf_op jit(solution)/shard_map/ppermute | solution.py:347
  193.4 0.7 copy-start.12
  193.4 0.7 copy-start.13
  193.5 0.7 copy-start.14
  193.5 0.7 copy-start.15
  (3 other events, 1.9 us)

commit v3 on v2

v3 whole, which is shorter than its diff:
```python
import jax
import jax.numpy as jnp
from jax import lax
from jax.experimental import pallas as pl
from jax.experimental.pallas import tpu as pltpu
from jax.sharding import Mesh
from jax.sharding import PartitionSpec as P


DP = ("dp_0", "dp_1")
YY = "mp_0"
CC = "mp_1"
F32 = jnp.float32
BF16 = jnp.bfloat16
HIGHEST = lax.Precision.HIGHEST
D, RANK, ROWS, TOK, COLS, WORKERS = 6144, 64, 384, 512, 768, 32
INTERPRET = False
BETA = 0.9

NN = (((1,), (0,)), ((), ()))
NT = (((1,), (1,)), ((), ()))


def dot(a, b, dims=NN, precision=None):
    return lax.dot_general(a, b, dims, precision=precision, preferred_element_type=F32)


def two_terms(x):
    high = x.astype(BF16)
    low = (x - high.astype(F32)).astype(BF16)
    return jnp.concatenate([high, low], axis=0)


def halves_added(x):
    return x[: x.shape[0] // 2] + x[x.shape[0] // 2 :]


def call(body, out_shape, flops, mib=8, **kw):
    return pl.pallas_call(
        body,
        out_shape=out_shape,
        interpret=INTERPRET,
        compiler_params=pltpu.CompilerParams(vmem_limit_bytes=mib << 20),
        cost_estimate=pl.CostEstimate(flops=flops, bytes_accessed=1 << 20, transcendentals=0),
        **kw,
    )


def sds(shape, dtype):
    return jax.ShapeDtypeStruct(shape, dtype)


def on_chip(shape, dtype):
    return pltpu.VMEM(shape, dtype)


VMEM = pl.BlockSpec(memory_space=pltpu.VMEM)
HBM = pl.BlockSpec(memory_space=pltpu.HBM)


def block_at(ahead, other):
    y, c = lax.axis_index(YY), lax.axis_index(CC)
    return 2 * lax.rem(y + ahead, 4) + (1 - c if other else c)


def columns(block):
    return pl.ds(pl.multiple_of(block * COLS, COLS), COLS)


def grads_sketch_body(grads, sketch_t, out, held, sem):
    cut = pltpu.make_async_copy(sketch_t.at[:, columns(block_at(0, False))], held, sem)
    cut.start()
    cut.wait()
    out[...] = dot(held[...], grads[...], NT)


def grads_sketch(grads, sketch_t):
    return call(
        grads_sketch_body,
        on_chip((RANK, TOK), F32),
        10**8,
        in_specs=[VMEM, HBM],
        out_specs=VMEM,
        scratch_shapes=[pltpu.VMEM((RANK, COLS), BF16), pltpu.SemaphoreType.DMA(())],
    )(grads, sketch_t)


def pair_body(a, b, out, rounded):
    total = a[...] + b[...]
    out[...] = total
    rounded[...] = total.astype(BF16)


def pair_sum(a, b):
    return call(pair_body, (on_chip(a.shape, F32), on_chip(a.shape, BF16)), 10**7)(a, b)


def error_sketch_body(error, sketch_t, out, held, sems):
    places = [columns(block_at(k % 4, k >= 4)) for k in range(8)]
    copies = [
        pltpu.make_async_copy(error.at[:, places[k]], held.at[k], sems.at[k]) for k in range(8)
    ]
    for c in copies:
        c.start()
    acc = jnp.zeros((RANK, ROWS), F32)
    for k in range(8):
        copies[k].wait()
        acc = acc + dot(sketch_t[:, places[k]], held[k], NT)
    out[...] = acc


def error_sketch(error, sketch_t):
    return call(
        error_sketch_body,
        (on_chip((RANK, ROWS), F32), on_chip((8, ROWS, COLS), BF16)),
        3 * 10**9,
        in_specs=[HBM, VMEM],
        out_specs=(VMEM, VMEM),
        scratch_shapes=[pltpu.SemaphoreType.DMA((8,))],
    )(error, sketch_t)


def left_term_body(own, one, two, three, acts, from_error, out):
    total = own[...] + one[...].astype(F32) + two[...].astype(F32) + three[...].astype(F32)
    left = halves_added(dot(two_terms(total), acts[...])) + from_error[...]
    for r in range(8):
        for j in range(3):
            out[4 * r + j] = left[8 * r : 8 * r + 8, 128 * j : 128 * j + 128]
        out[4 * r + 3] = jnp.zeros((8, 128), F32)


def left_term(own, parts, acts, from_error):
    return call(left_term_body, on_chip((WORKERS, 8, 128), F32), 10**8)(
        own, *parts, acts, from_error
    )


def sum_and_copy_body(arrived, out):
    total = jnp.sum(arrived[...].astype(F32), axis=0).astype(out.dtype)
    out[...] = jnp.broadcast_to(total[None], out.shape)


def sum_and_copy(arrived, dtype):
    return call(sum_and_copy_body, on_chip(arrived.shape, dtype), 10**7)(arrived)


def left_products_body(tiles, acts, left_out, left_terms, small):
    rows = [jnp.concatenate([tiles[4 * r + j] for j in range(3)], axis=1) for r in range(8)]
    left = jnp.concatenate(rows, axis=0)
    left_out[...] = left
    terms = two_terms(left)
    left_terms[...] = terms
    small[:, :TOK] = halves_added(dot(terms, acts[...], NT))
    gram = dot(left, left, NT, HIGHEST)
    small[:, TOK:] = jnp.concatenate([gram, jnp.zeros_like(gram)], axis=1)


def left_products(tiles, acts):
    return call(
        left_products_body,
        (
            on_chip((RANK, ROWS), F32),
            on_chip((2 * RANK, ROWS), BF16),
            on_chip((RANK, TOK + 128), F32),
        ),
        10**8,
    )(tiles, acts)


def right_far_body(left_terms, error, out):
    for k in range(4):
        out[k] = halves_added(dot(left_terms[...], error[4 + k]))


def right_near_body(left_terms, error, got, out):
    y = lax.axis_index(YY)
    for k in range(4):
        out[lax.rem(y + k, 4)] = halves_added(dot(left_terms[...], error[k])) + got[k]


def right_far(left_terms, error):
    shape = on_chip((4, RANK, COLS), F32)
    return call(right_far_body, shape, 10**9)(left_terms, error)


def right_near(left_terms, error, got):
    shape = on_chip((4, RANK, COLS), F32)
    return call(right_near_body, shape, 10**9)(left_terms, error, got)


def factor_body(own, one, two, three, left, inverse_out, basis_out, acts_left):
    small = own[...] + one[...] + two[...] + three[...]
    acts_left[...] = two_terms(small[:, :TOK])
    lanes = lax.broadcasted_iota(jnp.int32, (RANK, RANK), 1)
    subs = lax.broadcasted_iota(jnp.int32, (RANK, RANK), 0)
    eye = jnp.where(lanes == subs, 1.0, 0.0).astype(F32)
    work = jnp.concatenate([small[:, TOK : TOK + RANK], eye], axis=1)
    rows = lax.broadcasted_iota(jnp.int32, (RANK, 2 * RANK), 0)
    for j in range(RANK - 1):
        row = work[j : j + 1, :]
        ratio = work[:, j : j + 1] / work[j : j + 1, j : j + 1]
        work = work - jnp.where(rows > j, ratio * row, 0.0)
    pivots = jnp.sum(jnp.where(lanes == subs, work[:, :RANK], 0.0), axis=1, keepdims=True)
    inverse = work[:, RANK:] / jnp.sqrt(pivots)
    inverse_out[...] = inverse
    basis_out[...] = dot(inverse, left[...], NN, HIGHEST).T.astype(BF16)


def factor(own, parts, left):
    return call(
        factor_body,
        (on_chip((RANK, RANK), F32), on_chip((ROWS, RANK), BF16), on_chip((2 * RANK, TOK), BF16)),
        6 * 10**9,
    )(own, *parts, left)


def right_term_body(inverse, acts_left, grads, terms, out):
    total = terms[0] + terms[1] + terms[2] + terms[3]
    total = total + halves_added(dot(acts_left[...], grads[...]))
    right = dot(inverse[...], total, NN, HIGHEST)
    for j in range(6):
        for r in range(4):
            out[4 * j + r] = right[16 * r : 16 * r + 16, 128 * j : 128 * j + 128].astype(out.dtype)
    out[24:] = jnp.zeros((8, 16, 128), out.dtype)


def right_term(inverse, acts_left, grads, terms):
    return call(right_term_body, on_chip((WORKERS, 16, 128), BF16), 10**8)(
        inverse, acts_left, grads, terms
    )


def fed_body(acts, error, *rest):
    grads, out, held, sems = rest[:8], rest[8], rest[9], rest[10]
    loads = [pltpu.make_async_copy(grads[k], held.at[k], sems.at[k]) for k in range(8)]
    for c in loads:
        c.start()
    turned = acts[...].T
    for k in range(8):
        loads[k].wait()
        out[k] = (dot(turned, held[k]) + error[k].astype(F32)).astype(BF16)


def fed_of(acts, error, grads):
    return call(
        fed_body,
        on_chip((8, ROWS, COLS), BF16),
        6 * 10**9,
        16,
        in_specs=[VMEM, VMEM] + [HBM] * 8,
        out_specs=VMEM,
        scratch_shapes=[pltpu.VMEM((8, TOK, COLS), BF16), pltpu.SemaphoreType.DMA((8,))],
    )(acts, error, *grads)


def block_outputs(fed, basis, blocks, first, error_new, sketch_t, held, sems):
    stores = []
    scaled = (basis[...].astype(F32) * (1 / WORKERS)).astype(BF16)
    for i, tiles in enumerate(blocks):
        k = first + i
        where = block_at(k % 4, k >= 4)
        rows = [jnp.concatenate([tiles[4 * j + r] for j in range(6)], axis=1) for r in range(4)]
        block = jnp.concatenate(rows, axis=0)
        held[i] = (fed[k].astype(F32) - dot(scaled, block)).astype(BF16)
        store = pltpu.make_async_copy(held.at[i], error_new.at[0, :, columns(where)], sems.at[i])
        store.start()
        stores.append(store)
        sketch_t[:, columns(where)] = block
    return stores


def near_outputs_body(fed, basis, b0, b1, b2, b3, error_new, sketch_t, held, sems):
    stores = block_outputs(fed, basis, (b0, b1, b2, b3), 0, error_new, sketch_t, held, sems)
    for store in stores:
        store.wait()


OUTPUT_SCRATCH = [pltpu.VMEM((4, ROWS, COLS), BF16), pltpu.SemaphoreType.DMA((4,))]


def near_outputs(fed, basis, blocks):
    return call(
        near_outputs_body,
        (sds((1, ROWS, D), BF16), on_chip((RANK, D), BF16)),
        10**9,
        12,
        in_specs=[VMEM] * 6,
        out_specs=(HBM, VMEM),
        scratch_shapes=OUTPUT_SCRATCH,
    )(fed, basis, *blocks)


def far_outputs_body(
    fed, basis, b0, b1, b2, b3, momentum_t, _, near_t, error_new, momentum_new_t, sketch_t, held, sems
):
    for k in range(4):
        place = columns(block_at(k, False))
        sketch_t[:, place] = near_t[:, place]
    stores = block_outputs(fed, basis, (b0, b1, b2, b3), 4, error_new, sketch_t, held, sems)
    w = lax.axis_index(DP)
    quarter = lax.rem(w, 4)
    own = sketch_t[:, columns(w // 4)]
    part = own[:, 0:192]
    for i in (1, 2, 3):
        part = jnp.where(quarter == i, own[:, 192 * i : 192 * (i + 1)], part)
    part = part.astype(F32).T.astype(BF16)
    momentum_new_t[...] = BETA * momentum_t[...] + dot(part, basis[...], NT)
    for store in stores:
        store.wait()


def far_outputs(fed, basis, blocks, momentum_t, error_new, near_t):
    return call(
        far_outputs_body,
        (sds((1, ROWS, D), BF16), sds((192, ROWS), F32), sds((RANK, D), BF16)),
        10**9,
        12,
        in_specs=[VMEM] * 7 + [HBM, VMEM],
        out_specs=(HBM, VMEM, VMEM),
        scratch_shapes=OUTPUT_SCRATCH,
        input_output_aliases={7: 0},
    )(fed, basis, *blocks, momentum_t, error_new, near_t)


def along_y(x, k):
    return lax.ppermute(x, YY, [(i, (i + k) % 4) for i in range(4)])


def other_core(x):
    return lax.ppermute(x, CC, [(0, 1), (1, 0)])


def to_workers(x):
    return lax.all_to_all(x, DP, split_axis=0, concat_axis=0, tiled=True)


def after(x, *others):
    return lax.optimization_barrier((x, *others))[0]


def step(activations, out_grads, error, sketch, momentum):
    own_error = error[0]
    sketch_t = sketch.T

    mine = grads_sketch(out_grads, sketch_t)
    pair, rounded = pair_sum(mine, other_core(mine))
    others = []
    for k in (1, 2, 3):
        others.append(along_y(rounded, k))
    from_error, held_error = error_sketch(own_error, sketch_t)
    tiles = left_term(pair, others, activations, from_error)

    held = after(out_grads, *others)
    gathered = []
    for k in (1, 2, 3):
        gathered.append(along_y(held, -k % 4))

    arrived = to_workers(tiles)
    copies = sum_and_copy(arrived, F32)
    tiles = to_workers(copies)

    left, left_terms, small = left_products(tiles, activations)
    small = small + other_core(small)
    small_parts = [along_y(small, k) for k in (1, 2, 3)]
    send = right_far(left_terms, held_error)
    got = other_core(send)
    q = right_near(left_terms, held_error, got)
    terms = lax.all_to_all(q, YY, split_axis=0, concat_axis=0, tiled=True)
    inverse, basis, acts_left = factor(small, small_parts, left)
    pieces = right_term(inverse, acts_left, out_grads, terms)

    near_g = (out_grads, *gathered)
    far_g = []
    for k in range(4):
        far_g.append(other_core(after(near_g[k], pieces)))
    arrived = to_workers(pieces)
    copies = sum_and_copy(arrived, BF16)
    fed = fed_of(activations, held_error, (*near_g, *far_g))
    block = to_workers(copies)[:24]
    n3, n2, n1 = along_y(block, 1), along_y(block, 2), along_y(block, -1)
    near_n = (block, n1, n2, n3)
    far_n = []
    for k in range(4):
        far_n.append(other_core(near_n[k]))
    error_new, near_t = near_outputs(fed, basis, near_n)
    error_new, momentum_t, sketch_t = far_outputs(
        fed, basis, far_n, momentum.T, error_new, near_t
    )
    return error_new, momentum_t.T, sketch_t.T


def solution(mesh):
    split = Mesh(mesh.devices.reshape(8, 4, 4, 2), (*DP, YY, CC))
    mp = (YY, CC)
    return jax.shard_map(
        step,
        mesh=split,
        in_specs=(P(DP, mp), P(DP, mp), P(DP, mp, None), P(), P(mp, DP)),
        out_specs=(P(DP, mp, None), P(mp, DP), P()),
        check_vma=False,
    )
```

time: 202 us -> 173 us (0.86)
  Pallas kernels: 52.5 us -> 22.7 us
  local copies, waits for them, and re-layouts: 4.3 us -> 10.6 us
  waiting for transfers between devices: 58.2 us -> 54.1 us
  blocking collectives: 48 us -> 45.6 us
    pallas_call x13 -> x14, Pallas kernels: 52.5 us -> 22.7 us  [the longest x1 5.75 us: factor(): call(factor_body, (on_chip((RANK, RANK), F32), on_chip((ROWS, RANK), BF16...]
    unnamed x48 -> x26, local copies, waits for them, and re-layouts: 4.29 us -> 10.6 us
    ppermute x15 -> x12, starting transfers between devices: 16.3 us -> 11.3 us  [along_y(): return lax.ppermute(x, YY, [(i, (i + k) % 4) for i in range(4)])]
    all_to_all x0 -> x1, starting transfers between devices: none -> 3.67 us  [step(): terms = lax.all_to_all(q, YY, split_axis=0, concat_axis=0, tiled=True)]
    ppermute x15 -> x12, waiting for transfers between devices: 48 us -> 45 us  [along_y(): return lax.ppermute(x, YY, [(i, (i + k) % 4) for i in range(4)])]
    ppermute x11, starting transfers between devices: 17.2 us -> 20 us  [other_core(): return lax.ppermute(x, CC, [(0, 1), (1, 0)])]
    all_to_all x3, blocking collectives: 48 us -> 45.6 us  [to_workers(): return lax.all_to_all(x, DP, split_axis=0, concat_axis=0, tiled=True)]
  transfers between devices with their start and end apart: 27 -> 25, of which waited for: 8 -> 9; matrix products, arithmetic and copies ran while one was open for 0% -> 0% of each run, Pallas kernels for 15% -> 11%
where the time goes in v3:
time: 173 us
  waiting for transfers between devices  54.1 us (31%)
  blocking collectives  45.6 us (26%)
  starting transfers between devices  38.8 us (22%)
  Pallas kernels  22.7 us (13%)
  local copies, waits for them, and re-layouts  10.6 us (6%)
    all_to_all x3, blocking collectives, to_workers(): return lax.all_to_all(x, DP, split_axis=0, concat_axis=0, tiled=True)  45.6 us
    ppermute x12, waiting for transfers between devices, along_y(): return lax.ppermute(x, YY, [(i, (i + k) % 4) for i in range(4)])  45 us
    ppermute x11, starting transfers between devices, other_core(): return lax.ppermute(x, CC, [(0, 1), (1, 0)])  20 us
    ppermute x12, starting transfers between devices, along_y(): return lax.ppermute(x, YY, [(i, (i + k) % 4) for i in range(4)])  11.3 us
    unnamed x26, local copies, waits for them, and re-layouts  10.6 us
    all_to_all x1, waiting for transfers between devices, to_workers(): return lax.all_to_all(x, DP, split_axis=0, concat_axis=0, tiled=True)  6.05 us
    pallas_call x1, Pallas kernels, factor(): call(factor_body, (on_chip((RANK, RANK), F32), on_chip((ROWS, RANK), BF16...  5.75 us
    pallas_call x1, Pallas kernels, fed_of(): call(fed_body, on_chip((8, ROWS, COLS), BF16), 6 * 10 ** 9, 16, in_specs=...  5.22 us
  transfers between devices with their start and end apart: 25, of which 9 were waited for; matrix products, arithmetic and copies ran while one was open for 0% of the time, Pallas kernels for 11%

profile of v3, /device:TPU:1, one launch (start us, length us, event | category | flops | bytes accessed | tf_op | source)
XLA Modules:
  0.0 172.7 jit_solution(8041851026086318592)
XLA Ops:
  0.6 1.1 copy-done.2
  1.8 1.1 copy-done.5
  2.9 0.4 shard_map.77.a
  3.3 3.3 %collective-permute-start = (f32[64,512]{1,0:T(8,128)S(1)}, f32[64,512]{1,0:T(8,128)S(1)}, u32[]{:S(2)}, u32[]{:S(2)}) collective-permute-start(f32[64,512]{1,0:T(8,128)S(1)} %shard_map.77.a), channel_id=1, source_target_pairs={{0,1},{1,0},{2,3},{3,2},{4,5},{5,4},{6,7},{7,6},{8,9},{9,8},{10,11... | collective-permute-start | bytes 393224 | tf_op jit(solution)/shard_map/ppermute | solution.py:330
  6.6 1.0 collective-permute-done.b
  7.6 1.1 collective-permute-start.3
  8.7 0.3 collective-permute-start.2
  9.0 0.7 collective-permute-start.1
  9.7 1.1 copy-done.6
  10.9 2.3 %copy-done.8 = bf16[1,384,6144]{2,1,0:T(8,128)(2,1)S(1)} copy-done((bf16[1,384,6144]{2,1,0:T(8,128)(2,1)S(1)}, bf16[1,384,6144]{2,1,0:T(8,128)(2,1)}, u32[]{:S(2)}) %copy-start.8) | copy-done | bytes 4718616
  13.2 2.7 %shard_map.76 = (f32[64,384]{1,0:T(8,128)S(1)}, bf16[8,384,768]{2,1,0:T(8,128)(2,1)S(1)}) custom-call(bf16[384,6144]{1,0:T(8,128)(2,1)S(1)} %bitcast.8, bf16[64,6144]{1,0:T(8,128)(2,1)S(1)} %bitcast.6), custom_call_target="tpu_custom_call" | custom-call | flops 3000000000 | bytes 1048576 | tf_op jit(solution)/shard_map/pallas_call | solution.py:113
  16.0 0.2 shard_map.79
  16.2 20.3 %all_to_all.25.arrived = f32[32,8,128]{2,1,0:T(8,128)S(1)} all-to-all(f32[32,8,128]{2,1,0:T(8,128)S(1)} %shard_map.79), channel_id=1, replica_groups=mesh['dp_0'=8,'dp_1'=4,'mp_0'=4,'mp_1'=2] {'dp_0','dp_1'}, dimensions={0} | all-to-all | bytes 262144 | tf_op jit(solution)/shard_map/all_to_all | solution.py:334
  36.6 12.6 %all_to_all.26.tiles = f32[32,8,128]{2,1,0:T(8,128)S(1)} all-to-all(f32[32,8,128]{2,1,0:T(8,128)S(1)} %shard_map.80), channel_id=1, replica_groups=mesh['dp_0'=8,'dp_1'=4,'mp_0'=4,'mp_1'=2] {'dp_0','dp_1'}, dimensions={0} | all-to-all | bytes 262144 | tf_op jit(solution)/shard_map/all_to_all | solution.py:334
  49.2 0.4 shard_map.81
  49.6 0.6 shard_map.83
  50.2 4.0 %collective-permute-start.11 = (f32[4,64,768]{2,1,0:T(8,128)S(1)}, f32[4,64,768]{2,1,0:T(8,128)S(1)}, u32[]{:S(2)}, u32[]{:S(2)}) collective-permute-start(f32[4,64,768]{2,1,0:T(8,128)S(1)} %shard_map.83), channel_id=1, source_target_pairs={{0,1},{1,0},{2,3},{3,2},{4,5},{5,4},{6,7},{7,6},{8,9},{9,8},{10,11... | collective-permute-start | bytes 2359304 | tf_op jit(solution)/shard_map/ppermute | solution.py:330
  54.3 2.0 %collective-permute-done.7 = f32[64,640]{1,0:T(8,128)S(1)} collective-permute-done((f32[64,640]{1,0:T(8,128)S(1)}, f32[64,640]{1,0:T(8,128)S(1)}, u32[]{:S(2)}, u32[]{:S(2)}) %collective-permute-start.7) | collective-permute-done | bytes 163872 | tf_op jit(solution)/shard_map/ppermute | solution.py:330
  56.4 2.0 %collective-permute-start.10 = (f32[64,640]{1,0:T(8,128)S(1)}, f32[64,640]{1,0:T(8,128)S(1)}, u32[]{:S(2)}, u32[]{:S(2)}) collective-permute-start(f32[64,640]{1,0:T(8,128)S(1)} %add.3.own), channel_id=1, source_target_pairs={{0,6},{2,0},{4,2},{6,4},{1,7},{3,1},{5,3},{7,5},{8,14},{10,8},{12,... | collective-permute-start | bytes 491528 | tf_op jit(solution)/shard_map/ppermute | solution.py:326
  58.4 1.4 collective-permute-start.5
  59.8 2.1 %collective-permute-start.4 = (bf16[512,768]{1,0:T(8,128)(2,1)S(1)}, bf16[512,768]{1,0:T(8,128)(2,1)}, u32[]{:S(2)}, u32[]{:S(2)}) collective-permute-start(bf16[512,768]{1,0:T(8,128)(2,1)S(1)} %copy-done.3), channel_id=1, source_target_pairs={{0,6},{2,0},{4,2},{6,4},{1,7},{3,1},{5,3},{7,5},{8,14},{10,8},{12,... | collective-permute-start | bytes 2359304 | tf_op jit(solution)/shard_map/ppermute | solution.py:326
  61.9 1.6 collective-permute-start.9
  63.5 2.0 %collective-permute-start.8 = (f32[64,640]{1,0:T(8,128)S(1)}, f32[64,640]{1,0:T(8,128)S(1)}, u32[]{:S(2)}, u32[]{:S(2)}) collective-permute-start(f32[64,640]{1,0:T(8,128)S(1)} %add.3.own), channel_id=1, source_target_pairs={{0,2},{2,4},{4,6},{6,0},{1,3},{3,5},{5,7},{7,1},{8,10},{10,12},{12... | collective-permute-start | bytes 491528 | tf_op jit(solution)/shard_map/ppermute | solution.py:326
  65.5 1.5 shard_map.84
  67.0 3.7 %all-to-all-start.2 = ((f32[4,64,768]{2,1,0:T(8,128)}), f32[4,64,768]{2,1,0:T(8,128)S(1)}, u32[]{:S(2)}, u32[]{:S(2)}) async-start(f32[4,64,768]{2,1,0:T(8,128)} %shard_map.84), calls=%async_computation.2 | async-start | bytes 1572864 | tf_op jit(solution)/shard_map/all_to_all | solution.py:368
  70.7 26.7 %collective-permute-done.9.two = f32[64,640]{1,0:T(8,128)S(1)} collective-permute-done((f32[64,640]{1,0:T(8,128)S(1)}, f32[64,640]{1,0:T(8,128)S(1)}, u32[]{:S(2)}, u32[]{:S(2)}) %collective-permute-start.9) | collective-permute-done | bytes 163872 | tf_op jit(solution)/shard_map/ppermute | solution.py:326
  97.4 4.5 %collective-permute-done.8.one = f32[64,640]{1,0:T(8,128)S(1)} collective-permute-done((f32[64,640]{1,0:T(8,128)S(1)}, f32[64,640]{1,0:T(8,128)S(1)}, u32[]{:S(2)}, u32[]{:S(2)}) %collective-permute-start.8) | collective-permute-done | bytes 163872 | tf_op jit(solution)/shard_map/ppermute | solution.py:326
  101.9 0.7 copy-done.9
  102.5 0.9 copy-done.10
  103.5 0.9 copy-done.12
  104.4 5.8 %shard_map.82 = (f32[64,64]{1,0:T(8,128)S(1)}, bf16[384,64]{1,0:T(8,128)(2,1)S(1)}, bf16[128,512]{1,0:T(8,128)(2,1)S(1)}) custom-call(f32[64,640]{1,0:T(8,128)S(1)} %add.3.own, f32[64,640]{1,0:T(8,128)S(1)} %copy-done.10, f32[64,640]{1,0:T(8,128)S(1)} %collective-permute-done.9.two, f32[64,640]{1,0:T(8,128)S(1)} %collective-permute-done.10.three, ...), custom_call_target="tpu_custom_call" | custom-call | flops 6000000000 | bytes 1048576 | tf_op jit(solution)/shard_map/pallas_call | solution.py:210
  110.1 1.2 shard_map.85
  111.4 3.9 %all-to-all-start.3 = ((bf16[32,16,128]{2,1,0:T(8,128)(2,1)}), bf16[32,16,128]{2,1,0:T(8,128)(2,1)S(1)}, u32[]{:S(2)}, u32[]{:S(2)}) async-start(bf16[32,16,128]{2,1,0:T(8,128)(2,1)} %shard_map.85), calls=%async_computation.3 | async-start | bytes 262144 | tf_op jit(solution)/shard_map/all_to_all | solution.py:334
  115.3 2.7 %collective-permute-start.12 = (bf16[512,768]{1,0:T(8,128)(2,1)S(1)}, bf16[512,768]{1,0:T(8,128)(2,1)}, u32[]{:S(2)}, u32[]{:S(2)}) collective-permute-start(bf16[512,768]{1,0:T(8,128)(2,1)S(1)} %copy-done.3), channel_id=1, source_target_pairs={{0,1},{1,0},{2,3},{3,2},{4,5},{5,4},{6,7},{7,6},{8,9},{9,8},{10,11... | collective-permute-start | bytes 2359304 | tf_op jit(solution)/shard_map/ppermute | solution.py:330
  118.0 0.1 collective-permute-start.13
  118.1 0.4 collective-permute-start.14
  118.6 6.1 %all-to-all-done.3.arrived = bf16[32,16,128]{2,1,0:T(8,128)(2,1)S(1)} async-done(((bf16[32,16,128]{2,1,0:T(8,128)(2,1)}), bf16[32,16,128]{2,1,0:T(8,128)(2,1)S(1)}, u32[]{:S(2)}, u32[]{:S(2)}) %all-to-all-start.3) | async-done | bytes 131104 | tf_op jit(solution)/shard_map/all_to_all | solution.py:334
  124.7 12.6 %all_to_all.27 = bf16[32,16,128]{2,1,0:T(8,128)(2,1)S(1)} all-to-all(bf16[32,16,128]{2,1,0:T(8,128)(2,1)S(1)} %shard_map.87), channel_id=1, replica_groups=mesh['dp_0'=8,'dp_1'=4,'mp_0'=4,'mp_1'=2] {'dp_0','dp_1'}, dimensions={0} | all-to-all | bytes 262144 | tf_op jit(solution)/shard_map/all_to_all | solution.py:334
  137.4 4.7 %collective-permute-done.21.b3 = bf16[24,16,128]{2,1,0:T(8,128)(2,1)S(1)} collective-permute-done((bf16[24,16,128]{2,1,0:T(8,128)(2,1)S(1)}, bf16[24,16,128]{2,1,0:T(8,128)(2,1)S(1)}, u32[]{:S(2)}, u32[]{:S(2)}) %collective-permute-start.21) | collective-permute-done | bytes 98336 | tf_op jit(solution)/shard_map/ppermute | solution.py:326
  142.0 5.0 %collective-permute-done.19.b2 = bf16[24,16,128]{2,1,0:T(8,128)(2,1)S(1)} collective-permute-done((bf16[24,16,128]{2,1,0:T(8,128)(2,1)S(1)}, bf16[24,16,128]{2,1,0:T(8,128)(2,1)S(1)}, u32[]{:S(2)}, u32[]{:S(2)}) %collective-permute-start.19) | collective-permute-done | bytes 98336 | tf_op jit(solution)/shard_map/ppermute | solution.py:326
  147.1 4.0 %collective-permute-done.17.b1 = bf16[24,16,128]{2,1,0:T(8,128)(2,1)S(1)} collective-permute-done((bf16[24,16,128]{2,1,0:T(8,128)(2,1)S(1)}, bf16[24,16,128]{2,1,0:T(8,128)(2,1)S(1)}, u32[]{:S(2)}, u32[]{:S(2)}) %collective-permute-start.17) | collective-permute-done | bytes 98336 | tf_op jit(solution)/shard_map/ppermute | solution.py:326
  151.1 8.4 %collective-permute-start.16 = (bf16[24,16,128]{2,1,0:T(8,128)(2,1)S(1)}, bf16[24,16,128]{2,1,0:T(8,128)(2,1)S(1)}, u32[]{:S(2)}, u32[]{:S(2)}) collective-permute-start(bf16[24,16,128]{2,1,0:T(8,128)(2,1)S(1)} %slice.4.b0), channel_id=1, source_target_pairs={{0,1},{1,0},{2,3},{3,2},{4,5},{5,4},{6,7},{7,6},{8,9},{9,8},{10,11... | collective-permute-start | bytes 294920 | tf_op jit(solution)/shard_map/ppermute | solution.py:330
  159.5 0.5 collective-permute-start.20
  160.0 0.3 collective-permute-start.18
  160.3 2.3 %copy-done.1 = bf16[8,384,768]{2,1,0:T(8,128)(2,1)S(1)} copy-done((bf16[8,384,768]{2,1,0:T(8,128)(2,1)S(1)}, bf16[8,384,768]{2,1,0:T(8,128)(2,1)}, u32[]{:S(2)}) %copy-start.1) | copy-done | bytes 4718616
  162.7 5.2 %shard_map.86.fed = bf16[8,384,768]{2,1,0:T(8,128)(2,1)S(1)} custom-call(bf16[512,384]{1,0:T(8,128)(2,1)S(1)} %copy-done.4, bf16[8,384,768]{2,1,0:T(8,128)(2,1)S(1)} %copy-done.1, bf16[512,768]{1,0:T(8,128)(2,1)S(1)} %copy-done.3, bf16[512,768]{1,0:T(8,128)(2,1)} %collective-permute-done.4.rest_1_, bf16[512,768]{1,0:T(8,128)(2,1)} %collective-permute-done.5.rest_2_, ...), custom_call_target="tpu_custom_call" | custom-call | flops 6000000000 | bytes 1048576 | tf_op jit(solution)/shard_map/pallas_call | solution.py:245
  167.9 1.8 %shard_map.88 = (bf16[1,384,6144]{2,1,0:T(8,128)(2,1)}, bf16[64,6144]{1,0:T(8,128)(2,1)S(1)}) custom-call(bf16[8,384,768]{2,1,0:T(8,128)(2,1)S(1)} %shard_map.86.fed, bf16[384,64]{1,0:T(8,128)(2,1)S(1)} %get-tuple-element.37.basis, bf16[24,16,128]{2,1,0:T(8,128)(2,1)S(1)} %slice.4.b0, bf16[24,16,128]{2,1,0:T(8,128)(2,1)S(1)} %collective-permute-done.17.b1, ...), custom_call_target="tpu_custom_call" | custom-call | flops 1000000000 | bytes 1048576 | tf_op jit(solution)/shard_map/pallas_call | solution.py:282
  169.7 2.8 %shard_map.89 = (bf16[1,384,6144]{2,1,0:T(8,128)(2,1)}, f32[192,384]{1,0:T(8,128)}, bf16[64,6144]{1,0:T(8,128)(2,1)}) custom-call(bf16[8,384,768]{2,1,0:T(8,128)(2,1)S(1)} %shard_map.86.fed, bf16[384,64]{1,0:T(8,128)(2,1)S(1)} %get-tuple-element.37.basis, bf16[24,16,128]{2,1,0:T(8,128)(2,1)S(1)} %collective-permute-done.16.b0, ...), custom_call_target="tpu_custom_call", output_to_operand_aliasing={{0}: (7, {})} | custom-call | flops 1000000000 | bytes 1048576 | tf_op jit(solution)/shard_map/pallas_call | solution.py:313
  (47 shorter events, 0.6 us)
Async XLA Ops:
  0.6 1.1 copy-start.2
  1.8 1.1 copy-start.5
  3.3 4.3 %collective-permute-start = (f32[64,512]{1,0:T(8,128)S(1)}, f32[64,512]{1,0:T(8,128)S(1)}, u32[]{:S(2)}, u32[]{:S(2)}) collective-permute-start(f32[64,512]{1,0:T(8,128)S(1)} %shard_map.77.a), channel_id=1, source_target_pairs={{0,1},{1,0},{2,3},{3,2},{4,5},{5,4},{6,7},{7,6},{8,9},{9,8},{10,11... | collective-permute-start | bytes 393224 | tf_op jit(solution)/shard_map/ppermute | solution.py:330
  7.6 8.4 %collective-permute-start.3 = (bf16[64,512]{1,0:T(8,128)(2,1)S(1)}, bf16[64,512]{1,0:T(8,128)(2,1)S(1)}, u32[]{:S(2)}, u32[]{:S(2)}) collective-permute-start(bf16[64,512]{1,0:T(8,128)(2,1)S(1)} %get-tuple-element.24), channel_id=1, source_target_pairs={{0,6},{2,0},{4,2},{6,4},{1,7},{3,1},{5,3},{7,5},{8,14},{10,8},{12,... | collective-permute-start | bytes 196616 | tf_op jit(solution)/shard_map/ppermute | solution.py:326
  8.7 7.3 %collective-permute-start.2 = (bf16[64,512]{1,0:T(8,128)(2,1)S(1)}, bf16[64,512]{1,0:T(8,128)(2,1)S(1)}, u32[]{:S(2)}, u32[]{:S(2)}) collective-permute-start(bf16[64,512]{1,0:T(8,128)(2,1)S(1)} %get-tuple-element.24), channel_id=1, source_target_pairs={{0,4},{2,6},{4,0},{6,2},{1,5},{3,7},{5,1},{7,3},{8,12},{10,14},{12... | collective-permute-start | bytes 196616 | tf_op jit(solution)/shard_map/ppermute | solution.py:326
  9.0 6.9 %collective-permute-start.1 = (bf16[64,512]{1,0:T(8,128)(2,1)S(1)}, bf16[64,512]{1,0:T(8,128)(2,1)S(1)}, u32[]{:S(2)}, u32[]{:S(2)}) collective-permute-start(bf16[64,512]{1,0:T(8,128)(2,1)S(1)} %get-tuple-element.24), channel_id=1, source_target_pairs={{0,2},{2,4},{4,6},{6,0},{1,3},{3,5},{5,7},{7,1},{8,10},{10,12},{12... | collective-permute-start | bytes 196616 | tf_op jit(solution)/shard_map/ppermute | solution.py:326
  9.7 1.1 copy-start.6
  10.9 2.3 %copy-start.8 = (bf16[1,384,6144]{2,1,0:T(8,128)(2,1)S(1)}, bf16[1,384,6144]{2,1,0:T(8,128)(2,1)}, u32[]{:S(2)}) copy-start(bf16[1,384,6144]{2,1,0:T(8,128)(2,1)} %param.7) | copy-start | bytes 14155780
  13.2 2.8 %copy-start.4 = (bf16[512,384]{1,0:T(8,128)(2,1)S(1)}, bf16[512,384]{1,0:T(8,128)(2,1)}, u32[]{:S(2)}) copy-start(bf16[512,384]{1,0:T(8,128)(2,1)} %acts.5) | copy-start | bytes 1179652
  15.9 49.6 %copy-start = (bf16[8,384,768]{2,1,0:T(8,128)(2,1)}, bf16[8,384,768]{2,1,0:T(8,128)(2,1)S(1)}, u32[]{:S(2)}) copy-start(bf16[8,384,768]{2,1,0:T(8,128)(2,1)S(1)} %get-tuple-element.23.error) | copy-start | bytes 14155780
  15.9 42.4 %copy-start.3 = (bf16[512,768]{1,0:T(8,128)(2,1)S(1)}, bf16[512,768]{1,0:T(8,128)(2,1)}, u32[]{:S(2)}) copy-start(bf16[512,768]{1,0:T(8,128)(2,1)} %rest_0_.1) | copy-start | bytes 2359300
  49.6 13.9 %copy-start.11 = (f32[64,384]{1,0:T(8,128)}, f32[64,384]{1,0:T(8,128)S(1)}, u32[]{:S(2)}) copy-start(f32[64,384]{1,0:T(8,128)S(1)} %get-tuple-element.29.left) | copy-start | bytes 294916
  50.2 13.3 %collective-permute-start.11 = (f32[4,64,768]{2,1,0:T(8,128)S(1)}, f32[4,64,768]{2,1,0:T(8,128)S(1)}, u32[]{:S(2)}, u32[]{:S(2)}) collective-permute-start(f32[4,64,768]{2,1,0:T(8,128)S(1)} %shard_map.83), channel_id=1, source_target_pairs={{0,1},{1,0},{2,3},{3,2},{4,5},{5,4},{6,7},{7,6},{8,9},{9,8},{10,11... | collective-permute-start | bytes 2359304 | tf_op jit(solution)/shard_map/ppermute | solution.py:330
  54.2 2.1 %collective-permute-start.7 = (f32[64,640]{1,0:T(8,128)S(1)}, f32[64,640]{1,0:T(8,128)S(1)}, u32[]{:S(2)}, u32[]{:S(2)}) collective-permute-start(f32[64,640]{1,0:T(8,128)S(1)} %get-tuple-element.28), channel_id=1, source_target_pairs={{0,1},{1,0},{2,3},{3,2},{4,5},{5,4},{6,7},{7,6},{8,9},{9,8},{10,11... | collective-permute-start | bytes 491528 | tf_op jit(solution)/shard_map/ppermute | solution.py:330
  56.4 5.5 %collective-permute-start.10 = (f32[64,640]{1,0:T(8,128)S(1)}, f32[64,640]{1,0:T(8,128)S(1)}, u32[]{:S(2)}, u32[]{:S(2)}) collective-permute-start(f32[64,640]{1,0:T(8,128)S(1)} %add.3.own), channel_id=1, source_target_pairs={{0,6},{2,0},{4,2},{6,4},{1,7},{3,1},{5,3},{7,5},{8,14},{10,8},{12,... | collective-permute-start | bytes 491528 | tf_op jit(solution)/shard_map/ppermute | solution.py:326
  58.3 56.9 %collective-permute-start.6 = (bf16[512,768]{1,0:T(8,128)(2,1)S(1)}, bf16[512,768]{1,0:T(8,128)(2,1)S(1)}, u32[]{:S(2)}, u32[]{:S(2)}) collective-permute-start(bf16[512,768]{1,0:T(8,128)(2,1)S(1)} %copy-done.3), channel_id=1, source_target_pairs={{0,2},{2,4},{4,6},{6,0},{1,3},{3,5},{5,7},{7,1},{8,10},{10,12},{12... | collective-permute-start | bytes 2359304 | tf_op jit(solution)/shard_map/ppermute | solution.py:326
  58.4 56.9 %collective-permute-start.5 = (bf16[512,768]{1,0:T(8,128)(2,1)S(1)}, bf16[512,768]{1,0:T(8,128)(2,1)}, u32[]{:S(2)}, u32[]{:S(2)}) collective-permute-start(bf16[512,768]{1,0:T(8,128)(2,1)S(1)} %copy-done.3), channel_id=1, source_target_pairs={{0,4},{2,6},{4,0},{6,2},{1,5},{3,7},{5,1},{7,3},{8,12},{10,14},{12... | collective-permute-start | bytes 2359304 | tf_op jit(solution)/shard_map/ppermute | solution.py:326
  59.8 55.5 %collective-permute-start.4 = (bf16[512,768]{1,0:T(8,128)(2,1)S(1)}, bf16[512,768]{1,0:T(8,128)(2,1)}, u32[]{:S(2)}, u32[]{:S(2)}) collective-permute-start(bf16[512,768]{1,0:T(8,128)(2,1)S(1)} %copy-done.3), channel_id=1, source_target_pairs={{0,6},{2,0},{4,2},{6,4},{1,7},{3,1},{5,3},{7,5},{8,14},{10,8},{12,... | collective-permute-start | bytes 2359304 | tf_op jit(solution)/shard_map/ppermute | solution.py:326
  61.9 35.5 %collective-permute-start.9 = (f32[64,640]{1,0:T(8,128)S(1)}, f32[64,640]{1,0:T(8,128)S(1)}, u32[]{:S(2)}, u32[]{:S(2)}) collective-permute-start(f32[64,640]{1,0:T(8,128)S(1)} %add.3.own), channel_id=1, source_target_pairs={{0,4},{2,6},{4,0},{6,2},{1,5},{3,7},{5,1},{7,3},{8,12},{10,14},{12... | collective-permute-start | bytes 491528 | tf_op jit(solution)/shard_map/ppermute | solution.py:326
  63.5 38.4 %collective-permute-start.8 = (f32[64,640]{1,0:T(8,128)S(1)}, f32[64,640]{1,0:T(8,128)S(1)}, u32[]{:S(2)}, u32[]{:S(2)}) collective-permute-start(f32[64,640]{1,0:T(8,128)S(1)} %add.3.own), channel_id=1, source_target_pairs={{0,2},{2,4},{4,6},{6,0},{1,3},{3,5},{5,7},{7,1},{8,10},{10,12},{12... | collective-permute-start | bytes 491528 | tf_op jit(solution)/shard_map/ppermute | solution.py:326
  67.0 43.1 %all-to-all-start.2 = ((f32[4,64,768]{2,1,0:T(8,128)}), f32[4,64,768]{2,1,0:T(8,128)S(1)}, u32[]{:S(2)}, u32[]{:S(2)}) async-start(f32[4,64,768]{2,1,0:T(8,128)} %shard_map.84), calls=%async_computation.2 | async-start | bytes 1572864 | tf_op jit(solution)/shard_map/all_to_all | solution.py:368
  101.9 0.7 copy-start.9
  102.5 0.9 copy-start.10
  103.5 0.9 copy-start.12
  111.4 13.3 %all-to-all-start.3 = ((bf16[32,16,128]{2,1,0:T(8,128)(2,1)}), bf16[32,16,128]{2,1,0:T(8,128)(2,1)S(1)}, u32[]{:S(2)}, u32[]{:S(2)}) async-start(bf16[32,16,128]{2,1,0:T(8,128)(2,1)} %shard_map.85), calls=%async_computation.3 | async-start | bytes 262144 | tf_op jit(solution)/shard_map/all_to_all | solution.py:334
  115.3 44.2 %collective-permute-start.12 = (bf16[512,768]{1,0:T(8,128)(2,1)S(1)}, bf16[512,768]{1,0:T(8,128)(2,1)}, u32[]{:S(2)}, u32[]{:S(2)}) collective-permute-start(bf16[512,768]{1,0:T(8,128)(2,1)S(1)} %copy-done.3), channel_id=1, source_target_pairs={{0,1},{1,0},{2,3},{3,2},{4,5},{5,4},{6,7},{7,6},{8,9},{9,8},{10,11... | collective-permute-start | bytes 2359304 | tf_op jit(solution)/shard_map/ppermute | solution.py:330
  118.0 41.5 %collective-permute-start.13 = (bf16[512,768]{1,0:T(8,128)(2,1)}, bf16[512,768]{1,0:T(8,128)(2,1)}, u32[]{:S(2)}, u32[]{:S(2)}) collective-permute-start(bf16[512,768]{1,0:T(8,128)(2,1)} %collective-permute-done.4.rest_1_), channel_id=1, source_target_pairs={{0,1},{1,0},{2,3},{3,2},{4,5},{5,4},{6,7},{7,6},{8,9},{9,8},{10,11... | collective-permute-start | bytes 2359304 | tf_op jit(solution)/shard_map/ppermute | solution.py:330
  118.1 41.9 %collective-permute-start.14 = (bf16[512,768]{1,0:T(8,128)(2,1)}, bf16[512,768]{1,0:T(8,128)(2,1)}, u32[]{:S(2)}, u32[]{:S(2)}) collective-permute-start(bf16[512,768]{1,0:T(8,128)(2,1)} %collective-permute-done.5.rest_2_), channel_id=1, source_target_pairs={{0,1},{1,0},{2,3},{3,2},{4,5},{5,4},{6,7},{7,6},{8,9},{9,8},{10,11... | collective-permute-start | bytes 2359304 | tf_op jit(solution)/shard_map/ppermute | solution.py:330
  118.5 41.8 %collective-permute-start.15 = (bf16[512,768]{1,0:T(8,128)(2,1)S(1)}, bf16[512,768]{1,0:T(8,128)(2,1)}, u32[]{:S(2)}, u32[]{:S(2)}) collective-permute-start(bf16[512,768]{1,0:T(8,128)(2,1)S(1)} %collective-permute-done.6.rest_3_), channel_id=1, source_target_pairs={{0,1},{1,0},{2,3},{3,2},{4,5},{5,4},{6,7},{7,6},{8,9},{9,8},{10,11... | collective-permute-start | bytes 2359304 | tf_op jit(solution)/shard_map/ppermute | solution.py:330
  137.3 4.8 %collective-permute-start.21 = (bf16[24,16,128]{2,1,0:T(8,128)(2,1)S(1)}, bf16[24,16,128]{2,1,0:T(8,128)(2,1)S(1)}, u32[]{:S(2)}, u32[]{:S(2)}) collective-permute-start(bf16[24,16,128]{2,1,0:T(8,128)(2,1)S(1)} %slice.4.b0), channel_id=1, source_target_pairs={{0,2},{2,4},{4,6},{6,0},{1,3},{3,5},{5,7},{7,1},{8,10},{10,12},{12... | collective-permute-start | bytes 294920 | tf_op jit(solution)/shard_map/ppermute | solution.py:326
  142.0 5.0 %collective-permute-start.19 = (bf16[24,16,128]{2,1,0:T(8,128)(2,1)S(1)}, bf16[24,16,128]{2,1,0:T(8,128)(2,1)S(1)}, u32[]{:S(2)}, u32[]{:S(2)}) collective-permute-start(bf16[24,16,128]{2,1,0:T(8,128)(2,1)S(1)} %slice.4.b0), channel_id=1, source_target_pairs={{0,4},{2,6},{4,0},{6,2},{1,5},{3,7},{5,1},{7,3},{8,12},{10,14},{12... | collective-permute-start | bytes 294920 | tf_op jit(solution)/shard_map/ppermute | solution.py:326
  147.1 4.0 %collective-permute-start.17 = (bf16[24,16,128]{2,1,0:T(8,128)(2,1)S(1)}, bf16[24,16,128]{2,1,0:T(8,128)(2,1)S(1)}, u32[]{:S(2)}, u32[]{:S(2)}) collective-permute-start(bf16[24,16,128]{2,1,0:T(8,128)(2,1)S(1)} %slice.4.b0), channel_id=1, source_target_pairs={{0,6},{2,0},{4,2},{6,4},{1,7},{3,1},{5,3},{7,5},{8,14},{10,8},{12,... | collective-permute-start | bytes 294920 | tf_op jit(solution)/shard_map/ppermute | solution.py:326
  151.1 18.6 %collective-permute-start.16 = (bf16[24,16,128]{2,1,0:T(8,128)(2,1)S(1)}, bf16[24,16,128]{2,1,0:T(8,128)(2,1)S(1)}, u32[]{:S(2)}, u32[]{:S(2)}) collective-permute-start(bf16[24,16,128]{2,1,0:T(8,128)(2,1)S(1)} %slice.4.b0), channel_id=1, source_target_pairs={{0,1},{1,0},{2,3},{3,2},{4,5},{5,4},{6,7},{7,6},{8,9},{9,8},{10,11... | collective-permute-start | bytes 294920 | tf_op jit(solution)/shard_map/ppermute | solution.py:330
  159.5 10.2 %collective-permute-start.22 = (bf16[24,16,128]{2,1,0:T(8,128)(2,1)S(1)}, bf16[24,16,128]{2,1,0:T(8,128)(2,1)S(1)}, u32[]{:S(2)}, u32[]{:S(2)}) collective-permute-start(bf16[24,16,128]{2,1,0:T(8,128)(2,1)S(1)} %collective-permute-done.21.b3), channel_id=1, source_target_pairs={{0,1},{1,0},{2,3},{3,2},{4,5},{5,4},{6,7},{7,6},{8,9},{9,8},{10,11... | collective-permute-start | bytes 294920 | tf_op jit(solution)/shard_map/ppermute | solution.py:330
  159.5 10.2 %collective-permute-start.20 = (bf16[24,16,128]{2,1,0:T(8,128)(2,1)S(1)}, bf16[24,16,128]{2,1,0:T(8,128)(2,1)S(1)}, u32[]{:S(2)}, u32[]{:S(2)}) collective-permute-start(bf16[24,16,128]{2,1,0:T(8,128)(2,1)S(1)} %collective-permute-done.19.b2), channel_id=1, source_target_pairs={{0,1},{1,0},{2,3},{3,2},{4,5},{5,4},{6,7},{7,6},{8,9},{9,8},{10,11... | collective-permute-start | bytes 294920 | tf_op jit(solution)/shard_map/ppermute | solution.py:330
  160.0 9.7 %collective-permute-start.18 = (bf16[24,16,128]{2,1,0:T(8,128)(2,1)S(1)}, bf16[24,16,128]{2,1,0:T(8,128)(2,1)S(1)}, u32[]{:S(2)}, u32[]{:S(2)}) collective-permute-start(bf16[24,16,128]{2,1,0:T(8,128)(2,1)S(1)} %collective-permute-done.17.b1), channel_id=1, source_target_pairs={{0,1},{1,0},{2,3},{3,2},{4,5},{5,4},{6,7},{7,6},{8,9},{9,8},{10,11... | collective-permute-start | bytes 294920 | tf_op jit(solution)/shard_map/ppermute | solution.py:330
  160.3 2.3 %copy-start.1 = (bf16[8,384,768]{2,1,0:T(8,128)(2,1)S(1)}, bf16[8,384,768]{2,1,0:T(8,128)(2,1)}, u32[]{:S(2)}) copy-start(bf16[8,384,768]{2,1,0:T(8,128)(2,1)} %copy-done) | copy-start | bytes 14155780
  167.9 1.8 %copy-start.7 = (f32[384,192]{0,1:T(8,128)S(1)}, f32[384,192]{0,1:T(8,128)}, u32[]{:S(2)}) copy-start(f32[384,192]{0,1:T(8,128)} %param.9) | copy-start | bytes 884740

commit v4 on v3

--- a/solution.py
+++ b/solution.py
@@ -67,11 +67,22 @@
     return pl.ds(pl.multiple_of(block * COLS, COLS), COLS)
 
 
-def grads_sketch_body(grads, sketch_t, out, held, sem):
-    cut = pltpu.make_async_copy(sketch_t.at[:, columns(block_at(0, False))], held, sem)
+def grads_sketch_body(grads, sketch_t, out, held_s, held_g, sems):
+    cut = pltpu.make_async_copy(
+        sketch_t.at[:, columns(block_at(0, False))], held_s, sems.at[4]
+    )
     cut.start()
+    part = TOK // 4
+    loads = [
+        pltpu.make_async_copy(grads.at[pl.ds(part * i, part)], held_g.at[i], sems.at[i])
+        for i in range(4)
+    ]
+    for c in loads:
+        c.start()
     cut.wait()
-    out[...] = dot(held[...], grads[...], NT)
+    for i in range(4):
+        loads[i].wait()
+        out[:, part * i : part * (i + 1)] = dot(held_s[...], held_g[i], NT)
 
 
 def grads_sketch(grads, sketch_t):
@@ -79,9 +90,13 @@
         grads_sketch_body,
         on_chip((RANK, TOK), F32),
         10**8,
-        in_specs=[VMEM, HBM],
+        in_specs=[HBM, HBM],
         out_specs=VMEM,
-        scratch_shapes=[pltpu.VMEM((RANK, COLS), BF16), pltpu.SemaphoreType.DMA(())],
+        scratch_shapes=[
+            pltpu.VMEM((RANK, COLS), BF16),
+            pltpu.VMEM((4, TOK // 4, COLS), BF16),
+            pltpu.SemaphoreType.DMA((5,)),
+        ],
     )(grads, sketch_t)
 
 
@@ -95,28 +110,36 @@
     return call(pair_body, (on_chip(a.shape, F32), on_chip(a.shape, BF16)), 10**7)(a, b)
 
 
-def error_sketch_body(error, sketch_t, out, held, sems):
+def error_sketch_body(error, sketch_t, out, held, turned, sems):
     places = [columns(block_at(k % 4, k >= 4)) for k in range(8)]
+    load = pltpu.make_async_copy(sketch_t, turned, sems.at[8])
+    load.start()
     copies = [
         pltpu.make_async_copy(error.at[:, places[k]], held.at[k], sems.at[k]) for k in range(8)
     ]
     for c in copies:
         c.start()
+    load.wait()
     acc = jnp.zeros((RANK, ROWS), F32)
     for k in range(8):
         copies[k].wait()
-        acc = acc + dot(sketch_t[:, places[k]], held[k], NT)
+        acc = acc + dot(turned[:, places[k]], held[k], NT)
     out[...] = acc
 
 
 def error_sketch(error, sketch_t):
     return call(
         error_sketch_body,
-        (on_chip((RANK, ROWS), F32), on_chip((8, ROWS, COLS), BF16)),
+        on_chip((RANK, ROWS), F32),
         3 * 10**9,
-        in_specs=[HBM, VMEM],
-        out_specs=(VMEM, VMEM),
-        scratch_shapes=[pltpu.SemaphoreType.DMA((8,))],
+        12,
+        in_specs=[HBM, HBM],
+        out_specs=VMEM,
+        scratch_shapes=[
+            pltpu.VMEM((8, ROWS, COLS), BF16),
+            pltpu.VMEM((RANK, D), BF16),
+            pltpu.SemaphoreType.DMA((9,)),
+        ],
     )(error, sketch_t)
 
 
@@ -167,25 +190,39 @@
     )(tiles, acts)
 
 
-def right_far_body(left_terms, error, out):
-    for k in range(4):
-        out[k] = halves_added(dot(left_terms[...], error[4 + k]))
-
-
-def right_near_body(left_terms, error, got, out):
+def right_blocks_body(left_terms, error, far, near, held, sems):
     y = lax.axis_index(YY)
-    for k in range(4):
-        out[lax.rem(y + k, 4)] = halves_added(dot(left_terms[...], error[k])) + got[k]
-
-
-def right_far(left_terms, error):
-    shape = on_chip((4, RANK, COLS), F32)
-    return call(right_far_body, shape, 10**9)(left_terms, error)
-
-
-def right_near(left_terms, error, got):
-    shape = on_chip((4, RANK, COLS), F32)
-    return call(right_near_body, shape, 10**9)(left_terms, error, got)
+    order = [(k, True) for k in range(4)] + [(k, False) for k in range(4)]
+    copies = [
+        pltpu.make_async_copy(error.at[:, columns(block_at(*o))], held.at[i], sems.at[i])
+        for i, o in enumerate(order)
+    ]
+    for c in copies:
+        c.start()
+    for i, (k, other) in enumerate(order):
+        copies[i].wait()
+        out = far if other else near
+        out[lax.rem(y + k, 4)] = halves_added(dot(left_terms[...], held[i]))
+
+
+def right_blocks(left_terms, error):
+    return call(
+        right_blocks_body,
+        (on_chip((4, RANK, COLS), F32), on_chip((4, RANK, COLS), F32)),
+        10**10,
+        12,
+        in_specs=[VMEM, HBM],
+        out_specs=(VMEM, VMEM),
+        scratch_shapes=[pltpu.VMEM((8, ROWS, COLS), BF16), pltpu.SemaphoreType.DMA((8,))],
+    )(left_terms, error)
+
+
+def add_body(a, b, out):
+    out[...] = a[...] + b[...]
+
+
+def add(a, b):
+    return call(add_body, on_chip(a.shape, F32), 10**7)(a, b)
 
 
 def factor_body(own, one, two, three, left, inverse_out, basis_out, acts_left):
@@ -231,29 +268,48 @@
 
 
 def fed_body(acts, error, *rest):
-    grads, out, held, sems = rest[:8], rest[8], rest[9], rest[10]
-    loads = [pltpu.make_async_copy(grads[k], held.at[k], sems.at[k]) for k in range(8)]
-    for c in loads:
-        c.start()
+    grads, out, held, held_e, held_o, sems = rest[:8], rest[8], *rest[9:]
+    errors = [
+        pltpu.make_async_copy(
+            error.at[:, columns(block_at(k % 4, k >= 4))], held_e.at[k], sems.at[k]
+        )
+        for k in range(8)
+    ]
+    loads = [pltpu.make_async_copy(grads[k], held.at[k], sems.at[8 + k]) for k in range(8)]
+    for k in range(8):
+        loads[k].start()
+        errors[k].start()
     turned = acts[...].T
+    stores = []
     for k in range(8):
         loads[k].wait()
-        out[k] = (dot(turned, held[k]) + error[k].astype(F32)).astype(BF16)
+        errors[k].wait()
+        held_o[k] = (dot(turned, held[k]) + held_e[k].astype(F32)).astype(BF16)
+        store = pltpu.make_async_copy(held_o.at[k], out.at[k], sems.at[16 + k])
+        store.start()
+        stores.append(store)
+    for store in stores:
+        store.wait()
 
 
 def fed_of(acts, error, grads):
     return call(
         fed_body,
-        on_chip((8, ROWS, COLS), BF16),
+        pltpu.HBM((8, ROWS, COLS), BF16),
         6 * 10**9,
-        16,
-        in_specs=[VMEM, VMEM] + [HBM] * 8,
-        out_specs=VMEM,
-        scratch_shapes=[pltpu.VMEM((8, TOK, COLS), BF16), pltpu.SemaphoreType.DMA((8,))],
-    )(acts, error, *grads)
-
-
-def block_outputs(fed, basis, blocks, first, error_new, sketch_t, held, sems):
+        24,
+        in_specs=[VMEM, HBM] + [HBM] * 8,
+        out_specs=HBM,
+        scratch_shapes=[
+            pltpu.VMEM((8, TOK, COLS), BF16),
+            pltpu.VMEM((8, ROWS, COLS), BF16),
+            pltpu.VMEM((8, ROWS, COLS), BF16),
+            pltpu.SemaphoreType.DMA((24,)),
+        ],
+    )(acts, error, *map(in_hbm, grads))
+
+
+def block_outputs(fed, first, basis, blocks, error_new, sketch_t, held, sems):
     stores = []
     scaled = (basis[...].astype(F32) * (1 / WORKERS)).astype(BF16)
     for i, tiles in enumerate(blocks):
@@ -261,7 +317,7 @@
         where = block_at(k % 4, k >= 4)
         rows = [jnp.concatenate([tiles[4 * j + r] for j in range(6)], axis=1) for r in range(4)]
         block = jnp.concatenate(rows, axis=0)
-        held[i] = (fed[k].astype(F32) - dot(scaled, block)).astype(BF16)
+        held[i] = (fed[i].astype(F32) - dot(scaled, block)).astype(BF16)
         store = pltpu.make_async_copy(held.at[i], error_new.at[0, :, columns(where)], sems.at[i])
         store.start()
         stores.append(store)
@@ -269,24 +325,38 @@
     return stores
 
 
-def near_outputs_body(fed, basis, b0, b1, b2, b3, error_new, sketch_t, held, sems):
-    stores = block_outputs(fed, basis, (b0, b1, b2, b3), 0, error_new, sketch_t, held, sems)
-    for store in stores:
-        store.wait()
-
-
-OUTPUT_SCRATCH = [pltpu.VMEM((4, ROWS, COLS), BF16), pltpu.SemaphoreType.DMA((4,))]
+def near_outputs_body(
+    fed, basis, b0, b1, b2, b3, error_new, sketch_t, fed_far, held_f, held, sems, load_sems
+):
+    loads = [
+        pltpu.make_async_copy(
+            fed.at[k], held_f.at[k] if k < 4 else fed_far.at[k - 4], load_sems.at[k]
+        )
+        for k in range(8)
+    ]
+    for c in loads:
+        c.start()
+    for c in loads[:4]:
+        c.wait()
+    stores = block_outputs(held_f, 0, basis, (b0, b1, b2, b3), error_new, sketch_t, held, sems)
+    for c in loads[4:] + stores:
+        c.wait()
 
 
 def near_outputs(fed, basis, blocks):
     return call(
         near_outputs_body,
-        (sds((1, ROWS, D), BF16), on_chip((RANK, D), BF16)),
+        (sds((1, ROWS, D), BF16), on_chip((RANK, D), BF16), on_chip((4, ROWS, COLS), BF16)),
         10**9,
         12,
-        in_specs=[VMEM] * 6,
-        out_specs=(HBM, VMEM),
-        scratch_shapes=OUTPUT_SCRATCH,
+        in_specs=[HBM] + [VMEM] * 5,
+        out_specs=(HBM, VMEM, VMEM),
+        scratch_shapes=[
+            pltpu.VMEM((4, ROWS, COLS), BF16),
+            pltpu.VMEM((4, ROWS, COLS), BF16),
+            pltpu.SemaphoreType.DMA((4,)),
+            pltpu.SemaphoreType.DMA((8,)),
+        ],
     )(fed, basis, *blocks)
 
 
@@ -296,7 +366,7 @@
     for k in range(4):
         place = columns(block_at(k, False))
         sketch_t[:, place] = near_t[:, place]
-    stores = block_outputs(fed, basis, (b0, b1, b2, b3), 4, error_new, sketch_t, held, sems)
+    stores = block_outputs(fed, 4, basis, (b0, b1, b2, b3), error_new, sketch_t, held, sems)
     w = lax.axis_index(DP)
     quarter = lax.rem(w, 4)
     own = sketch_t[:, columns(w // 4)]
@@ -309,7 +379,7 @@
         store.wait()
 
 
-def far_outputs(fed, basis, blocks, momentum_t, error_new, near_t):
+def far_outputs(fed_far, basis, blocks, momentum_t, error_new, near_t):
     return call(
         far_outputs_body,
         (sds((1, ROWS, D), BF16), sds((192, ROWS), F32), sds((RANK, D), BF16)),
@@ -317,9 +387,9 @@
         12,
         in_specs=[VMEM] * 7 + [HBM, VMEM],
         out_specs=(HBM, VMEM, VMEM),
-        scratch_shapes=OUTPUT_SCRATCH,
+        scratch_shapes=[pltpu.VMEM((4, ROWS, COLS), BF16), pltpu.SemaphoreType.DMA((4,))],
         input_output_aliases={7: 0},
-    )(fed, basis, *blocks, momentum_t, error_new, near_t)
+    )(fed_far, basis, *blocks, momentum_t, error_new, near_t)
 
 
 def along_y(x, k):
@@ -334,20 +404,25 @@
     return lax.all_to_all(x, DP, split_axis=0, concat_axis=0, tiled=True)
 
 
+def in_hbm(x):
+    return pltpu.with_memory_space_constraint(x, pltpu.HBM)
+
+
 def after(x, *others):
     return lax.optimization_barrier((x, *others))[0]
 
 
 def step(activations, out_grads, error, sketch, momentum):
-    own_error = error[0]
-    sketch_t = sketch.T
+    own_error = in_hbm(error[0])
+    sketch_t = in_hbm(sketch.T)
+    own_grads, out_grads = out_grads, in_hbm(out_grads)
 
     mine = grads_sketch(out_grads, sketch_t)
     pair, rounded = pair_sum(mine, other_core(mine))
     others = []
     for k in (1, 2, 3):
         others.append(along_y(rounded, k))
-    from_error, held_error = error_sketch(own_error, sketch_t)
+    from_error = error_sketch(own_error, sketch_t)
     tiles = left_term(pair, others, activations, from_error)
 
     held = after(out_grads, *others)
@@ -360,14 +435,17 @@
     tiles = to_workers(copies)
 
     left, left_terms, small = left_products(tiles, activations)
-    small = small + other_core(small)
-    small_parts = [along_y(small, k) for k in (1, 2, 3)]
-    send = right_far(left_terms, held_error)
-    got = other_core(send)
-    q = right_near(left_terms, held_error, got)
+    other_small = other_core(small)
+    far, near = right_blocks(left_terms, own_error)
+    got = other_core(far)
+    small_parts = []
+    small = add(small, other_small)
+    for k in (1, 2, 3):
+        small_parts.append(along_y(small, k))
+    q = add(near, got)
     terms = lax.all_to_all(q, YY, split_axis=0, concat_axis=0, tiled=True)
     inverse, basis, acts_left = factor(small, small_parts, left)
-    pieces = right_term(inverse, acts_left, out_grads, terms)
+    pieces = right_term(inverse, acts_left, own_grads, terms)
 
     near_g = (out_grads, *gathered)
     far_g = []
@@ -375,16 +453,16 @@
         far_g.append(other_core(after(near_g[k], pieces)))
     arrived = to_workers(pieces)
     copies = sum_and_copy(arrived, BF16)
-    fed = fed_of(activations, held_error, (*near_g, *far_g))
+    fed = fed_of(activations, own_error, (*near_g, *far_g))
     block = to_workers(copies)[:24]
     n3, n2, n1 = along_y(block, 1), along_y(block, 2), along_y(block, -1)
     near_n = (block, n1, n2, n3)
     far_n = []
     for k in range(4):
         far_n.append(other_core(near_n[k]))
-    error_new, near_t = near_outputs(fed, basis, near_n)
+    error_new, near_t, fed_far = near_outputs(in_hbm(fed), basis, near_n)
     error_new, momentum_t, sketch_t = far_outputs(
-        fed, basis, far_n, momentum.T, error_new, near_t
+        fed_far, basis, far_n, momentum.T, error_new, near_t
     )
     return error_new, momentum_t.T, sketch_t.T
 

time: 173 us -> 173 us (level)
  local copies, waits for them, and re-layouts: 10.6 us -> 0.07 us
  Pallas kernels: 22.7 us -> 31.3 us
  waiting for transfers between devices: 54.1 us -> 58.9 us
  starting transfers between devices: 38.8 us -> 36.1 us
    unnamed x26 -> x8, local copies, waits for them, and re-layouts: 10.6 us -> 0.06 us
    pallas_call x5 -> x6, Pallas kernels: 10.4 us -> 17.3 us  [the longest x1 6.92 us: fed_of(): call(fed_body, pltpu.HBM((8, ROWS, COLS), BF16), 6 * 10 ** 9, 24, in_spec...]
    ppermute x12, waiting for transfers between devices: 45 us -> 48 us  [along_y(): return lax.ppermute(x, YY, [(i, (i + k) % 4) for i in range(4)])]
  transfers between devices with their start and end apart: 25 -> 25, of which waited for: 9 -> 11; matrix products, arithmetic and copies ran while one was open for 0% -> 0% of each run, Pallas kernels for 11% -> 13%
where the time goes in v4:
time: 173 us
  waiting for transfers between devices  58.9 us (34%)
  blocking collectives  45.6 us (26%)
  starting transfers between devices  36.1 us (21%)
  Pallas kernels  31.3 us (18%)
    ppermute x12, waiting for transfers between devices, along_y(): return lax.ppermute(x, YY, [(i, (i + k) % 4) for i in range(4)])  48 us
    all_to_all x3, blocking collectives, to_workers(): return lax.all_to_all(x, DP, split_axis=0, concat_axis=0, tiled=True)  45.6 us
    ppermute x11, starting transfers between devices, other_core(): return lax.ppermute(x, CC, [(0, 1), (1, 0)])  18.7 us
    ppermute x12, starting transfers between devices, along_y(): return lax.ppermute(x, YY, [(i, (i + k) % 4) for i in range(4)])  9.88 us
    pallas_call x1, Pallas kernels, fed_of(): call(fed_body, pltpu.HBM((8, ROWS, COLS), BF16), 6 * 10 ** 9, 24, in_spec...  6.92 us
    all_to_all x1, waiting for transfers between devices, to_workers(): return lax.all_to_all(x, DP, split_axis=0, concat_axis=0, tiled=True)  6.14 us
    pallas_call x1, Pallas kernels, factor(): call(factor_body, (on_chip((RANK, RANK), F32), on_chip((ROWS, RANK), BF16...  5.75 us
    all_to_all x1, starting transfers between devices, to_workers(): return lax.all_to_all(x, DP, split_axis=0, concat_axis=0, tiled=True)  3.86 us
  transfers between devices with their start and end apart: 25, of which 11 were waited for; matrix products, arithmetic and copies ran while one was open for 0% of the time, Pallas kernels for 13%

profile of v4, /device:TPU:1, one launch (start us, length us, event | category | flops | bytes accessed | tf_op | source)
XLA Modules:
  0.0 172.9 jit_solution(7790035626730257951)
XLA Ops:
  0.6 2.0 %shard_map.76.a = f32[64,512]{1,0:T(8,128)S(1)} custom-call(bf16[512,768]{1,0:T(8,128)(2,1)} %rest_0_.1, bf16[64,6144]{1,0:T(8,128)(2,1)} %bitcast.6), custom_call_target="tpu_custom_call" | custom-call | flops 100000000 | bytes 1048576 | tf_op jit(solution)/shard_map/pallas_call | solution.py:89
  2.6 3.3 %collective-permute-start = (f32[64,512]{1,0:T(8,128)S(1)}, f32[64,512]{1,0:T(8,128)S(1)}, u32[]{:S(2)}, u32[]{:S(2)}) collective-permute-start(f32[64,512]{1,0:T(8,128)S(1)} %shard_map.76.a), channel_id=1, source_target_pairs={{0,1},{1,0},{2,3},{3,2},{4,5},{5,4},{6,7},{7,6},{8,9},{9,8},{10,11... | collective-permute-start | bytes 393224 | tf_op jit(solution)/shard_map/ppermute | solution.py:400
  5.9 1.0 collective-permute-done.b
  6.9 1.1 collective-permute-start.3
  8.0 0.3 collective-permute-start.2
  8.4 0.7 collective-permute-start.1
  9.0 3.8 %shard_map.78.from_error = f32[64,384]{1,0:T(8,128)S(1)} custom-call(bf16[384,6144]{1,0:T(8,128)(2,1)} %bitcast.8, bf16[64,6144]{1,0:T(8,128)(2,1)} %bitcast.7), custom_call_target="tpu_custom_call" | custom-call | flops 3000000000 | bytes 1048576 | tf_op jit(solution)/shard_map/pallas_call | solution.py:131
  12.9 1.3 collective-permute-done.1.one
  14.2 0.2 shard_map.79
  14.4 20.5 %all_to_all.25.arrived = f32[32,8,128]{2,1,0:T(8,128)S(1)} all-to-all(f32[32,8,128]{2,1,0:T(8,128)S(1)} %shard_map.79), channel_id=1, replica_groups=mesh['dp_0'=8,'dp_1'=4,'mp_0'=4,'mp_1'=2] {'dp_0','dp_1'}, dimensions={0} | all-to-all | bytes 262144 | tf_op jit(solution)/shard_map/all_to_all | solution.py:404
  35.0 12.6 %all_to_all.26.tiles = f32[32,8,128]{2,1,0:T(8,128)S(1)} all-to-all(f32[32,8,128]{2,1,0:T(8,128)S(1)} %shard_map.80), channel_id=1, replica_groups=mesh['dp_0'=8,'dp_1'=4,'mp_0'=4,'mp_1'=2] {'dp_0','dp_1'}, dimensions={0} | all-to-all | bytes 262144 | tf_op jit(solution)/shard_map/all_to_all | solution.py:404
  47.6 0.4 shard_map.81
  48.0 3.6 %shard_map.84 = (f32[4,64,768]{2,1,0:T(8,128)S(1)}, f32[4,64,768]{2,1,0:T(8,128)S(1)}) custom-call(bf16[128,384]{1,0:T(8,128)(2,1)S(1)} %get-tuple-element.31.left_terms, bf16[384,6144]{1,0:T(8,128)(2,1)} %bitcast.9), custom_call_target="tpu_custom_call" | custom-call | flops 10000000000 | bytes 1048576 | tf_op jit(solution)/shard_map/pallas_call | solution.py:209
  51.6 3.7 %collective-permute-start.11 = (f32[4,64,768]{2,1,0:T(8,128)S(1)}, f32[4,64,768]{2,1,0:T(8,128)S(1)}, u32[]{:S(2)}, u32[]{:S(2)}) collective-permute-start(f32[4,64,768]{2,1,0:T(8,128)S(1)} %get-tuple-element.33), channel_id=1, source_target_pairs={{0,1},{1,0},{2,3},{3,2},{4,5},{5,4},{6,7},{7,6},{8,9},{9,8},{10,11... | collective-permute-start | bytes 2359304 | tf_op jit(solution)/shard_map/ppermute | solution.py:400
  55.3 0.1 collective-permute-start.7
  55.4 2.0 %collective-permute-done.7.b = f32[64,640]{1,0:T(8,128)S(1)} collective-permute-done((f32[64,640]{1,0:T(8,128)S(1)}, f32[64,640]{1,0:T(8,128)S(1)}, u32[]{:S(2)}, u32[]{:S(2)}) %collective-permute-start.7) | collective-permute-done | bytes 163872 | tf_op jit(solution)/shard_map/ppermute | solution.py:400
  57.4 0.7 collective-permute-start.10
  58.2 0.8 collective-permute-start.6
  59.0 0.8 collective-permute-start.5
  59.7 1.9 %collective-permute-start.4 = (bf16[512,768]{1,0:T(8,128)(2,1)S(1)}, bf16[512,768]{1,0:T(8,128)(2,1)}, u32[]{:S(2)}, u32[]{:S(2)}) collective-permute-start(bf16[512,768]{1,0:T(8,128)(2,1)S(1)} %copy-done), channel_id=1, source_target_pairs={{0,6},{2,0},{4,2},{6,4},{1,7},{3,1},{5,3},{7,5},{8,14},{10,8},{12,... | collective-permute-start | bytes 2359304 | tf_op jit(solution)/shard_map/ppermute | solution.py:396
  61.6 1.3 collective-permute-done.10.three
  62.9 0.9 collective-permute-start.9
  63.8 1.6 collective-permute-start.8
  65.3 1.0 shard_map.85
  66.3 3.7 %all-to-all-start.2 = ((f32[4,64,768]{2,1,0:T(8,128)}), f32[4,64,768]{2,1,0:T(8,128)S(1)}, u32[]{:S(2)}, u32[]{:S(2)}) async-start(f32[4,64,768]{2,1,0:T(8,128)} %shard_map.85), calls=%async_computation.2 | async-start | bytes 1572864 | tf_op jit(solution)/shard_map/all_to_all | solution.py:446
  70.0 27.1 %collective-permute-done.9.two = f32[64,640]{1,0:T(8,128)S(1)} collective-permute-done((f32[64,640]{1,0:T(8,128)S(1)}, f32[64,640]{1,0:T(8,128)S(1)}, u32[]{:S(2)}, u32[]{:S(2)}) %collective-permute-start.9) | collective-permute-done | bytes 163872 | tf_op jit(solution)/shard_map/ppermute | solution.py:396
  97.1 4.6 %collective-permute-done.8.one = f32[64,640]{1,0:T(8,128)S(1)} collective-permute-done((f32[64,640]{1,0:T(8,128)S(1)}, f32[64,640]{1,0:T(8,128)S(1)}, u32[]{:S(2)}, u32[]{:S(2)}) %collective-permute-start.8) | collective-permute-done | bytes 163872 | tf_op jit(solution)/shard_map/ppermute | solution.py:396
  101.7 5.8 %shard_map.83 = (f32[64,64]{1,0:T(8,128)S(1)}, bf16[384,64]{1,0:T(8,128)(2,1)S(1)}, bf16[128,512]{1,0:T(8,128)(2,1)S(1)}) custom-call(f32[64,640]{1,0:T(8,128)S(1)} %shard_map.82.own, f32[64,640]{1,0:T(8,128)S(1)} %collective-permute-done.8.one, f32[64,640]{1,0:T(8,128)S(1)} %collective-permute-done.9.two, f32[64,640]{1,0:T(8,128)S(1)} %collective-permute-done.10.three, ...), custom_call_target="tpu_custom_call" | custom-call | flops 6000000000 | bytes 1048576 | tf_op jit(solution)/shard_map/pallas_call | solution.py:247
  107.4 1.7 all-to-all-done.2.terms
  109.1 1.2 shard_map.86
  110.3 3.9 %all-to-all-start.3 = ((bf16[32,16,128]{2,1,0:T(8,128)(2,1)}), bf16[32,16,128]{2,1,0:T(8,128)(2,1)S(1)}, u32[]{:S(2)}, u32[]{:S(2)}) async-start(bf16[32,16,128]{2,1,0:T(8,128)(2,1)} %shard_map.86), calls=%async_computation.3 | async-start | bytes 262144 | tf_op jit(solution)/shard_map/all_to_all | solution.py:404
  114.2 2.6 %collective-permute-start.12 = (bf16[512,768]{1,0:T(8,128)(2,1)S(1)}, bf16[512,768]{1,0:T(8,128)(2,1)S(1)}, u32[]{:S(2)}, u32[]{:S(2)}) collective-permute-start(bf16[512,768]{1,0:T(8,128)(2,1)S(1)} %copy-done), channel_id=1, source_target_pairs={{0,1},{1,0},{2,3},{3,2},{4,5},{5,4},{6,7},{7,6},{8,9},{9,8},{10,11... | collective-permute-start | bytes 2359304 | tf_op jit(solution)/shard_map/ppermute | solution.py:400
  116.8 0.1 collective-permute-start.13
  116.9 0.4 collective-permute-start.14
  117.4 0.1 collective-permute-start.15
  117.5 6.1 %all-to-all-done.3.arrived = bf16[32,16,128]{2,1,0:T(8,128)(2,1)S(1)} async-done(((bf16[32,16,128]{2,1,0:T(8,128)(2,1)}), bf16[32,16,128]{2,1,0:T(8,128)(2,1)S(1)}, u32[]{:S(2)}, u32[]{:S(2)}) %all-to-all-start.3) | async-done | bytes 131104 | tf_op jit(solution)/shard_map/all_to_all | solution.py:404
  123.6 12.5 %all_to_all.27 = bf16[32,16,128]{2,1,0:T(8,128)(2,1)S(1)} all-to-all(bf16[32,16,128]{2,1,0:T(8,128)(2,1)S(1)} %shard_map.88), channel_id=1, replica_groups=mesh['dp_0'=8,'dp_1'=4,'mp_0'=4,'mp_1'=2] {'dp_0','dp_1'}, dimensions={0} | all-to-all | bytes 262144 | tf_op jit(solution)/shard_map/all_to_all | solution.py:404
  136.3 4.7 %collective-permute-done.18.b3 = bf16[24,16,128]{2,1,0:T(8,128)(2,1)S(1)} collective-permute-done((bf16[24,16,128]{2,1,0:T(8,128)(2,1)S(1)}, bf16[24,16,128]{2,1,0:T(8,128)(2,1)S(1)}, u32[]{:S(2)}, u32[]{:S(2)}) %collective-permute-start.18) | collective-permute-done | bytes 98336 | tf_op jit(solution)/shard_map/ppermute | solution.py:396
  141.0 1.0 collective-permute-start.17
  141.9 4.7 %collective-permute-done.17.b2 = bf16[24,16,128]{2,1,0:T(8,128)(2,1)S(1)} collective-permute-done((bf16[24,16,128]{2,1,0:T(8,128)(2,1)S(1)}, bf16[24,16,128]{2,1,0:T(8,128)(2,1)S(1)}, u32[]{:S(2)}, u32[]{:S(2)}) %collective-permute-start.17) | collective-permute-done | bytes 98336 | tf_op jit(solution)/shard_map/ppermute | solution.py:396
  146.6 4.4 %collective-permute-done.16.b1 = bf16[24,16,128]{2,1,0:T(8,128)(2,1)S(1)} collective-permute-done((bf16[24,16,128]{2,1,0:T(8,128)(2,1)S(1)}, bf16[24,16,128]{2,1,0:T(8,128)(2,1)S(1)}, u32[]{:S(2)}, u32[]{:S(2)}) %collective-permute-start.16) | collective-permute-done | bytes 98336 | tf_op jit(solution)/shard_map/ppermute | solution.py:396
  151.0 7.6 %collective-permute-start.19 = (bf16[24,16,128]{2,1,0:T(8,128)(2,1)S(1)}, bf16[24,16,128]{2,1,0:T(8,128)(2,1)S(1)}, u32[]{:S(2)}, u32[]{:S(2)}) collective-permute-start(bf16[24,16,128]{2,1,0:T(8,128)(2,1)S(1)} %slice.4.b0), channel_id=1, source_target_pairs={{0,1},{1,0},{2,3},{3,2},{4,5},{5,4},{6,7},{7,6},{8,9},{9,8},{10,11... | collective-permute-start | bytes 294920 | tf_op jit(solution)/shard_map/ppermute | solution.py:400
  158.6 0.1 collective-permute-start.22
  158.7 0.4 collective-permute-start.21
  159.1 0.3 collective-permute-start.20
  159.4 6.9 %shard_map.87.fed = bf16[8,384,768]{2,1,0:T(8,128)(2,1)} custom-call(bf16[512,384]{1,0:T(8,128)(2,1)S(1)} %copy-done.1, bf16[384,6144]{1,0:T(8,128)(2,1)} %bitcast.10, bf16[512,768]{1,0:T(8,128)(2,1)} %rest_0_.1, bf16[512,768]{1,0:T(8,128)(2,1)} %collective-permute-done.4.rest_1_, bf16[512,768]{1,0:T(8,128)(2,1)} %collective-permute-done.5.rest_2_, ...), custom_call_target="tpu_custom_call" | custom-call | flops 6000000000 | bytes 1048576 | tf_op jit(solution)/shard_map/pallas_call | solution.py:296
  166.4 3.5 %shard_map.89 = (bf16[1,384,6144]{2,1,0:T(8,128)(2,1)}, bf16[64,6144]{1,0:T(8,128)(2,1)S(1)}, bf16[4,384,768]{2,1,0:T(8,128)(2,1)S(1)}) custom-call(bf16[8,384,768]{2,1,0:T(8,128)(2,1)} %shard_map.87.fed, bf16[384,64]{1,0:T(8,128)(2,1)S(1)} %get-tuple-element.38.basis, bf16[24,16,128]{2,1,0:T(8,128)(2,1)S(1)} %slice.4.b0, ...), custom_call_target="tpu_custom_call" | custom-call | flops 1000000000 | bytes 1048576 | tf_op jit(solution)/shard_map/pallas_call | solution.py:347
  169.9 2.8 %shard_map.90 = (bf16[1,384,6144]{2,1,0:T(8,128)(2,1)}, f32[192,384]{1,0:T(8,128)}, bf16[64,6144]{1,0:T(8,128)(2,1)}) custom-call(bf16[4,384,768]{2,1,0:T(8,128)(2,1)S(1)} %get-tuple-element.39.fed, bf16[384,64]{1,0:T(8,128)(2,1)S(1)} %get-tuple-element.38.basis, ...), custom_call_target="tpu_custom_call", output_to_operand_aliasing={{0}: (7, {})} | custom-call | flops 1000000000 | bytes 1048576 | tf_op jit(solution)/shard_map/pallas_call | solution.py:383
  (29 shorter events, 0.4 us)
Async XLA Ops:
  2.6 4.3 %collective-permute-start = (f32[64,512]{1,0:T(8,128)S(1)}, f32[64,512]{1,0:T(8,128)S(1)}, u32[]{:S(2)}, u32[]{:S(2)}) collective-permute-start(f32[64,512]{1,0:T(8,128)S(1)} %shard_map.76.a), channel_id=1, source_target_pairs={{0,1},{1,0},{2,3},{3,2},{4,5},{5,4},{6,7},{7,6},{8,9},{9,8},{10,11... | collective-permute-start | bytes 393224 | tf_op jit(solution)/shard_map/ppermute | solution.py:400
  6.9 5.9 %collective-permute-start.3 = (bf16[64,512]{1,0:T(8,128)(2,1)S(1)}, bf16[64,512]{1,0:T(8,128)(2,1)S(1)}, u32[]{:S(2)}, u32[]{:S(2)}) collective-permute-start(bf16[64,512]{1,0:T(8,128)(2,1)S(1)} %get-tuple-element.24), channel_id=1, source_target_pairs={{0,6},{2,0},{4,2},{6,4},{1,7},{3,1},{5,3},{7,5},{8,14},{10,8},{12,... | collective-permute-start | bytes 196616 | tf_op jit(solution)/shard_map/ppermute | solution.py:396
  8.0 4.8 %collective-permute-start.2 = (bf16[64,512]{1,0:T(8,128)(2,1)S(1)}, bf16[64,512]{1,0:T(8,128)(2,1)S(1)}, u32[]{:S(2)}, u32[]{:S(2)}) collective-permute-start(bf16[64,512]{1,0:T(8,128)(2,1)S(1)} %get-tuple-element.24), channel_id=1, source_target_pairs={{0,4},{2,6},{4,0},{6,2},{1,5},{3,7},{5,1},{7,3},{8,12},{10,14},{12... | collective-permute-start | bytes 196616 | tf_op jit(solution)/shard_map/ppermute | solution.py:396
  8.4 5.8 %collective-permute-start.1 = (bf16[64,512]{1,0:T(8,128)(2,1)S(1)}, bf16[64,512]{1,0:T(8,128)(2,1)S(1)}, u32[]{:S(2)}, u32[]{:S(2)}) collective-permute-start(bf16[64,512]{1,0:T(8,128)(2,1)S(1)} %get-tuple-element.24), channel_id=1, source_target_pairs={{0,2},{2,4},{4,6},{6,0},{1,3},{3,5},{5,7},{7,1},{8,10},{10,12},{12... | collective-permute-start | bytes 196616 | tf_op jit(solution)/shard_map/ppermute | solution.py:396
  9.0 5.1 %copy-start.1 = (bf16[512,384]{1,0:T(8,128)(2,1)S(1)}, bf16[512,384]{1,0:T(8,128)(2,1)}, u32[]{:S(2)}) copy-start(bf16[512,384]{1,0:T(8,128)(2,1)} %acts.5) | copy-start | bytes 1179652
  47.9 10.2 %copy-start = (bf16[512,768]{1,0:T(8,128)(2,1)S(1)}, bf16[512,768]{1,0:T(8,128)(2,1)}, u32[]{:S(2)}) copy-start(bf16[512,768]{1,0:T(8,128)(2,1)} %rest_0_.1) | copy-start | bytes 2359300
  51.6 12.2 %collective-permute-start.11 = (f32[4,64,768]{2,1,0:T(8,128)S(1)}, f32[4,64,768]{2,1,0:T(8,128)S(1)}, u32[]{:S(2)}, u32[]{:S(2)}) collective-permute-start(f32[4,64,768]{2,1,0:T(8,128)S(1)} %get-tuple-element.33), channel_id=1, source_target_pairs={{0,1},{1,0},{2,3},{3,2},{4,5},{5,4},{6,7},{7,6},{8,9},{9,8},{10,11... | collective-permute-start | bytes 2359304 | tf_op jit(solution)/shard_map/ppermute | solution.py:400
  55.3 2.1 %collective-permute-start.7 = (f32[64,640]{1,0:T(8,128)S(1)}, f32[64,640]{1,0:T(8,128)S(1)}, u32[]{:S(2)}, u32[]{:S(2)}) collective-permute-start(f32[64,640]{1,0:T(8,128)S(1)} %get-tuple-element.27.a), channel_id=1, source_target_pairs={{0,1},{1,0},{2,3},{3,2},{4,5},{5,4},{6,7},{7,6},{8,9},{9,8},{10,11... | collective-permute-start | bytes 491528 | tf_op jit(solution)/shard_map/ppermute | solution.py:400
  57.4 5.5 %collective-permute-start.10 = (f32[64,640]{1,0:T(8,128)S(1)}, f32[64,640]{1,0:T(8,128)S(1)}, u32[]{:S(2)}, u32[]{:S(2)}) collective-permute-start(f32[64,640]{1,0:T(8,128)S(1)} %shard_map.82.own), channel_id=1, source_target_pairs={{0,6},{2,0},{4,2},{6,4},{1,7},{3,1},{5,3},{7,5},{8,14},{10,8},{12,... | collective-permute-start | bytes 491528 | tf_op jit(solution)/shard_map/ppermute | solution.py:396
  58.2 56.0 %collective-permute-start.6 = (bf16[512,768]{1,0:T(8,128)(2,1)S(1)}, bf16[512,768]{1,0:T(8,128)(2,1)}, u32[]{:S(2)}, u32[]{:S(2)}) collective-permute-start(bf16[512,768]{1,0:T(8,128)(2,1)S(1)} %copy-done), channel_id=1, source_target_pairs={{0,2},{2,4},{4,6},{6,0},{1,3},{3,5},{5,7},{7,1},{8,10},{10,12},{12... | collective-permute-start | bytes 2359304 | tf_op jit(solution)/shard_map/ppermute | solution.py:396
  59.0 55.2 %collective-permute-start.5 = (bf16[512,768]{1,0:T(8,128)(2,1)S(1)}, bf16[512,768]{1,0:T(8,128)(2,1)}, u32[]{:S(2)}, u32[]{:S(2)}) collective-permute-start(bf16[512,768]{1,0:T(8,128)(2,1)S(1)} %copy-done), channel_id=1, source_target_pairs={{0,4},{2,6},{4,0},{6,2},{1,5},{3,7},{5,1},{7,3},{8,12},{10,14},{12... | collective-permute-start | bytes 2359304 | tf_op jit(solution)/shard_map/ppermute | solution.py:396
  59.7 54.5 %collective-permute-start.4 = (bf16[512,768]{1,0:T(8,128)(2,1)S(1)}, bf16[512,768]{1,0:T(8,128)(2,1)}, u32[]{:S(2)}, u32[]{:S(2)}) collective-permute-start(bf16[512,768]{1,0:T(8,128)(2,1)S(1)} %copy-done), channel_id=1, source_target_pairs={{0,6},{2,0},{4,2},{6,4},{1,7},{3,1},{5,3},{7,5},{8,14},{10,8},{12,... | collective-permute-start | bytes 2359304 | tf_op jit(solution)/shard_map/ppermute | solution.py:396
  62.9 34.2 %collective-permute-start.9 = (f32[64,640]{1,0:T(8,128)S(1)}, f32[64,640]{1,0:T(8,128)S(1)}, u32[]{:S(2)}, u32[]{:S(2)}) collective-permute-start(f32[64,640]{1,0:T(8,128)S(1)} %shard_map.82.own), channel_id=1, source_target_pairs={{0,4},{2,6},{4,0},{6,2},{1,5},{3,7},{5,1},{7,3},{8,12},{10,14},{12... | collective-permute-start | bytes 491528 | tf_op jit(solution)/shard_map/ppermute | solution.py:396
  63.8 37.9 %collective-permute-start.8 = (f32[64,640]{1,0:T(8,128)S(1)}, f32[64,640]{1,0:T(8,128)S(1)}, u32[]{:S(2)}, u32[]{:S(2)}) collective-permute-start(f32[64,640]{1,0:T(8,128)S(1)} %shard_map.82.own), channel_id=1, source_target_pairs={{0,2},{2,4},{4,6},{6,0},{1,3},{3,5},{5,7},{7,1},{8,10},{10,12},{12... | collective-permute-start | bytes 491528 | tf_op jit(solution)/shard_map/ppermute | solution.py:396
  66.3 42.8 %all-to-all-start.2 = ((f32[4,64,768]{2,1,0:T(8,128)}), f32[4,64,768]{2,1,0:T(8,128)S(1)}, u32[]{:S(2)}, u32[]{:S(2)}) async-start(f32[4,64,768]{2,1,0:T(8,128)} %shard_map.85), calls=%async_computation.2 | async-start | bytes 1572864 | tf_op jit(solution)/shard_map/all_to_all | solution.py:446
  110.3 13.3 %all-to-all-start.3 = ((bf16[32,16,128]{2,1,0:T(8,128)(2,1)}), bf16[32,16,128]{2,1,0:T(8,128)(2,1)S(1)}, u32[]{:S(2)}, u32[]{:S(2)}) async-start(bf16[32,16,128]{2,1,0:T(8,128)(2,1)} %shard_map.86), calls=%async_computation.3 | async-start | bytes 262144 | tf_op jit(solution)/shard_map/all_to_all | solution.py:404
  114.2 44.3 %collective-permute-start.12 = (bf16[512,768]{1,0:T(8,128)(2,1)S(1)}, bf16[512,768]{1,0:T(8,128)(2,1)S(1)}, u32[]{:S(2)}, u32[]{:S(2)}) collective-permute-start(bf16[512,768]{1,0:T(8,128)(2,1)S(1)} %copy-done), channel_id=1, source_target_pairs={{0,1},{1,0},{2,3},{3,2},{4,5},{5,4},{6,7},{7,6},{8,9},{9,8},{10,11... | collective-permute-start | bytes 2359304 | tf_op jit(solution)/shard_map/ppermute | solution.py:400
  116.8 41.8 %collective-permute-start.13 = (bf16[512,768]{1,0:T(8,128)(2,1)}, bf16[512,768]{1,0:T(8,128)(2,1)}, u32[]{:S(2)}, u32[]{:S(2)}) collective-permute-start(bf16[512,768]{1,0:T(8,128)(2,1)} %collective-permute-done.4.rest_1_), channel_id=1, source_target_pairs={{0,1},{1,0},{2,3},{3,2},{4,5},{5,4},{6,7},{7,6},{8,9},{9,8},{10,11... | collective-permute-start | bytes 2359304 | tf_op jit(solution)/shard_map/ppermute | solution.py:400
  116.9 42.1 %collective-permute-start.14 = (bf16[512,768]{1,0:T(8,128)(2,1)}, bf16[512,768]{1,0:T(8,128)(2,1)}, u32[]{:S(2)}, u32[]{:S(2)}) collective-permute-start(bf16[512,768]{1,0:T(8,128)(2,1)} %collective-permute-done.5.rest_2_), channel_id=1, source_target_pairs={{0,1},{1,0},{2,3},{3,2},{4,5},{5,4},{6,7},{7,6},{8,9},{9,8},{10,11... | collective-permute-start | bytes 2359304 | tf_op jit(solution)/shard_map/ppermute | solution.py:400
  117.4 42.0 %collective-permute-start.15 = (bf16[512,768]{1,0:T(8,128)(2,1)}, bf16[512,768]{1,0:T(8,128)(2,1)}, u32[]{:S(2)}, u32[]{:S(2)}) collective-permute-start(bf16[512,768]{1,0:T(8,128)(2,1)} %collective-permute-done.6.rest_3_), channel_id=1, source_target_pairs={{0,1},{1,0},{2,3},{3,2},{4,5},{5,4},{6,7},{7,6},{8,9},{9,8},{10,11... | collective-permute-start | bytes 2359304 | tf_op jit(solution)/shard_map/ppermute | solution.py:400
  136.2 4.8 %collective-permute-start.18 = (bf16[24,16,128]{2,1,0:T(8,128)(2,1)S(1)}, bf16[24,16,128]{2,1,0:T(8,128)(2,1)S(1)}, u32[]{:S(2)}, u32[]{:S(2)}) collective-permute-start(bf16[24,16,128]{2,1,0:T(8,128)(2,1)S(1)} %slice.4.b0), channel_id=1, source_target_pairs={{0,2},{2,4},{4,6},{6,0},{1,3},{3,5},{5,7},{7,1},{8,10},{10,12},{12... | collective-permute-start | bytes 294920 | tf_op jit(solution)/shard_map/ppermute | solution.py:396
  141.0 5.6 %collective-permute-start.17 = (bf16[24,16,128]{2,1,0:T(8,128)(2,1)S(1)}, bf16[24,16,128]{2,1,0:T(8,128)(2,1)S(1)}, u32[]{:S(2)}, u32[]{:S(2)}) collective-permute-start(bf16[24,16,128]{2,1,0:T(8,128)(2,1)S(1)} %slice.4.b0), channel_id=1, source_target_pairs={{0,4},{2,6},{4,0},{6,2},{1,5},{3,7},{5,1},{7,3},{8,12},{10,14},{12... | collective-permute-start | bytes 294920 | tf_op jit(solution)/shard_map/ppermute | solution.py:396
  146.6 4.4 %collective-permute-start.16 = (bf16[24,16,128]{2,1,0:T(8,128)(2,1)S(1)}, bf16[24,16,128]{2,1,0:T(8,128)(2,1)S(1)}, u32[]{:S(2)}, u32[]{:S(2)}) collective-permute-start(bf16[24,16,128]{2,1,0:T(8,128)(2,1)S(1)} %slice.4.b0), channel_id=1, source_target_pairs={{0,6},{2,0},{4,2},{6,4},{1,7},{3,1},{5,3},{7,5},{8,14},{10,8},{12,... | collective-permute-start | bytes 294920 | tf_op jit(solution)/shard_map/ppermute | solution.py:396
  151.0 18.9 %collective-permute-start.19 = (bf16[24,16,128]{2,1,0:T(8,128)(2,1)S(1)}, bf16[24,16,128]{2,1,0:T(8,128)(2,1)S(1)}, u32[]{:S(2)}, u32[]{:S(2)}) collective-permute-start(bf16[24,16,128]{2,1,0:T(8,128)(2,1)S(1)} %slice.4.b0), channel_id=1, source_target_pairs={{0,1},{1,0},{2,3},{3,2},{4,5},{5,4},{6,7},{7,6},{8,9},{9,8},{10,11... | collective-permute-start | bytes 294920 | tf_op jit(solution)/shard_map/ppermute | solution.py:400
  158.6 0.9 copy-start.3
  158.6 11.3 %collective-permute-start.22 = (bf16[24,16,128]{2,1,0:T(8,128)(2,1)S(1)}, bf16[24,16,128]{2,1,0:T(8,128)(2,1)S(1)}, u32[]{:S(2)}, u32[]{:S(2)}) collective-permute-start(bf16[24,16,128]{2,1,0:T(8,128)(2,1)S(1)} %collective-permute-done.18.b3), channel_id=1, source_target_pairs={{0,1},{1,0},{2,3},{3,2},{4,5},{5,4},{6,7},{7,6},{8,9},{9,8},{10,11... | collective-permute-start | bytes 294920 | tf_op jit(solution)/shard_map/ppermute | solution.py:400
  158.7 11.2 %collective-permute-start.21 = (bf16[24,16,128]{2,1,0:T(8,128)(2,1)S(1)}, bf16[24,16,128]{2,1,0:T(8,128)(2,1)S(1)}, u32[]{:S(2)}, u32[]{:S(2)}) collective-permute-start(bf16[24,16,128]{2,1,0:T(8,128)(2,1)S(1)} %collective-permute-done.17.b2), channel_id=1, source_target_pairs={{0,1},{1,0},{2,3},{3,2},{4,5},{5,4},{6,7},{7,6},{8,9},{9,8},{10,11... | collective-permute-start | bytes 294920 | tf_op jit(solution)/shard_map/ppermute | solution.py:400
  159.1 10.8 %collective-permute-start.20 = (bf16[24,16,128]{2,1,0:T(8,128)(2,1)S(1)}, bf16[24,16,128]{2,1,0:T(8,128)(2,1)S(1)}, u32[]{:S(2)}, u32[]{:S(2)}) collective-permute-start(bf16[24,16,128]{2,1,0:T(8,128)(2,1)S(1)} %collective-permute-done.16.b1), channel_id=1, source_target_pairs={{0,1},{1,0},{2,3},{3,2},{4,5},{5,4},{6,7},{7,6},{8,9},{9,8},{10,11... | collective-permute-start | bytes 294920 | tf_op jit(solution)/shard_map/ppermute | solution.py:400
  166.4 3.6 %copy-start.2 = (f32[384,192]{0,1:T(8,128)S(1)}, f32[384,192]{0,1:T(8,128)}, u32[]{:S(2)}) copy-start(f32[384,192]{0,1:T(8,128)} %param.9) | copy-start | bytes 884740

commit v5 on v4

--- a/solution.py
+++ b/solution.py
@@ -267,25 +267,42 @@
     )
 
 
+def copies_of_grads(pieces, place, sems):
+    own, up, half_a, half_b, down = pieces
+    h = TOK // 2
+    return [
+        [pltpu.make_async_copy(own, place.at[0], sems.at[0])],
+        [pltpu.make_async_copy(up, place.at[1], sems.at[1])],
+        [
+            pltpu.make_async_copy(half_a, place.at[2, pl.ds(0, h)], sems.at[2]),
+            pltpu.make_async_copy(half_b, place.at[2, pl.ds(h, h)], sems.at[3]),
+        ],
+        [pltpu.make_async_copy(down, place.at[3], sems.at[4])],
+    ]
+
+
 def fed_body(acts, error, *rest):
-    grads, out, held, held_e, held_o, sems = rest[:8], rest[8], *rest[9:]
+    grads, out, held, held_e, held_o, sems, near_sems, far_sems = rest[:10], *rest[10:]
     errors = [
         pltpu.make_async_copy(
             error.at[:, columns(block_at(k % 4, k >= 4))], held_e.at[k], sems.at[k]
         )
         for k in range(8)
     ]
-    loads = [pltpu.make_async_copy(grads[k], held.at[k], sems.at[8 + k]) for k in range(8)]
+    loads = copies_of_grads(grads[:5], held.at[pl.ds(0, 4)], near_sems)
+    loads += copies_of_grads(grads[5:], held.at[pl.ds(4, 4)], far_sems)
     for k in range(8):
-        loads[k].start()
+        for c in loads[k]:
+            c.start()
         errors[k].start()
     turned = acts[...].T
     stores = []
     for k in range(8):
-        loads[k].wait()
+        for c in loads[k]:
+            c.wait()
         errors[k].wait()
         held_o[k] = (dot(turned, held[k]) + held_e[k].astype(F32)).astype(BF16)
-        store = pltpu.make_async_copy(held_o.at[k], out.at[k], sems.at[16 + k])
+        store = pltpu.make_async_copy(held_o.at[k], out.at[k], sems.at[8 + k])
         store.start()
         stores.append(store)
     for store in stores:
@@ -298,15 +315,22 @@
         pltpu.HBM((8, ROWS, COLS), BF16),
         6 * 10**9,
         24,
-        in_specs=[VMEM, HBM] + [HBM] * 8,
+        in_specs=[VMEM, HBM] + [HBM] * 10,
         out_specs=HBM,
         scratch_shapes=[
             pltpu.VMEM((8, TOK, COLS), BF16),
             pltpu.VMEM((8, ROWS, COLS), BF16),
             pltpu.VMEM((8, ROWS, COLS), BF16),
-            pltpu.SemaphoreType.DMA((24,)),
+            pltpu.SemaphoreType.DMA((16,)),
+            pltpu.SemaphoreType.DMA((5,)),
+            pltpu.SemaphoreType.DMA((5,)),
         ],
     )(acts, error, *map(in_hbm, grads))
+
+
+def joined(tiles):
+    rows = [jnp.concatenate([tiles[4 * j + r] for j in range(6)], axis=1) for r in range(4)]
+    return jnp.concatenate(rows, axis=0)
 
 
 def block_outputs(fed, first, basis, blocks, error_new, sketch_t, held, sems):
@@ -315,8 +339,7 @@
     for i, tiles in enumerate(blocks):
         k = first + i
         where = block_at(k % 4, k >= 4)
-        rows = [jnp.concatenate([tiles[4 * j + r] for j in range(6)], axis=1) for r in range(4)]
-        block = jnp.concatenate(rows, axis=0)
+        block = joined(tiles)
         held[i] = (fed[i].astype(F32) - dot(scaled, block)).astype(BF16)
         store = pltpu.make_async_copy(held.at[i], error_new.at[0, :, columns(where)], sems.at[i])
         store.start()
@@ -325,39 +348,62 @@
     return stores
 
 
-def near_outputs_body(
-    fed, basis, b0, b1, b2, b3, error_new, sketch_t, fed_far, held_f, held, sems, load_sems
+def own_outputs_body(
+    fed, basis, b0, error_new, sketch_t, fed_near, fed_far, held_f, held, sems, load_sems
 ):
+    places = [held_f.at[0]] + [fed_near.at[k] for k in range(3)] + [fed_far.at[k] for k in range(4)]
     loads = [
-        pltpu.make_async_copy(
-            fed.at[k], held_f.at[k] if k < 4 else fed_far.at[k - 4], load_sems.at[k]
-        )
-        for k in range(8)
+        pltpu.make_async_copy(fed.at[k], places[k], load_sems.at[k]) for k in range(8)
     ]
     for c in loads:
         c.start()
-    for c in loads[:4]:
+    loads[0].wait()
+    stores = block_outputs(held_f, 0, basis, (b0,), error_new, sketch_t, held, sems)
+    for c in loads[1:] + stores:
         c.wait()
-    stores = block_outputs(held_f, 0, basis, (b0, b1, b2, b3), error_new, sketch_t, held, sems)
-    for c in loads[4:] + stores:
-        c.wait()
-
-
-def near_outputs(fed, basis, blocks):
-    return call(
-        near_outputs_body,
-        (sds((1, ROWS, D), BF16), on_chip((RANK, D), BF16), on_chip((4, ROWS, COLS), BF16)),
+
+
+def own_outputs(fed, basis, b0):
+    return call(
+        own_outputs_body,
+        (
+            sds((1, ROWS, D), BF16),
+            on_chip((RANK, D), BF16),
+            on_chip((3, ROWS, COLS), BF16),
+            on_chip((4, ROWS, COLS), BF16),
+        ),
         10**9,
-        12,
-        in_specs=[HBM] + [VMEM] * 5,
-        out_specs=(HBM, VMEM, VMEM),
+        8,
+        in_specs=[HBM, VMEM, VMEM],
+        out_specs=(HBM, VMEM, VMEM, VMEM),
         scratch_shapes=[
-            pltpu.VMEM((4, ROWS, COLS), BF16),
-            pltpu.VMEM((4, ROWS, COLS), BF16),
-            pltpu.SemaphoreType.DMA((4,)),
+            pltpu.VMEM((1, ROWS, COLS), BF16),
+            pltpu.VMEM((1, ROWS, COLS), BF16),
+            pltpu.SemaphoreType.DMA((1,)),
             pltpu.SemaphoreType.DMA((8,)),
         ],
-    )(fed, basis, *blocks)
+    )(fed, basis, b0)
+
+
+def near_outputs_body(fed, basis, b1, b2, b3, _, own_t, error_new, sketch_t, held, sems):
+    place = columns(block_at(0, False))
+    sketch_t[:, place] = own_t[:, place]
+    stores = block_outputs(fed, 1, basis, (b1, b2, b3), error_new, sketch_t, held, sems)
+    for c in stores:
+        c.wait()
+
+
+def near_outputs(fed_near, basis, blocks, error_new, own_t):
+    return call(
+        near_outputs_body,
+        (sds((1, ROWS, D), BF16), on_chip((RANK, D), BF16)),
+        10**9,
+        8,
+        in_specs=[VMEM] * 5 + [HBM, VMEM],
+        out_specs=(HBM, VMEM),
+        scratch_shapes=[pltpu.VMEM((3, ROWS, COLS), BF16), pltpu.SemaphoreType.DMA((3,))],
+        input_output_aliases={5: 0},
+    )(fed_near, basis, *blocks, error_new, own_t)
 
 
 def far_outputs_body(
@@ -425,10 +471,9 @@
     from_error = error_sketch(own_error, sketch_t)
     tiles = left_term(pair, others, activations, from_error)
 
-    held = after(out_grads, *others)
-    gathered = []
-    for k in (1, 2, 3):
-        gathered.append(along_y(held, -k % 4))
+    held = after(own_grads, *others)
+    g1 = along_y(held, -1)
+    g3 = along_y(held, 1)
 
     arrived = to_workers(tiles)
     copies = sum_and_copy(arrived, F32)
@@ -447,20 +492,26 @@
     inverse, basis, acts_left = factor(small, small_parts, left)
     pieces = right_term(inverse, acts_left, own_grads, terms)
 
-    near_g = (out_grads, *gathered)
+    half = TOK // 2
+    g2a = along_y(after(g1, pieces)[:half], -1)
+    g2b = along_y(after(g3, pieces)[half:], 1)
+    near_g = (own_grads, g1, g2a, g2b, g3)
     far_g = []
-    for k in range(4):
+    for k in range(5):
         far_g.append(other_core(after(near_g[k], pieces)))
     arrived = to_workers(pieces)
     copies = sum_and_copy(arrived, BF16)
     fed = fed_of(activations, own_error, (*near_g, *far_g))
     block = to_workers(copies)[:24]
-    n3, n2, n1 = along_y(block, 1), along_y(block, 2), along_y(block, -1)
-    near_n = (block, n1, n2, n3)
+    spread = []
+    for k in (1, 2, 3):
+        spread.append(along_y(block, -k % 4))
+    near_n = (block, *spread)
     far_n = []
     for k in range(4):
         far_n.append(other_core(near_n[k]))
-    error_new, near_t, fed_far = near_outputs(in_hbm(fed), basis, near_n)
+    error_new, own_t, fed_near, fed_far = own_outputs(in_hbm(fed), basis, block)
+    error_new, near_t = near_outputs(fed_near, basis, spread, error_new, own_t)
     error_new, momentum_t, sketch_t = far_outputs(
         fed_far, basis, far_n, momentum.T, error_new, near_t
     )

time: 173 us -> 154 us (0.89)
  waiting for transfers between devices: 58.9 us -> 38.2 us
  blocking collectives: 45.6 us -> 32.8 us
  starting transfers between devices: 36.1 us -> 45.9 us
  local copies, waits for them, and re-layouts: 0.07 us -> 2.43 us
    ppermute x12 -> x13, waiting for transfers between devices: 48 us -> 4.42 us  [along_y(): return lax.ppermute(x, YY, [(i, (i + k) % 4) for i in range(4)])]
    all_to_all x1, waiting for transfers between devices: 1.66 us -> 18.5 us  [step(): terms = lax.all_to_all(q, YY, split_axis=0, concat_axis=0, tiled=True)]
    all_to_all x3 -> x2, blocking collectives: 45.6 us -> 32.8 us  [to_workers(): return lax.all_to_all(x, DP, split_axis=0, concat_axis=0, tiled=True)]
    all_to_all x1 -> x2, starting transfers between devices: 3.86 us -> 8.57 us  [to_workers(): return lax.all_to_all(x, DP, split_axis=0, concat_axis=0, tiled=True)]
    all_to_all x1 -> x2, waiting for transfers between devices: 6.14 us -> 10.8 us  [to_workers(): return lax.all_to_all(x, DP, split_axis=0, concat_axis=0, tiled=True)]
    ppermute x12 -> x13, starting transfers between devices: 9.88 us -> 13.6 us  [along_y(): return lax.ppermute(x, YY, [(i, (i + k) % 4) for i in range(4)])]
    pallas_call x0 -> x1, Pallas kernels: none -> 2.51 us  [own_outputs(): call(own_outputs_body, (sds((1, ROWS, D), BF16), on_chip((RANK, D), BF16)...]
    slice x0 -> x2, local copies, waits for them, and re-layouts: none -> 2.05 us  [the longest x1 1.02 us: step(): g2b = along_y(after(g3, pieces)[half:], 1)]
  transfers between devices with their start and end apart: 25 -> 28, of which waited for: 11 -> 8; matrix products, arithmetic and copies ran while one was open for 0% -> 1% of each run, Pallas kernels for 13% -> 15%
where the time goes in v5:
time: 154 us; the launch traced here: 153 us
  starting transfers between devices  45.9 us (30%)
  waiting for transfers between devices  38.2 us (25%)
  blocking collectives  32.8 us (21%)
  Pallas kernels  32.7 us (21%)
  local copies, waits for them, and re-layouts  2.43 us (2%)
    all_to_all x2, blocking collectives, to_workers(): return lax.all_to_all(x, DP, split_axis=0, concat_axis=0, tiled=True)  32.8 us
    ppermute x12, starting transfers between devices, other_core(): return lax.ppermute(x, CC, [(0, 1), (1, 0)])  20.2 us
    all_to_all x1, waiting for transfers between devices, step(): terms = lax.all_to_all(q, YY, split_axis=0, concat_axis=0, tiled=True)  18.5 us
    ppermute x13, starting transfers between devices, along_y(): return lax.ppermute(x, YY, [(i, (i + k) % 4) for i in range(4)])  13.6 us
    all_to_all x2, waiting for transfers between devices, to_workers(): return lax.all_to_all(x, DP, split_axis=0, concat_axis=0, tiled=True)  10.8 us
    all_to_all x2, starting transfers between devices, to_workers(): return lax.all_to_all(x, DP, split_axis=0, concat_axis=0, tiled=True)  8.57 us
    pallas_call x1, Pallas kernels, fed_of(): call(fed_body, pltpu.HBM((8, ROWS, COLS), BF16), 6 * 10 ** 9, 24, in_spec...  7.17 us
    pallas_call x1, Pallas kernels, factor(): call(factor_body, (on_chip((RANK, RANK), F32), on_chip((ROWS, RANK), BF16...  5.75 us
  transfers between devices with their start and end apart: 28, of which 8 were waited for; matrix products, arithmetic and copies ran while one was open for 1% of the time, Pallas kernels for 15%

profile of v5, /device:TPU:1, one launch (start us, length us, event | category | flops | bytes accessed | tf_op | source)
XLA Modules:
  0.0 153.2 jit_solution(3772788759361054537)
XLA Ops:
  0.6 2.0 %shard_map.76.a = f32[64,512]{1,0:T(8,128)S(1)} custom-call(bf16[512,768]{1,0:T(8,128)(2,1)} %rest_0_.1, bf16[64,6144]{1,0:T(8,128)(2,1)} %bitcast.6), custom_call_target="tpu_custom_call" | custom-call | flops 100000000 | bytes 1048576 | tf_op jit(solution)/shard_map/pallas_call | solution.py:89
  2.6 3.3 %collective-permute-start = (f32[64,512]{1,0:T(8,128)S(1)}, f32[64,512]{1,0:T(8,128)S(1)}, u32[]{:S(2)}, u32[]{:S(2)}) collective-permute-start(f32[64,512]{1,0:T(8,128)S(1)} %shard_map.76.a), channel_id=1, source_target_pairs={{0,1},{1,0},{2,3},{3,2},{4,5},{5,4},{6,7},{7,6},{8,9},{9,8},{10,11... | collective-permute-start | bytes 393224 | tf_op jit(solution)/shard_map/ppermute | solution.py:446
  5.9 1.0 collective-permute-done.b
  7.0 2.2 %collective-permute-start.2 = (bf16[64,512]{1,0:T(8,128)(2,1)S(1)}, bf16[64,512]{1,0:T(8,128)(2,1)S(1)}, u32[]{:S(2)}, u32[]{:S(2)}) collective-permute-start(bf16[64,512]{1,0:T(8,128)(2,1)S(1)} %get-tuple-element.28), channel_id=1, source_target_pairs={{0,4},{2,6},{4,0},{6,2},{1,5},{3,7},{5,1},{7,3},{8,12},{10,14},{12... | collective-permute-start | bytes 196616 | tf_op jit(solution)/shard_map/ppermute | solution.py:442
  9.2 1.1 collective-permute-start.3
  10.3 3.8 %shard_map.78.from_error = f32[64,384]{1,0:T(8,128)S(1)} custom-call(bf16[384,6144]{1,0:T(8,128)(2,1)} %bitcast.8, bf16[64,6144]{1,0:T(8,128)(2,1)} %bitcast.7), custom_call_target="tpu_custom_call" | custom-call | flops 3000000000 | bytes 1048576 | tf_op jit(solution)/shard_map/pallas_call | solution.py:131
  14.1 0.2 shard_map.79
  14.3 20.2 %all_to_all.25.arrived = f32[32,8,128]{2,1,0:T(8,128)S(1)} all-to-all(f32[32,8,128]{2,1,0:T(8,128)S(1)} %shard_map.79), channel_id=1, replica_groups=mesh['dp_0'=8,'dp_1'=4,'mp_0'=4,'mp_1'=2] {'dp_0','dp_1'}, dimensions={0} | all-to-all | bytes 262144 | tf_op jit(solution)/shard_map/all_to_all | solution.py:450
  34.5 12.6 %all_to_all.26.tiles = f32[32,8,128]{2,1,0:T(8,128)S(1)} all-to-all(f32[32,8,128]{2,1,0:T(8,128)S(1)} %shard_map.80), channel_id=1, replica_groups=mesh['dp_0'=8,'dp_1'=4,'mp_0'=4,'mp_1'=2] {'dp_0','dp_1'}, dimensions={0} | all-to-all | bytes 262144 | tf_op jit(solution)/shard_map/all_to_all | solution.py:450
  47.2 0.4 shard_map.81
  47.6 3.6 %shard_map.84 = (f32[4,64,768]{2,1,0:T(8,128)S(1)}, f32[4,64,768]{2,1,0:T(8,128)S(1)}) custom-call(bf16[128,384]{1,0:T(8,128)(2,1)S(1)} %get-tuple-element.35.left_terms, bf16[384,6144]{1,0:T(8,128)(2,1)} %bitcast.9), custom_call_target="tpu_custom_call" | custom-call | flops 10000000000 | bytes 1048576 | tf_op jit(solution)/shard_map/pallas_call | solution.py:209
  51.2 3.9 %collective-permute-start.9 = (f32[4,64,768]{2,1,0:T(8,128)S(1)}, f32[4,64,768]{2,1,0:T(8,128)S(1)}, u32[]{:S(2)}, u32[]{:S(2)}) collective-permute-start(f32[4,64,768]{2,1,0:T(8,128)S(1)} %get-tuple-element.37), channel_id=1, source_target_pairs={{0,1},{1,0},{2,3},{3,2},{4,5},{5,4},{6,7},{7,6},{8,9},{9,8},{10,11... | collective-permute-start | bytes 2359304 | tf_op jit(solution)/shard_map/ppermute | solution.py:446
  55.2 2.0 %collective-permute-done.5.b = f32[64,640]{1,0:T(8,128)S(1)} collective-permute-done((f32[64,640]{1,0:T(8,128)S(1)}, f32[64,640]{1,0:T(8,128)S(1)}, u32[]{:S(2)}, u32[]{:S(2)}) %collective-permute-start.5) | collective-permute-done | bytes 163872 | tf_op jit(solution)/shard_map/ppermute | solution.py:446
  57.3 0.5 collective-permute-start.6
  57.8 2.1 %collective-permute-start.7 = (f32[64,640]{1,0:T(8,128)S(1)}, f32[64,640]{1,0:T(8,128)S(1)}, u32[]{:S(2)}, u32[]{:S(2)}) collective-permute-start(f32[64,640]{1,0:T(8,128)S(1)} %shard_map.82.own), channel_id=1, source_target_pairs={{0,4},{2,6},{4,0},{6,2},{1,5},{3,7},{5,1},{7,3},{8,12},{10,14},{12... | collective-permute-start | bytes 491528 | tf_op jit(solution)/shard_map/ppermute | solution.py:442
  59.9 0.4 collective-permute-start.8
  60.3 1.1 collective-permute-start.11
  61.4 1.0 shard_map.85
  62.3 3.5 %all-to-all-start.2 = ((f32[4,64,768]{2,1,0:T(8,128)}), f32[4,64,768]{2,1,0:T(8,128)S(1)}, u32[]{:S(2)}, u32[]{:S(2)}) async-start(f32[4,64,768]{2,1,0:T(8,128)} %shard_map.85), calls=%async_computation.2 | async-start | bytes 1572864 | tf_op jit(solution)/shard_map/all_to_all | solution.py:491
  65.8 2.6 %collective-permute-start.4 = (bf16[512,768]{1,0:T(8,128)(2,1)S(1)}, bf16[512,768]{1,0:T(8,128)(2,1)}, u32[]{:S(2)}, u32[]{:S(2)}) collective-permute-start(bf16[512,768]{1,0:T(8,128)(2,1)S(1)} %copy-done), channel_id=1, source_target_pairs={{0,6},{2,0},{4,2},{6,4},{1,7},{3,1},{5,3},{7,5},{8,14},{10,8},{12,... | collective-permute-start | bytes 2359304 | tf_op jit(solution)/shard_map/ppermute | solution.py:442
  68.5 5.8 %shard_map.83 = (f32[64,64]{1,0:T(8,128)S(1)}, bf16[384,64]{1,0:T(8,128)(2,1)S(1)}, bf16[128,512]{1,0:T(8,128)(2,1)S(1)}) custom-call(f32[64,640]{1,0:T(8,128)S(1)} %shard_map.82.own, f32[64,640]{1,0:T(8,128)S(1)} %collective-permute-done.6.one, f32[64,640]{1,0:T(8,128)S(1)} %collective-permute-done.7.two, f32[64,640]{1,0:T(8,128)S(1)} %collective-permute-done.8.three, ...), custom_call_target="tpu_custom_call" | custom-call | flops 6000000000 | bytes 1048576 | tf_op jit(solution)/shard_map/pallas_call | solution.py:247
  74.2 18.5 %all-to-all-done.2.terms = f32[4,64,768]{2,1,0:T(8,128)S(1)} async-done(((f32[4,64,768]{2,1,0:T(8,128)}), f32[4,64,768]{2,1,0:T(8,128)S(1)}, u32[]{:S(2)}, u32[]{:S(2)}) %all-to-all-start.2) | async-done | bytes 786464 | tf_op jit(solution)/shard_map/all_to_all | solution.py:491
  92.7 1.2 shard_map.86
  93.9 3.9 %all-to-all-start.3 = ((bf16[32,16,128]{2,1,0:T(8,128)(2,1)}), bf16[32,16,128]{2,1,0:T(8,128)(2,1)S(1)}, u32[]{:S(2)}, u32[]{:S(2)}) async-start(bf16[32,16,128]{2,1,0:T(8,128)(2,1)} %shard_map.86), calls=%async_computation.3 | async-start | bytes 262144 | tf_op jit(solution)/shard_map/all_to_all | solution.py:450
  97.8 1.0 slice.10
  98.9 1.0 slice.9
  100.0 2.7 %collective-permute-start.10 = (bf16[256,768]{1,0:T(8,128)(2,1)S(1)}, bf16[256,768]{1,0:T(8,128)(2,1)}, u32[]{:S(2)}, u32[]{:S(2)}) collective-permute-start(bf16[256,768]{1,0:T(8,128)(2,1)S(1)} %slice.9), channel_id=1, source_target_pairs={{0,6},{2,0},{4,2},{6,4},{1,7},{3,1},{5,3},{7,5},{8,14},{10,8},{12,... | collective-permute-start | bytes 1179656 | tf_op jit(solution)/shard_map/ppermute | solution.py:442
  102.7 4.5 %all-to-all-done.3.arrived = bf16[32,16,128]{2,1,0:T(8,128)(2,1)S(1)} async-done(((bf16[32,16,128]{2,1,0:T(8,128)(2,1)}), bf16[32,16,128]{2,1,0:T(8,128)(2,1)S(1)}, u32[]{:S(2)}, u32[]{:S(2)}) %all-to-all-start.3) | async-done | bytes 131104 | tf_op jit(solution)/shard_map/all_to_all | solution.py:450
  107.2 0.7 shard_map.88
  107.9 4.7 %all-to-all-start.4 = ((bf16[32,16,128]{2,1,0:T(8,128)(2,1)}), bf16[32,16,128]{2,1,0:T(8,128)(2,1)S(1)}, u32[]{:S(2)}, u32[]{:S(2)}) async-start(bf16[32,16,128]{2,1,0:T(8,128)(2,1)} %shard_map.88), calls=%async_computation.4 | async-start | bytes 262144 | tf_op jit(solution)/shard_map/all_to_all | solution.py:450
  112.6 2.5 %collective-permute-start.17 = (bf16[512,768]{1,0:T(8,128)(2,1)}, bf16[512,768]{1,0:T(8,128)(2,1)S(1)}, u32[]{:S(2)}, u32[]{:S(2)}) collective-permute-start(bf16[512,768]{1,0:T(8,128)(2,1)} %collective-permute-done.11.rest_4_), channel_id=1, source_target_pairs={{0,1},{1,0},{2,3},{3,2},{4,5},{5,4},{6,7},{7,6},{8,9},{9,8},{10,11... | collective-permute-start | bytes 2359304 | tf_op jit(solution)/shard_map/ppermute | solution.py:446
  115.2 0.4 collective-permute-start.14
  115.6 6.3 %all-to-all-done.4 = bf16[32,16,128]{2,1,0:T(8,128)(2,1)S(1)} async-done(((bf16[32,16,128]{2,1,0:T(8,128)(2,1)}), bf16[32,16,128]{2,1,0:T(8,128)(2,1)S(1)}, u32[]{:S(2)}, u32[]{:S(2)}) %all-to-all-start.4) | async-done | bytes 131104 | tf_op jit(solution)/shard_map/all_to_all | solution.py:450
  122.0 0.2 collective-permute-start.19
  122.2 0.6 collective-permute-start.21
  122.8 2.8 %collective-permute-done.19.b1 = bf16[24,16,128]{2,1,0:T(8,128)(2,1)S(1)} collective-permute-done((bf16[24,16,128]{2,1,0:T(8,128)(2,1)S(1)}, bf16[24,16,128]{2,1,0:T(8,128)(2,1)S(1)}, u32[]{:S(2)}, u32[]{:S(2)}) %collective-permute-start.19) | collective-permute-done | bytes 98336 | tf_op jit(solution)/shard_map/ppermute | solution.py:442
  125.5 1.6 %collective-permute-done.21.b2 = bf16[24,16,128]{2,1,0:T(8,128)(2,1)S(1)} collective-permute-done((bf16[24,16,128]{2,1,0:T(8,128)(2,1)S(1)}, bf16[24,16,128]{2,1,0:T(8,128)(2,1)S(1)}, u32[]{:S(2)}, u32[]{:S(2)}) %collective-permute-start.21) | collective-permute-done | bytes 98336 | tf_op jit(solution)/shard_map/ppermute | solution.py:442
  127.2 4.8 %collective-permute-start.16 = (bf16[256,768]{1,0:T(8,128)(2,1)}, bf16[256,768]{1,0:T(8,128)(2,1)S(1)}, u32[]{:S(2)}, u32[]{:S(2)}) collective-permute-start(bf16[256,768]{1,0:T(8,128)(2,1)} %collective-permute-done.12.rest_3_), channel_id=1, source_target_pairs={{0,1},{1,0},{2,3},{3,2},{4,5},{5,4},{6,7},{7,6},{8,9},{9,8},{10,11... | collective-permute-start | bytes 1179656 | tf_op jit(solution)/shard_map/ppermute | solution.py:446
  131.9 4.2 %collective-permute-start.15 = (bf16[256,768]{1,0:T(8,128)(2,1)}, bf16[256,768]{1,0:T(8,128)(2,1)S(1)}, u32[]{:S(2)}, u32[]{:S(2)}) collective-permute-start(bf16[256,768]{1,0:T(8,128)(2,1)} %collective-permute-done.10.rest_2_), channel_id=1, source_target_pairs={{0,1},{1,0},{2,3},{3,2},{4,5},{5,4},{6,7},{7,6},{8,9},{9,8},{10,11... | collective-permute-start | bytes 1179656 | tf_op jit(solution)/shard_map/ppermute | solution.py:446
  136.2 1.5 collective-permute-done.15.rest_7_
  137.7 0.4 collective-permute-start.20
  138.1 0.1 collective-permute-start.22
  138.2 0.4 collective-permute-start.24
  138.6 0.4 copy-done.3
  138.9 7.2 %shard_map.87.fed = bf16[8,384,768]{2,1,0:T(8,128)(2,1)} custom-call(bf16[512,384]{1,0:T(8,128)(2,1)S(1)} %copy-done.1, bf16[384,6144]{1,0:T(8,128)(2,1)} %bitcast.10, bf16[512,768]{1,0:T(8,128)(2,1)} %rest_0_.1, bf16[512,768]{1,0:T(8,128)(2,1)} %collective-permute-done.4.rest_1_, bf16[256,768]{1,0:T(8,128)(2,1)} %collective-permute-done.10.rest_2_, ...), custom_call_target="tpu_custom_call" | custom-call | flops 6000000000 | bytes 1048576 | tf_op jit(solution)/shard_map/pallas_call | solution.py:313
  146.1 2.5 %shard_map.89 = (bf16[1,384,6144]{2,1,0:T(8,128)(2,1)}, bf16[64,6144]{1,0:T(8,128)(2,1)S(1)}, bf16[3,384,768]{2,1,0:T(8,128)(2,1)S(1)}, bf16[4,384,768]{2,1,0:T(8,128)(2,1)S(1)}) custom-call(bf16[8,384,768]{2,1,0:T(8,128)(2,1)} %shard_map.87.fed, bf16[384,64]{1,0:T(8,128)(2,1)S(1)} %get-tuple-element.43.basis, bf16[24,16,128]{2,1,0:T(8,128)(2,1)S(1)} %slice.12.b0), custom_call_target="tpu_custom_call" | custom-call | flops 1000000000 | bytes 1048576 | tf_op jit(solution)/shard_map/pallas_call | solution.py:367
  148.6 1.6 %shard_map.90 = (bf16[1,384,6144]{2,1,0:T(8,128)(2,1)}, bf16[64,6144]{1,0:T(8,128)(2,1)S(1)}) custom-call(bf16[3,384,768]{2,1,0:T(8,128)(2,1)S(1)} %get-tuple-element.45.fed, bf16[384,64]{1,0:T(8,128)(2,1)S(1)} %get-tuple-element.43.basis, bf16[24,16,128]{2,1,0:T(8,128)(2,1)S(1)} %collective-permute-done.19.b1, ...), custom_call_target="tpu_custom_call", output_to_operand_aliasing={{0}: (5, {})} | custom-call | flops 1000000000 | bytes 1048576 | tf_op jit(solution)/shard_map/pallas_call | solution.py:397
  150.3 2.8 %shard_map.91 = (bf16[1,384,6144]{2,1,0:T(8,128)(2,1)}, f32[192,384]{1,0:T(8,128)}, bf16[64,6144]{1,0:T(8,128)(2,1)}) custom-call(bf16[4,384,768]{2,1,0:T(8,128)(2,1)S(1)} %get-tuple-element.44.fed, bf16[384,64]{1,0:T(8,128)(2,1)S(1)} %get-tuple-element.43.basis, ...), custom_call_target="tpu_custom_call", output_to_operand_aliasing={{0}: (7, {})} | custom-call | flops 1000000000 | bytes 1048576 | tf_op jit(solution)/shard_map/pallas_call | solution.py:429
  (41 shorter events, 0.6 us)
Async XLA Ops:
  2.6 4.3 %collective-permute-start = (f32[64,512]{1,0:T(8,128)S(1)}, f32[64,512]{1,0:T(8,128)S(1)}, u32[]{:S(2)}, u32[]{:S(2)}) collective-permute-start(f32[64,512]{1,0:T(8,128)S(1)} %shard_map.76.a), channel_id=1, source_target_pairs={{0,1},{1,0},{2,3},{3,2},{4,5},{5,4},{6,7},{7,6},{8,9},{9,8},{10,11... | collective-permute-start | bytes 393224 | tf_op jit(solution)/shard_map/ppermute | solution.py:446
  6.9 7.1 %collective-permute-start.1 = (bf16[64,512]{1,0:T(8,128)(2,1)S(1)}, bf16[64,512]{1,0:T(8,128)(2,1)S(1)}, u32[]{:S(2)}, u32[]{:S(2)}) collective-permute-start(bf16[64,512]{1,0:T(8,128)(2,1)S(1)} %get-tuple-element.28), channel_id=1, source_target_pairs={{0,2},{2,4},{4,6},{6,0},{1,3},{3,5},{5,7},{7,1},{8,10},{10,12},{12... | collective-permute-start | bytes 196616 | tf_op jit(solution)/shard_map/ppermute | solution.py:442
  7.0 7.1 %collective-permute-start.2 = (bf16[64,512]{1,0:T(8,128)(2,1)S(1)}, bf16[64,512]{1,0:T(8,128)(2,1)S(1)}, u32[]{:S(2)}, u32[]{:S(2)}) collective-permute-start(bf16[64,512]{1,0:T(8,128)(2,1)S(1)} %get-tuple-element.28), channel_id=1, source_target_pairs={{0,4},{2,6},{4,0},{6,2},{1,5},{3,7},{5,1},{7,3},{8,12},{10,14},{12... | collective-permute-start | bytes 196616 | tf_op jit(solution)/shard_map/ppermute | solution.py:442
  9.2 4.9 %collective-permute-start.3 = (bf16[64,512]{1,0:T(8,128)(2,1)S(1)}, bf16[64,512]{1,0:T(8,128)(2,1)S(1)}, u32[]{:S(2)}, u32[]{:S(2)}) collective-permute-start(bf16[64,512]{1,0:T(8,128)(2,1)S(1)} %get-tuple-element.28), channel_id=1, source_target_pairs={{0,6},{2,0},{4,2},{6,4},{1,7},{3,1},{5,3},{7,5},{8,14},{10,8},{12,... | collective-permute-start | bytes 196616 | tf_op jit(solution)/shard_map/ppermute | solution.py:442
  10.3 3.8 %copy-start.1 = (bf16[512,384]{1,0:T(8,128)(2,1)S(1)}, bf16[512,384]{1,0:T(8,128)(2,1)}, u32[]{:S(2)}) copy-start(bf16[512,384]{1,0:T(8,128)(2,1)} %acts.5) | copy-start | bytes 1179652
  47.6 12.7 %copy-start = (bf16[512,768]{1,0:T(8,128)(2,1)S(1)}, bf16[512,768]{1,0:T(8,128)(2,1)}, u32[]{:S(2)}) copy-start(bf16[512,768]{1,0:T(8,128)(2,1)} %rest_0_.1) | copy-start | bytes 2359300
  51.2 10.1 %collective-permute-start.9 = (f32[4,64,768]{2,1,0:T(8,128)S(1)}, f32[4,64,768]{2,1,0:T(8,128)S(1)}, u32[]{:S(2)}, u32[]{:S(2)}) collective-permute-start(f32[4,64,768]{2,1,0:T(8,128)S(1)} %get-tuple-element.37), channel_id=1, source_target_pairs={{0,1},{1,0},{2,3},{3,2},{4,5},{5,4},{6,7},{7,6},{8,9},{9,8},{10,11... | collective-permute-start | bytes 2359304 | tf_op jit(solution)/shard_map/ppermute | solution.py:446
  55.1 2.1 %collective-permute-start.5 = (f32[64,640]{1,0:T(8,128)S(1)}, f32[64,640]{1,0:T(8,128)S(1)}, u32[]{:S(2)}, u32[]{:S(2)}) collective-permute-start(f32[64,640]{1,0:T(8,128)S(1)} %get-tuple-element.31.a), channel_id=1, source_target_pairs={{0,1},{1,0},{2,3},{3,2},{4,5},{5,4},{6,7},{7,6},{8,9},{9,8},{10,11... | collective-permute-start | bytes 491528 | tf_op jit(solution)/shard_map/ppermute | solution.py:446
  57.3 11.2 %collective-permute-start.6 = (f32[64,640]{1,0:T(8,128)S(1)}, f32[64,640]{1,0:T(8,128)S(1)}, u32[]{:S(2)}, u32[]{:S(2)}) collective-permute-start(f32[64,640]{1,0:T(8,128)S(1)} %shard_map.82.own), channel_id=1, source_target_pairs={{0,2},{2,4},{4,6},{6,0},{1,3},{3,5},{5,7},{7,1},{8,10},{10,12},{12... | collective-permute-start | bytes 491528 | tf_op jit(solution)/shard_map/ppermute | solution.py:442
  57.8 10.7 %collective-permute-start.7 = (f32[64,640]{1,0:T(8,128)S(1)}, f32[64,640]{1,0:T(8,128)S(1)}, u32[]{:S(2)}, u32[]{:S(2)}) collective-permute-start(f32[64,640]{1,0:T(8,128)S(1)} %shard_map.82.own), channel_id=1, source_target_pairs={{0,4},{2,6},{4,0},{6,2},{1,5},{3,7},{5,1},{7,3},{8,12},{10,14},{12... | collective-permute-start | bytes 491528 | tf_op jit(solution)/shard_map/ppermute | solution.py:442
  59.9 8.6 %collective-permute-start.8 = (f32[64,640]{1,0:T(8,128)S(1)}, f32[64,640]{1,0:T(8,128)S(1)}, u32[]{:S(2)}, u32[]{:S(2)}) collective-permute-start(f32[64,640]{1,0:T(8,128)S(1)} %shard_map.82.own), channel_id=1, source_target_pairs={{0,6},{2,0},{4,2},{6,4},{1,7},{3,1},{5,3},{7,5},{8,14},{10,8},{12,... | collective-permute-start | bytes 491528 | tf_op jit(solution)/shard_map/ppermute | solution.py:442
  60.3 37.5 %collective-permute-start.11 = (bf16[512,768]{1,0:T(8,128)(2,1)S(1)}, bf16[512,768]{1,0:T(8,128)(2,1)}, u32[]{:S(2)}, u32[]{:S(2)}) collective-permute-start(bf16[512,768]{1,0:T(8,128)(2,1)S(1)} %copy-done), channel_id=1, source_target_pairs={{0,2},{2,4},{4,6},{6,0},{1,3},{3,5},{5,7},{7,1},{8,10},{10,12},{12... | collective-permute-start | bytes 2359304 | tf_op jit(solution)/shard_map/ppermute | solution.py:442
  62.3 30.4 %all-to-all-start.2 = ((f32[4,64,768]{2,1,0:T(8,128)}), f32[4,64,768]{2,1,0:T(8,128)S(1)}, u32[]{:S(2)}, u32[]{:S(2)}) async-start(f32[4,64,768]{2,1,0:T(8,128)} %shard_map.85), calls=%async_computation.2 | async-start | bytes 1572864 | tf_op jit(solution)/shard_map/all_to_all | solution.py:491
  65.8 33.1 %collective-permute-start.4 = (bf16[512,768]{1,0:T(8,128)(2,1)S(1)}, bf16[512,768]{1,0:T(8,128)(2,1)}, u32[]{:S(2)}, u32[]{:S(2)}) collective-permute-start(bf16[512,768]{1,0:T(8,128)(2,1)S(1)} %copy-done), channel_id=1, source_target_pairs={{0,6},{2,0},{4,2},{6,4},{1,7},{3,1},{5,3},{7,5},{8,14},{10,8},{12,... | collective-permute-start | bytes 2359304 | tf_op jit(solution)/shard_map/ppermute | solution.py:442
  93.9 13.3 %all-to-all-start.3 = ((bf16[32,16,128]{2,1,0:T(8,128)(2,1)}), bf16[32,16,128]{2,1,0:T(8,128)(2,1)S(1)}, u32[]{:S(2)}, u32[]{:S(2)}) async-start(bf16[32,16,128]{2,1,0:T(8,128)(2,1)} %shard_map.86), calls=%async_computation.3 | async-start | bytes 262144 | tf_op jit(solution)/shard_map/all_to_all | solution.py:450
  98.8 23.1 %collective-permute-start.12 = (bf16[256,768]{1,0:T(8,128)(2,1)S(1)}, bf16[256,768]{1,0:T(8,128)(2,1)}, u32[]{:S(2)}, u32[]{:S(2)}) collective-permute-start(bf16[256,768]{1,0:T(8,128)(2,1)S(1)} %slice.10), channel_id=1, source_target_pairs={{0,2},{2,4},{4,6},{6,0},{1,3},{3,5},{5,7},{7,1},{8,10},{10,12},{12... | collective-permute-start | bytes 1179656 | tf_op jit(solution)/shard_map/ppermute | solution.py:442
  100.0 22.2 %collective-permute-start.10 = (bf16[256,768]{1,0:T(8,128)(2,1)S(1)}, bf16[256,768]{1,0:T(8,128)(2,1)}, u32[]{:S(2)}, u32[]{:S(2)}) collective-permute-start(bf16[256,768]{1,0:T(8,128)(2,1)S(1)} %slice.9), channel_id=1, source_target_pairs={{0,6},{2,0},{4,2},{6,4},{1,7},{3,1},{5,3},{7,5},{8,14},{10,8},{12,... | collective-permute-start | bytes 1179656 | tf_op jit(solution)/shard_map/ppermute | solution.py:442
  107.9 14.1 %all-to-all-start.4 = ((bf16[32,16,128]{2,1,0:T(8,128)(2,1)}), bf16[32,16,128]{2,1,0:T(8,128)(2,1)S(1)}, u32[]{:S(2)}, u32[]{:S(2)}) async-start(bf16[32,16,128]{2,1,0:T(8,128)(2,1)} %shard_map.88), calls=%async_computation.4 | async-start | bytes 262144 | tf_op jit(solution)/shard_map/all_to_all | solution.py:450
  112.6 25.4 %collective-permute-start.17 = (bf16[512,768]{1,0:T(8,128)(2,1)}, bf16[512,768]{1,0:T(8,128)(2,1)S(1)}, u32[]{:S(2)}, u32[]{:S(2)}) collective-permute-start(bf16[512,768]{1,0:T(8,128)(2,1)} %collective-permute-done.11.rest_4_), channel_id=1, source_target_pairs={{0,1},{1,0},{2,3},{3,2},{4,5},{5,4},{6,7},{7,6},{8,9},{9,8},{10,11... | collective-permute-start | bytes 2359304 | tf_op jit(solution)/shard_map/ppermute | solution.py:446
  115.1 23.1 %collective-permute-start.13 = (bf16[512,768]{1,0:T(8,128)(2,1)S(1)}, bf16[512,768]{1,0:T(8,128)(2,1)}, u32[]{:S(2)}, u32[]{:S(2)}) collective-permute-start(bf16[512,768]{1,0:T(8,128)(2,1)S(1)} %copy-done), channel_id=1, source_target_pairs={{0,1},{1,0},{2,3},{3,2},{4,5},{5,4},{6,7},{7,6},{8,9},{9,8},{10,11... | collective-permute-start | bytes 2359304 | tf_op jit(solution)/shard_map/ppermute | solution.py:446
  115.2 23.4 %collective-permute-start.14 = (bf16[512,768]{1,0:T(8,128)(2,1)}, bf16[512,768]{1,0:T(8,128)(2,1)}, u32[]{:S(2)}, u32[]{:S(2)}) collective-permute-start(bf16[512,768]{1,0:T(8,128)(2,1)} %collective-permute-done.4.rest_1_), channel_id=1, source_target_pairs={{0,1},{1,0},{2,3},{3,2},{4,5},{5,4},{6,7},{7,6},{8,9},{9,8},{10,11... | collective-permute-start | bytes 2359304 | tf_op jit(solution)/shard_map/ppermute | solution.py:446
  122.0 3.5 %collective-permute-start.19 = (bf16[24,16,128]{2,1,0:T(8,128)(2,1)S(1)}, bf16[24,16,128]{2,1,0:T(8,128)(2,1)S(1)}, u32[]{:S(2)}, u32[]{:S(2)}) collective-permute-start(bf16[24,16,128]{2,1,0:T(8,128)(2,1)S(1)} %slice.12.b0), channel_id=1, source_target_pairs={{0,6},{2,0},{4,2},{6,4},{1,7},{3,1},{5,3},{7,5},{8,14},{10,8},{12,... | collective-permute-start | bytes 294920 | tf_op jit(solution)/shard_map/ppermute | solution.py:442
  122.2 5.0 %collective-permute-start.21 = (bf16[24,16,128]{2,1,0:T(8,128)(2,1)S(1)}, bf16[24,16,128]{2,1,0:T(8,128)(2,1)S(1)}, u32[]{:S(2)}, u32[]{:S(2)}) collective-permute-start(bf16[24,16,128]{2,1,0:T(8,128)(2,1)S(1)} %slice.12.b0), channel_id=1, source_target_pairs={{0,4},{2,6},{4,0},{6,2},{1,5},{3,7},{5,1},{7,3},{8,12},{10,14},{12... | collective-permute-start | bytes 294920 | tf_op jit(solution)/shard_map/ppermute | solution.py:442
  125.5 6.4 %collective-permute-start.23 = (bf16[24,16,128]{2,1,0:T(8,128)(2,1)S(1)}, bf16[24,16,128]{2,1,0:T(8,128)(2,1)S(1)}, u32[]{:S(2)}, u32[]{:S(2)}) collective-permute-start(bf16[24,16,128]{2,1,0:T(8,128)(2,1)S(1)} %slice.12.b0), channel_id=1, source_target_pairs={{0,2},{2,4},{4,6},{6,0},{1,3},{3,5},{5,7},{7,1},{8,10},{10,12},{12... | collective-permute-start | bytes 294920 | tf_op jit(solution)/shard_map/ppermute | solution.py:442
  127.2 9.0 %collective-permute-start.16 = (bf16[256,768]{1,0:T(8,128)(2,1)}, bf16[256,768]{1,0:T(8,128)(2,1)S(1)}, u32[]{:S(2)}, u32[]{:S(2)}) collective-permute-start(bf16[256,768]{1,0:T(8,128)(2,1)} %collective-permute-done.12.rest_3_), channel_id=1, source_target_pairs={{0,1},{1,0},{2,3},{3,2},{4,5},{5,4},{6,7},{7,6},{8,9},{9,8},{10,11... | collective-permute-start | bytes 1179656 | tf_op jit(solution)/shard_map/ppermute | solution.py:446
  131.9 5.7 %collective-permute-start.15 = (bf16[256,768]{1,0:T(8,128)(2,1)}, bf16[256,768]{1,0:T(8,128)(2,1)S(1)}, u32[]{:S(2)}, u32[]{:S(2)}) collective-permute-start(bf16[256,768]{1,0:T(8,128)(2,1)} %collective-permute-done.10.rest_2_), channel_id=1, source_target_pairs={{0,1},{1,0},{2,3},{3,2},{4,5},{5,4},{6,7},{7,6},{8,9},{9,8},{10,11... | collective-permute-start | bytes 1179656 | tf_op jit(solution)/shard_map/ppermute | solution.py:446
  136.1 2.5 %copy-start.4 = (bf16[256,768]{1,0:T(8,128)(2,1)}, bf16[256,768]{1,0:T(8,128)(2,1)S(1)}, u32[]{:S(2)}) copy-start(bf16[256,768]{1,0:T(8,128)(2,1)S(1)} %collective-permute-done.16.rest_8_) | copy-start | bytes 1179652
  136.1 14.1 %collective-permute-start.18 = (bf16[24,16,128]{2,1,0:T(8,128)(2,1)S(1)}, bf16[24,16,128]{2,1,0:T(8,128)(2,1)S(1)}, u32[]{:S(2)}, u32[]{:S(2)}) collective-permute-start(bf16[24,16,128]{2,1,0:T(8,128)(2,1)S(1)} %slice.12.b0), channel_id=1, source_target_pairs={{0,1},{1,0},{2,3},{3,2},{4,5},{5,4},{6,7},{7,6},{8,9},{9,8},{10,11... | collective-permute-start | bytes 294920 | tf_op jit(solution)/shard_map/ppermute | solution.py:446
  137.7 0.9 copy-start.5
  137.7 12.5 %collective-permute-start.20 = (bf16[24,16,128]{2,1,0:T(8,128)(2,1)S(1)}, bf16[24,16,128]{2,1,0:T(8,128)(2,1)S(1)}, u32[]{:S(2)}, u32[]{:S(2)}) collective-permute-start(bf16[24,16,128]{2,1,0:T(8,128)(2,1)S(1)} %collective-permute-done.19.b1), channel_id=1, source_target_pairs={{0,1},{1,0},{2,3},{3,2},{4,5},{5,4},{6,7},{7,6},{8,9},{9,8},{10,11... | collective-permute-start | bytes 294920 | tf_op jit(solution)/shard_map/ppermute | solution.py:446
  138.1 0.9 copy-start.3
  138.1 12.2 %collective-permute-start.22 = (bf16[24,16,128]{2,1,0:T(8,128)(2,1)S(1)}, bf16[24,16,128]{2,1,0:T(8,128)(2,1)S(1)}, u32[]{:S(2)}, u32[]{:S(2)}) collective-permute-start(bf16[24,16,128]{2,1,0:T(8,128)(2,1)S(1)} %collective-permute-done.21.b2), channel_id=1, source_target_pairs={{0,1},{1,0},{2,3},{3,2},{4,5},{5,4},{6,7},{7,6},{8,9},{9,8},{10,11... | collective-permute-start | bytes 294920 | tf_op jit(solution)/shard_map/ppermute | solution.py:446
  138.2 12.0 %collective-permute-start.24 = (bf16[24,16,128]{2,1,0:T(8,128)(2,1)S(1)}, bf16[24,16,128]{2,1,0:T(8,128)(2,1)S(1)}, u32[]{:S(2)}, u32[]{:S(2)}) collective-permute-start(bf16[24,16,128]{2,1,0:T(8,128)(2,1)S(1)} %collective-permute-done.23.b3), channel_id=1, source_target_pairs={{0,1},{1,0},{2,3},{3,2},{4,5},{5,4},{6,7},{7,6},{8,9},{9,8},{10,11... | collective-permute-start | bytes 294920 | tf_op jit(solution)/shard_map/ppermute | solution.py:446
  148.6 1.6 %copy-start.2 = (f32[384,192]{0,1:T(8,128)S(1)}, f32[384,192]{0,1:T(8,128)}, u32[]{:S(2)}) copy-start(f32[384,192]{0,1:T(8,128)} %param.9) | copy-start | bytes 884740

commit v6 on v5

--- a/solution.py
+++ b/solution.py
@@ -167,15 +167,24 @@
     return call(sum_and_copy_body, on_chip(arrived.shape, dtype), 10**7)(arrived)
 
 
-def left_products_body(tiles, acts, left_out, left_terms, small):
+HALF = TOK // 2
+
+
+def left_products_body(tiles, acts, left_out, left_terms, mine, theirs):
     rows = [jnp.concatenate([tiles[4 * r + j] for j in range(3)], axis=1) for r in range(8)]
     left = jnp.concatenate(rows, axis=0)
     left_out[...] = left
     terms = two_terms(left)
     left_terms[...] = terms
-    small[:, :TOK] = halves_added(dot(terms, acts[...], NT))
+    acts_left = halves_added(dot(terms, acts[...], NT))
     gram = dot(left, left, NT, HIGHEST)
-    small[:, TOK:] = jnp.concatenate([gram, jnp.zeros_like(gram)], axis=1)
+    gram = jnp.concatenate([gram, jnp.zeros_like(gram)], axis=1)
+    first = lax.axis_index(CC) == 0
+    low, high = acts_left[:, :HALF], acts_left[:, HALF:]
+    mine[:, :HALF] = jnp.where(first, low, high)
+    mine[:, HALF:] = gram
+    theirs[:, :HALF] = jnp.where(first, high, low)
+    theirs[:, HALF:] = gram
 
 
 def left_products(tiles, acts):
@@ -184,10 +193,23 @@
         (
             on_chip((RANK, ROWS), F32),
             on_chip((2 * RANK, ROWS), BF16),
-            on_chip((RANK, TOK + 128), F32),
+            on_chip((RANK, HALF + 128), F32),
+            on_chip((RANK, HALF + 128), F32),
         ),
         10**8,
     )(tiles, acts)
+
+
+def small_sum_body(own, one, two, three, acts_left, gram):
+    total = own[...] + one[...] + two[...] + three[...]
+    acts_left[...] = total[:, :HALF]
+    gram[...] = total[:, HALF:]
+
+
+def small_sum(own, parts):
+    return call(
+        small_sum_body, (on_chip((RANK, HALF), F32), on_chip((RANK, 128), F32)), 10**7
+    )(own, *parts)
 
 
 def right_blocks_body(left_terms, error, far, near, held, sems):
@@ -225,35 +247,44 @@
     return call(add_body, on_chip(a.shape, F32), 10**7)(a, b)
 
 
-def factor_body(own, one, two, three, left, inverse_out, basis_out, acts_left):
-    small = own[...] + one[...] + two[...] + three[...]
-    acts_left[...] = two_terms(small[:, :TOK])
-    lanes = lax.broadcasted_iota(jnp.int32, (RANK, RANK), 1)
-    subs = lax.broadcasted_iota(jnp.int32, (RANK, RANK), 0)
-    eye = jnp.where(lanes == subs, 1.0, 0.0).astype(F32)
-    work = jnp.concatenate([small[:, TOK : TOK + RANK], eye], axis=1)
-    rows = lax.broadcasted_iota(jnp.int32, (RANK, 2 * RANK), 0)
+def factor_body(gram, left, inverse_out, basis_out):
+    lanes = lax.broadcasted_iota(jnp.int32, (8, 2 * RANK), 1)
+    subs = lax.broadcasted_iota(jnp.int32, (8, 2 * RANK), 0)
+    work = []
+    for i in range(8):
+        eye = jnp.where(lanes == subs + (RANK + 8 * i), 1.0, 0.0).astype(F32)
+        work.append(jnp.where(lanes < RANK, gram[8 * i : 8 * i + 8, :], eye))
     for j in range(RANK - 1):
-        row = work[j : j + 1, :]
-        ratio = work[:, j : j + 1] / work[j : j + 1, j : j + 1]
-        work = work - jnp.where(rows > j, ratio * row, 0.0)
-    pivots = jnp.sum(jnp.where(lanes == subs, work[:, :RANK], 0.0), axis=1, keepdims=True)
-    inverse = work[:, RANK:] / jnp.sqrt(pivots)
+        t, r = divmod(j, 8)
+        row = work[t][r : r + 1, :]
+        row = row * (1.0 / row[:, j : j + 1])
+        for i in range(t, 8):
+            change = work[i][:, j : j + 1] * row
+            if i == t:
+                change = jnp.where(subs > r, change, 0.0)
+            work[i] = work[i] - change
+    parts = []
+    for i in range(8):
+        pivot = jnp.sum(jnp.where(lanes == subs + 8 * i, work[i], 0.0), axis=1, keepdims=True)
+        parts.append(work[i][:, RANK:] / jnp.sqrt(pivot))
+    inverse = jnp.concatenate(parts, axis=0)
     inverse_out[...] = inverse
     basis_out[...] = dot(inverse, left[...], NN, HIGHEST).T.astype(BF16)
 
 
-def factor(own, parts, left):
-    return call(
-        factor_body,
-        (on_chip((RANK, RANK), F32), on_chip((ROWS, RANK), BF16), on_chip((2 * RANK, TOK), BF16)),
-        6 * 10**9,
-    )(own, *parts, left)
-
-
-def right_term_body(inverse, acts_left, grads, terms, out):
+def factor(gram, left):
+    return call(
+        factor_body, (on_chip((RANK, RANK), F32), on_chip((ROWS, RANK), BF16)), 6 * 10**9
+    )(gram, left)
+
+
+def right_term_body(inverse, half, other, grads, terms, out):
+    first = lax.axis_index(CC) == 0
+    low = jnp.where(first, half[...], other[...])
+    high = jnp.where(first, other[...], half[...])
+    acts_left = two_terms(jnp.concatenate([low, high], axis=1))
     total = terms[0] + terms[1] + terms[2] + terms[3]
-    total = total + halves_added(dot(acts_left[...], grads[...]))
+    total = total + halves_added(dot(acts_left, grads[...]))
     right = dot(inverse[...], total, NN, HIGHEST)
     for j in range(6):
         for r in range(4):
@@ -261,9 +292,9 @@
     out[24:] = jnp.zeros((8, 16, 128), out.dtype)
 
 
-def right_term(inverse, acts_left, grads, terms):
+def right_term(inverse, half, other, grads, terms):
     return call(right_term_body, on_chip((WORKERS, 16, 128), BF16), 10**8)(
-        inverse, acts_left, grads, terms
+        inverse, half, other, grads, terms
     )
 
 
@@ -479,8 +510,8 @@
     copies = sum_and_copy(arrived, F32)
     tiles = to_workers(copies)
 
-    left, left_terms, small = left_products(tiles, activations)
-    other_small = other_core(small)
+    left, left_terms, small, theirs = left_products(tiles, activations)
+    other_small = other_core(theirs)
     far, near = right_blocks(left_terms, own_error)
     got = other_core(far)
     small_parts = []
@@ -489,8 +520,10 @@
         small_parts.append(along_y(small, k))
     q = add(near, got)
     terms = lax.all_to_all(q, YY, split_axis=0, concat_axis=0, tiled=True)
-    inverse, basis, acts_left = factor(small, small_parts, left)
-    pieces = right_term(inverse, acts_left, own_grads, terms)
+    acts_left, gram = small_sum(small, small_parts)
+    acts_left_other = other_core(acts_left)
+    inverse, basis = factor(gram, left)
+    pieces = right_term(inverse, acts_left, acts_left_other, own_grads, terms)
 
     half = TOK // 2
     g2a = along_y(after(g1, pieces)[:half], -1)

time: 154 us -> 150 us (0.974)
  waiting for transfers between devices: 38.2 us -> 33.7 us
  starting transfers between devices: 45.9 us -> 47.6 us
    all_to_all x1, waiting for transfers between devices: 18.5 us -> 13.3 us  [step(): terms = lax.all_to_all(q, YY, split_axis=0, concat_axis=0, tiled=True)]
    ppermute x12 -> x13, starting transfers between devices: 20.2 us -> 22.7 us  [other_core(): return lax.ppermute(x, CC, [(0, 1), (1, 0)])]
    ppermute x12 -> x13, waiting for transfers between devices: 4.52 us -> 4.43 us  [other_core(): return lax.ppermute(x, CC, [(0, 1), (1, 0)])]
  transfers between devices with their start and end apart: 28 -> 29, of which waited for: 8 -> 8; matrix products, arithmetic and copies ran while one was open for 1% -> 1% of each run, Pallas kernels for 15% -> 16%
where the time goes in v6:
time: 150 us; the launch traced here: 149 us
  starting transfers between devices  47.6 us (32%)
  waiting for transfers between devices  33.7 us (22%)
  blocking collectives  32.8 us (22%)
  Pallas kernels  32.7 us (22%)
    all_to_all x2, blocking collectives, to_workers(): return lax.all_to_all(x, DP, split_axis=0, concat_axis=0, tiled=True)  32.8 us
    ppermute x13, starting transfers between devices, other_core(): return lax.ppermute(x, CC, [(0, 1), (1, 0)])  22.7 us
    ppermute x13, starting transfers between devices, along_y(): return lax.ppermute(x, YY, [(i, (i + k) % 4) for i in range(4)])  13.7 us
    all_to_all x1, waiting for transfers between devices, step(): terms = lax.all_to_all(q, YY, split_axis=0, concat_axis=0, tiled=True)  13.3 us
    all_to_all x2, waiting for transfers between devices, to_workers(): return lax.all_to_all(x, DP, split_axis=0, concat_axis=0, tiled=True)  11.8 us
    all_to_all x2, starting transfers between devices, to_workers(): return lax.all_to_all(x, DP, split_axis=0, concat_axis=0, tiled=True)  7.72 us
    pallas_call x1, Pallas kernels, fed_of(): call(fed_body, pltpu.HBM((8, ROWS, COLS), BF16), 6 * 10 ** 9, 24, in_spec...  7.16 us
    pallas_call x1, Pallas kernels, factor(): call(factor_body, (on_chip((RANK, RANK), F32), on_chip((ROWS, RANK), BF16...  5.71 us
  transfers between devices with their start and end apart: 29, of which 8 were waited for; matrix products, arithmetic and copies ran while one was open for 1% of the time, Pallas kernels for 16%

profile of v6, /device:TPU:1, one launch (start us, length us, event | category | flops | bytes accessed | tf_op | source)
XLA Modules:
  0.0 149.2 jit_solution(16344202100386996727)
XLA Ops:
  0.6 2.0 %shard_map.76.a = f32[64,512]{1,0:T(8,128)S(1)} custom-call(bf16[512,768]{1,0:T(8,128)(2,1)} %rest_0_.1, bf16[64,6144]{1,0:T(8,128)(2,1)} %bitcast.6), custom_call_target="tpu_custom_call" | custom-call | flops 100000000 | bytes 1048576 | tf_op jit(solution)/shard_map/pallas_call | solution.py:89
  2.6 3.3 %collective-permute-start = (f32[64,512]{1,0:T(8,128)S(1)}, f32[64,512]{1,0:T(8,128)S(1)}, u32[]{:S(2)}, u32[]{:S(2)}) collective-permute-start(f32[64,512]{1,0:T(8,128)S(1)} %shard_map.76.a), channel_id=1, source_target_pairs={{0,1},{1,0},{2,3},{3,2},{4,5},{5,4},{6,7},{7,6},{8,9},{9,8},{10,11... | collective-permute-start | bytes 393224 | tf_op jit(solution)/shard_map/ppermute | solution.py:477
  5.9 1.0 collective-permute-done.b
  7.0 2.2 %collective-permute-start.2 = (bf16[64,512]{1,0:T(8,128)(2,1)S(1)}, bf16[64,512]{1,0:T(8,128)(2,1)S(1)}, u32[]{:S(2)}, u32[]{:S(2)}) collective-permute-start(bf16[64,512]{1,0:T(8,128)(2,1)S(1)} %get-tuple-element.30), channel_id=1, source_target_pairs={{0,4},{2,6},{4,0},{6,2},{1,5},{3,7},{5,1},{7,3},{8,12},{10,14},{12... | collective-permute-start | bytes 196616 | tf_op jit(solution)/shard_map/ppermute | solution.py:473
  9.2 1.1 collective-permute-start.3
  10.3 3.8 %shard_map.78.from_error = f32[64,384]{1,0:T(8,128)S(1)} custom-call(bf16[384,6144]{1,0:T(8,128)(2,1)} %bitcast.8, bf16[64,6144]{1,0:T(8,128)(2,1)} %bitcast.7), custom_call_target="tpu_custom_call" | custom-call | flops 3000000000 | bytes 1048576 | tf_op jit(solution)/shard_map/pallas_call | solution.py:131
  14.1 0.2 shard_map.79
  14.3 20.2 %all_to_all.25.arrived = f32[32,8,128]{2,1,0:T(8,128)S(1)} all-to-all(f32[32,8,128]{2,1,0:T(8,128)S(1)} %shard_map.79), channel_id=1, replica_groups=mesh['dp_0'=8,'dp_1'=4,'mp_0'=4,'mp_1'=2] {'dp_0','dp_1'}, dimensions={0} | all-to-all | bytes 262144 | tf_op jit(solution)/shard_map/all_to_all | solution.py:481
  34.5 12.6 %all_to_all.26.tiles = f32[32,8,128]{2,1,0:T(8,128)S(1)} all-to-all(f32[32,8,128]{2,1,0:T(8,128)S(1)} %shard_map.80), channel_id=1, replica_groups=mesh['dp_0'=8,'dp_1'=4,'mp_0'=4,'mp_1'=2] {'dp_0','dp_1'}, dimensions={0} | all-to-all | bytes 262144 | tf_op jit(solution)/shard_map/all_to_all | solution.py:481
  47.2 0.4 shard_map.81
  47.6 3.6 %shard_map.85 = (f32[4,64,768]{2,1,0:T(8,128)S(1)}, f32[4,64,768]{2,1,0:T(8,128)S(1)}) custom-call(bf16[128,384]{1,0:T(8,128)(2,1)S(1)} %get-tuple-element.39.left_terms, bf16[384,6144]{1,0:T(8,128)(2,1)} %bitcast.9), custom_call_target="tpu_custom_call" | custom-call | flops 10000000000 | bytes 1048576 | tf_op jit(solution)/shard_map/pallas_call | solution.py:231
  51.2 3.9 %collective-permute-start.10 = (f32[4,64,768]{2,1,0:T(8,128)S(1)}, f32[4,64,768]{2,1,0:T(8,128)S(1)}, u32[]{:S(2)}, u32[]{:S(2)}) collective-permute-start(f32[4,64,768]{2,1,0:T(8,128)S(1)} %get-tuple-element.41), channel_id=1, source_target_pairs={{0,1},{1,0},{2,3},{3,2},{4,5},{5,4},{6,7},{7,6},{8,9},{9,8},{10,11... | collective-permute-start | bytes 2359304 | tf_op jit(solution)/shard_map/ppermute | solution.py:477
  55.1 0.1 collective-permute-start.5
  55.2 2.0 %collective-permute-done.5.b = f32[64,384]{1,0:T(8,128)S(1)} collective-permute-done((f32[64,384]{1,0:T(8,128)S(1)}, f32[64,384]{1,0:T(8,128)S(1)}, u32[]{:S(2)}, u32[]{:S(2)}) %collective-permute-start.5) | collective-permute-done | bytes 98336 | tf_op jit(solution)/shard_map/ppermute | solution.py:477
  57.2 0.5 collective-permute-start.6
  57.7 2.1 %collective-permute-start.7 = (f32[64,384]{1,0:T(8,128)S(1)}, f32[64,384]{1,0:T(8,128)S(1)}, u32[]{:S(2)}, u32[]{:S(2)}) collective-permute-start(f32[64,384]{1,0:T(8,128)S(1)} %shard_map.82.own), channel_id=1, source_target_pairs={{0,4},{2,6},{4,0},{6,2},{1,5},{3,7},{5,1},{7,3},{8,12},{10,14},{12... | collective-permute-start | bytes 294920 | tf_op jit(solution)/shard_map/ppermute | solution.py:473
  59.8 0.4 collective-permute-start.8
  60.2 1.1 collective-permute-start.12
  61.3 1.0 shard_map.86
  62.2 3.5 %all-to-all-start.2 = ((f32[4,64,768]{2,1,0:T(8,128)}), f32[4,64,768]{2,1,0:T(8,128)S(1)}, u32[]{:S(2)}, u32[]{:S(2)}) async-start(f32[4,64,768]{2,1,0:T(8,128)} %shard_map.86), calls=%async_computation.2 | async-start | bytes 1572864 | tf_op jit(solution)/shard_map/all_to_all | solution.py:522
  65.7 2.6 %collective-permute-start.4 = (bf16[512,768]{1,0:T(8,128)(2,1)S(1)}, bf16[512,768]{1,0:T(8,128)(2,1)}, u32[]{:S(2)}, u32[]{:S(2)}) collective-permute-start(bf16[512,768]{1,0:T(8,128)(2,1)S(1)} %copy-done), channel_id=1, source_target_pairs={{0,6},{2,0},{4,2},{6,4},{1,7},{3,1},{5,3},{7,5},{8,14},{10,8},{12,... | collective-permute-start | bytes 2359304 | tf_op jit(solution)/shard_map/ppermute | solution.py:473
  68.4 2.3 %collective-permute-start.9 = (f32[64,256]{1,0:T(8,128)S(1)}, f32[64,256]{1,0:T(8,128)S(1)}, u32[]{:S(2)}, u32[]{:S(2)}) collective-permute-start(f32[64,256]{1,0:T(8,128)S(1)} %get-tuple-element.38.half), channel_id=1, source_target_pairs={{0,1},{1,0},{2,3},{3,2},{4,5},{5,4},{6,7},{7,6},{8,9},{9,8},{10,11... | collective-permute-start | bytes 196616 | tf_op jit(solution)/shard_map/ppermute | solution.py:477
  70.7 5.7 %shard_map.84 = (f32[64,64]{1,0:T(8,128)S(1)}, bf16[384,64]{1,0:T(8,128)(2,1)S(1)}) custom-call(f32[64,128]{1,0:T(8,128)S(1)} %get-tuple-element.35.gram, f32[64,384]{1,0:T(8,128)S(1)} %get-tuple-element.36.left), custom_call_target="tpu_custom_call" | custom-call | flops 6000000000 | bytes 1048576 | tf_op jit(solution)/shard_map/pallas_call | solution.py:276
  76.5 13.3 %all-to-all-done.2.terms = f32[4,64,768]{2,1,0:T(8,128)S(1)} async-done(((f32[4,64,768]{2,1,0:T(8,128)}), f32[4,64,768]{2,1,0:T(8,128)S(1)}, u32[]{:S(2)}, u32[]{:S(2)}) %all-to-all-start.2) | async-done | bytes 786464 | tf_op jit(solution)/shard_map/all_to_all | solution.py:522
  89.7 1.2 shard_map.87
  91.0 3.9 %all-to-all-start.3 = ((bf16[32,16,128]{2,1,0:T(8,128)(2,1)}), bf16[32,16,128]{2,1,0:T(8,128)(2,1)S(1)}, u32[]{:S(2)}, u32[]{:S(2)}) async-start(bf16[32,16,128]{2,1,0:T(8,128)(2,1)} %shard_map.87), calls=%async_computation.3 | async-start | bytes 262144 | tf_op jit(solution)/shard_map/all_to_all | solution.py:481
  95.0 1.2 slice.9
  96.2 2.6 %collective-permute-start.11 = (bf16[256,768]{1,0:T(8,128)(2,1)S(1)}, bf16[256,768]{1,0:T(8,128)(2,1)}, u32[]{:S(2)}, u32[]{:S(2)}) collective-permute-start(bf16[256,768]{1,0:T(8,128)(2,1)S(1)} %slice.9), channel_id=1, source_target_pairs={{0,6},{2,0},{4,2},{6,4},{1,7},{3,1},{5,3},{7,5},{8,14},{10,8},{12,... | collective-permute-start | bytes 1179656 | tf_op jit(solution)/shard_map/ppermute | solution.py:473
  98.8 5.5 %all-to-all-done.3.arrived = bf16[32,16,128]{2,1,0:T(8,128)(2,1)S(1)} async-done(((bf16[32,16,128]{2,1,0:T(8,128)(2,1)}), bf16[32,16,128]{2,1,0:T(8,128)(2,1)S(1)}, u32[]{:S(2)}, u32[]{:S(2)}) %all-to-all-start.3) | async-done | bytes 131104 | tf_op jit(solution)/shard_map/all_to_all | solution.py:481
  104.2 0.7 shard_map.89
  104.9 3.9 %all-to-all-start.4 = ((bf16[32,16,128]{2,1,0:T(8,128)(2,1)}), bf16[32,16,128]{2,1,0:T(8,128)(2,1)S(1)}, u32[]{:S(2)}, u32[]{:S(2)}) async-start(bf16[32,16,128]{2,1,0:T(8,128)(2,1)} %shard_map.89), calls=%async_computation.4 | async-start | bytes 262144 | tf_op jit(solution)/shard_map/all_to_all | solution.py:481
  108.8 2.6 %collective-permute-start.18 = (bf16[512,768]{1,0:T(8,128)(2,1)S(1)}, bf16[512,768]{1,0:T(8,128)(2,1)}, u32[]{:S(2)}, u32[]{:S(2)}) collective-permute-start(bf16[512,768]{1,0:T(8,128)(2,1)S(1)} %collective-permute-done.12.rest_4_), channel_id=1, source_target_pairs={{0,1},{1,0},{2,3},{3,2},{4,5},{5,4},{6,7},{7,6},{8,9},{9,8},{10,11... | collective-permute-start | bytes 2359304 | tf_op jit(solution)/shard_map/ppermute | solution.py:477
  111.4 0.1 collective-permute-start.14
  111.5 0.4 collective-permute-start.15
  111.9 6.3 %all-to-all-done.4 = bf16[32,16,128]{2,1,0:T(8,128)(2,1)S(1)} async-done(((bf16[32,16,128]{2,1,0:T(8,128)(2,1)}), bf16[32,16,128]{2,1,0:T(8,128)(2,1)S(1)}, u32[]{:S(2)}, u32[]{:S(2)}) %all-to-all-start.4) | async-done | bytes 131104 | tf_op jit(solution)/shard_map/all_to_all | solution.py:481
  118.3 0.9 collective-permute-start.22
  119.2 2.6 %collective-permute-done.20.b1 = bf16[24,16,128]{2,1,0:T(8,128)(2,1)S(1)} collective-permute-done((bf16[24,16,128]{2,1,0:T(8,128)(2,1)S(1)}, bf16[24,16,128]{2,1,0:T(8,128)(2,1)S(1)}, u32[]{:S(2)}, u32[]{:S(2)}) %collective-permute-start.20) | collective-permute-done | bytes 98336 | tf_op jit(solution)/shard_map/ppermute | solution.py:473
  121.8 1.6 %collective-permute-done.22.b2 = bf16[24,16,128]{2,1,0:T(8,128)(2,1)S(1)} collective-permute-done((bf16[24,16,128]{2,1,0:T(8,128)(2,1)S(1)}, bf16[24,16,128]{2,1,0:T(8,128)(2,1)S(1)}, u32[]{:S(2)}, u32[]{:S(2)}) %collective-permute-start.22) | collective-permute-done | bytes 98336 | tf_op jit(solution)/shard_map/ppermute | solution.py:473
  123.4 4.8 %collective-permute-start.17 = (bf16[256,768]{1,0:T(8,128)(2,1)}, bf16[256,768]{1,0:T(8,128)(2,1)S(1)}, u32[]{:S(2)}, u32[]{:S(2)}) collective-permute-start(bf16[256,768]{1,0:T(8,128)(2,1)} %collective-permute-done.13.rest_3_), channel_id=1, source_target_pairs={{0,1},{1,0},{2,3},{3,2},{4,5},{5,4},{6,7},{7,6},{8,9},{9,8},{10,11... | collective-permute-start | bytes 1179656 | tf_op jit(solution)/shard_map/ppermute | solution.py:477
  128.2 4.2 %collective-permute-start.16 = (bf16[256,768]{1,0:T(8,128)(2,1)}, bf16[256,768]{1,0:T(8,128)(2,1)S(1)}, u32[]{:S(2)}, u32[]{:S(2)}) collective-permute-start(bf16[256,768]{1,0:T(8,128)(2,1)} %collective-permute-done.11.rest_2_), channel_id=1, source_target_pairs={{0,1},{1,0},{2,3},{3,2},{4,5},{5,4},{6,7},{7,6},{8,9},{9,8},{10,11... | collective-permute-start | bytes 1179656 | tf_op jit(solution)/shard_map/ppermute | solution.py:477
  132.5 1.5 collective-permute-done.16.rest_7_
  134.0 0.4 collective-permute-start.21
  134.3 0.1 collective-permute-start.23
  134.5 0.4 collective-permute-start.25
  134.9 7.2 %shard_map.88.fed = bf16[8,384,768]{2,1,0:T(8,128)(2,1)} custom-call(bf16[512,384]{1,0:T(8,128)(2,1)S(1)} %copy-done.1, bf16[384,6144]{1,0:T(8,128)(2,1)} %bitcast.10, bf16[512,768]{1,0:T(8,128)(2,1)} %rest_0_.1, bf16[512,768]{1,0:T(8,128)(2,1)} %collective-permute-done.4.rest_1_, bf16[256,768]{1,0:T(8,128)(2,1)} %collective-permute-done.11.rest_2_, ...), custom_call_target="tpu_custom_call" | custom-call | flops 6000000000 | bytes 1048576 | tf_op jit(solution)/shard_map/pallas_call | solution.py:344
  142.0 2.5 %shard_map.90 = (bf16[1,384,6144]{2,1,0:T(8,128)(2,1)}, bf16[64,6144]{1,0:T(8,128)(2,1)S(1)}, bf16[3,384,768]{2,1,0:T(8,128)(2,1)S(1)}, bf16[4,384,768]{2,1,0:T(8,128)(2,1)S(1)}) custom-call(bf16[8,384,768]{2,1,0:T(8,128)(2,1)} %shard_map.88.fed, bf16[384,64]{1,0:T(8,128)(2,1)S(1)} %get-tuple-element.47.basis, bf16[24,16,128]{2,1,0:T(8,128)(2,1)S(1)} %slice.12.b0), custom_call_target="tpu_custom_call" | custom-call | flops 1000000000 | bytes 1048576 | tf_op jit(solution)/shard_map/pallas_call | solution.py:398
  144.6 1.6 %shard_map.91 = (bf16[1,384,6144]{2,1,0:T(8,128)(2,1)}, bf16[64,6144]{1,0:T(8,128)(2,1)S(1)}) custom-call(bf16[3,384,768]{2,1,0:T(8,128)(2,1)S(1)} %get-tuple-element.49.fed, bf16[384,64]{1,0:T(8,128)(2,1)S(1)} %get-tuple-element.47.basis, bf16[24,16,128]{2,1,0:T(8,128)(2,1)S(1)} %collective-permute-done.20.b1, ...), custom_call_target="tpu_custom_call", output_to_operand_aliasing={{0}: (5, {})} | custom-call | flops 1000000000 | bytes 1048576 | tf_op jit(solution)/shard_map/pallas_call | solution.py:428
  146.2 2.8 %shard_map.92 = (bf16[1,384,6144]{2,1,0:T(8,128)(2,1)}, f32[192,384]{1,0:T(8,128)}, bf16[64,6144]{1,0:T(8,128)(2,1)}) custom-call(bf16[4,384,768]{2,1,0:T(8,128)(2,1)S(1)} %get-tuple-element.48.fed, bf16[384,64]{1,0:T(8,128)(2,1)S(1)} %get-tuple-element.47.basis, ...), custom_call_target="tpu_custom_call", output_to_operand_aliasing={{0}: (7, {})} | custom-call | flops 1000000000 | bytes 1048576 | tf_op jit(solution)/shard_map/pallas_call | solution.py:460
  (44 shorter events, 0.6 us)
Async XLA Ops:
  2.6 4.3 %collective-permute-start = (f32[64,512]{1,0:T(8,128)S(1)}, f32[64,512]{1,0:T(8,128)S(1)}, u32[]{:S(2)}, u32[]{:S(2)}) collective-permute-start(f32[64,512]{1,0:T(8,128)S(1)} %shard_map.76.a), channel_id=1, source_target_pairs={{0,1},{1,0},{2,3},{3,2},{4,5},{5,4},{6,7},{7,6},{8,9},{9,8},{10,11... | collective-permute-start | bytes 393224 | tf_op jit(solution)/shard_map/ppermute | solution.py:477
  6.9 7.1 %collective-permute-start.1 = (bf16[64,512]{1,0:T(8,128)(2,1)S(1)}, bf16[64,512]{1,0:T(8,128)(2,1)S(1)}, u32[]{:S(2)}, u32[]{:S(2)}) collective-permute-start(bf16[64,512]{1,0:T(8,128)(2,1)S(1)} %get-tuple-element.30), channel_id=1, source_target_pairs={{0,2},{2,4},{4,6},{6,0},{1,3},{3,5},{5,7},{7,1},{8,10},{10,12},{12... | collective-permute-start | bytes 196616 | tf_op jit(solution)/shard_map/ppermute | solution.py:473
  7.0 7.1 %collective-permute-start.2 = (bf16[64,512]{1,0:T(8,128)(2,1)S(1)}, bf16[64,512]{1,0:T(8,128)(2,1)S(1)}, u32[]{:S(2)}, u32[]{:S(2)}) collective-permute-start(bf16[64,512]{1,0:T(8,128)(2,1)S(1)} %get-tuple-element.30), channel_id=1, source_target_pairs={{0,4},{2,6},{4,0},{6,2},{1,5},{3,7},{5,1},{7,3},{8,12},{10,14},{12... | collective-permute-start | bytes 196616 | tf_op jit(solution)/shard_map/ppermute | solution.py:473
  9.2 4.9 %collective-permute-start.3 = (bf16[64,512]{1,0:T(8,128)(2,1)S(1)}, bf16[64,512]{1,0:T(8,128)(2,1)S(1)}, u32[]{:S(2)}, u32[]{:S(2)}) collective-permute-start(bf16[64,512]{1,0:T(8,128)(2,1)S(1)} %get-tuple-element.30), channel_id=1, source_target_pairs={{0,6},{2,0},{4,2},{6,4},{1,7},{3,1},{5,3},{7,5},{8,14},{10,8},{12,... | collective-permute-start | bytes 196616 | tf_op jit(solution)/shard_map/ppermute | solution.py:473
  10.3 3.8 %copy-start.1 = (bf16[512,384]{1,0:T(8,128)(2,1)S(1)}, bf16[512,384]{1,0:T(8,128)(2,1)}, u32[]{:S(2)}) copy-start(bf16[512,384]{1,0:T(8,128)(2,1)} %acts.5) | copy-start | bytes 1179652
  47.6 12.6 %copy-start = (bf16[512,768]{1,0:T(8,128)(2,1)S(1)}, bf16[512,768]{1,0:T(8,128)(2,1)}, u32[]{:S(2)}) copy-start(bf16[512,768]{1,0:T(8,128)(2,1)} %rest_0_.1) | copy-start | bytes 2359300
  51.2 10.0 %collective-permute-start.10 = (f32[4,64,768]{2,1,0:T(8,128)S(1)}, f32[4,64,768]{2,1,0:T(8,128)S(1)}, u32[]{:S(2)}, u32[]{:S(2)}) collective-permute-start(f32[4,64,768]{2,1,0:T(8,128)S(1)} %get-tuple-element.41), channel_id=1, source_target_pairs={{0,1},{1,0},{2,3},{3,2},{4,5},{5,4},{6,7},{7,6},{8,9},{9,8},{10,11... | collective-permute-start | bytes 2359304 | tf_op jit(solution)/shard_map/ppermute | solution.py:477
  55.1 2.1 %collective-permute-start.5 = (f32[64,384]{1,0:T(8,128)S(1)}, f32[64,384]{1,0:T(8,128)S(1)}, u32[]{:S(2)}, u32[]{:S(2)}) collective-permute-start(f32[64,384]{1,0:T(8,128)S(1)} %get-tuple-element.34), channel_id=1, source_target_pairs={{0,1},{1,0},{2,3},{3,2},{4,5},{5,4},{6,7},{7,6},{8,9},{9,8},{10,11... | collective-permute-start | bytes 294920 | tf_op jit(solution)/shard_map/ppermute | solution.py:477
  57.2 11.2 %collective-permute-start.6 = (f32[64,384]{1,0:T(8,128)S(1)}, f32[64,384]{1,0:T(8,128)S(1)}, u32[]{:S(2)}, u32[]{:S(2)}) collective-permute-start(f32[64,384]{1,0:T(8,128)S(1)} %shard_map.82.own), channel_id=1, source_target_pairs={{0,2},{2,4},{4,6},{6,0},{1,3},{3,5},{5,7},{7,1},{8,10},{10,12},{12... | collective-permute-start | bytes 294920 | tf_op jit(solution)/shard_map/ppermute | solution.py:473
  57.7 10.7 %collective-permute-start.7 = (f32[64,384]{1,0:T(8,128)S(1)}, f32[64,384]{1,0:T(8,128)S(1)}, u32[]{:S(2)}, u32[]{:S(2)}) collective-permute-start(f32[64,384]{1,0:T(8,128)S(1)} %shard_map.82.own), channel_id=1, source_target_pairs={{0,4},{2,6},{4,0},{6,2},{1,5},{3,7},{5,1},{7,3},{8,12},{10,14},{12... | collective-permute-start | bytes 294920 | tf_op jit(solution)/shard_map/ppermute | solution.py:473
  59.8 8.6 %collective-permute-start.8 = (f32[64,384]{1,0:T(8,128)S(1)}, f32[64,384]{1,0:T(8,128)S(1)}, u32[]{:S(2)}, u32[]{:S(2)}) collective-permute-start(f32[64,384]{1,0:T(8,128)S(1)} %shard_map.82.own), channel_id=1, source_target_pairs={{0,6},{2,0},{4,2},{6,4},{1,7},{3,1},{5,3},{7,5},{8,14},{10,8},{12,... | collective-permute-start | bytes 294920 | tf_op jit(solution)/shard_map/ppermute | solution.py:473
  60.2 34.7 %collective-permute-start.12 = (bf16[512,768]{1,0:T(8,128)(2,1)S(1)}, bf16[512,768]{1,0:T(8,128)(2,1)S(1)}, u32[]{:S(2)}, u32[]{:S(2)}) collective-permute-start(bf16[512,768]{1,0:T(8,128)(2,1)S(1)} %copy-done), channel_id=1, source_target_pairs={{0,2},{2,4},{4,6},{6,0},{1,3},{3,5},{5,7},{7,1},{8,10},{10,12},{12... | collective-permute-start | bytes 2359304 | tf_op jit(solution)/shard_map/ppermute | solution.py:473
  62.2 27.5 %all-to-all-start.2 = ((f32[4,64,768]{2,1,0:T(8,128)}), f32[4,64,768]{2,1,0:T(8,128)S(1)}, u32[]{:S(2)}, u32[]{:S(2)}) async-start(f32[4,64,768]{2,1,0:T(8,128)} %shard_map.86), calls=%async_computation.2 | async-start | bytes 1572864 | tf_op jit(solution)/shard_map/all_to_all | solution.py:522
  65.7 29.3 %collective-permute-start.4 = (bf16[512,768]{1,0:T(8,128)(2,1)S(1)}, bf16[512,768]{1,0:T(8,128)(2,1)}, u32[]{:S(2)}, u32[]{:S(2)}) collective-permute-start(bf16[512,768]{1,0:T(8,128)(2,1)S(1)} %copy-done), channel_id=1, source_target_pairs={{0,6},{2,0},{4,2},{6,4},{1,7},{3,1},{5,3},{7,5},{8,14},{10,8},{12,... | collective-permute-start | bytes 2359304 | tf_op jit(solution)/shard_map/ppermute | solution.py:473
  68.4 8.0 %collective-permute-start.9 = (f32[64,256]{1,0:T(8,128)S(1)}, f32[64,256]{1,0:T(8,128)S(1)}, u32[]{:S(2)}, u32[]{:S(2)}) collective-permute-start(f32[64,256]{1,0:T(8,128)S(1)} %get-tuple-element.38.half), channel_id=1, source_target_pairs={{0,1},{1,0},{2,3},{3,2},{4,5},{5,4},{6,7},{7,6},{8,9},{9,8},{10,11... | collective-permute-start | bytes 196616 | tf_op jit(solution)/shard_map/ppermute | solution.py:477
  91.0 13.3 %all-to-all-start.3 = ((bf16[32,16,128]{2,1,0:T(8,128)(2,1)}), bf16[32,16,128]{2,1,0:T(8,128)(2,1)S(1)}, u32[]{:S(2)}, u32[]{:S(2)}) async-start(bf16[32,16,128]{2,1,0:T(8,128)(2,1)} %shard_map.87), calls=%async_computation.3 | async-start | bytes 262144 | tf_op jit(solution)/shard_map/all_to_all | solution.py:481
  94.8 40.0 %copy-start.3 = (bf16[512,768]{1,0:T(8,128)(2,1)}, bf16[512,768]{1,0:T(8,128)(2,1)S(1)}, u32[]{:S(2)}) copy-start(bf16[512,768]{1,0:T(8,128)(2,1)S(1)} %collective-permute-done.12.rest_4_) | copy-start | bytes 2359300
  94.9 23.3 %collective-permute-start.13 = (bf16[256,768]{1,0:T(8,128)(2,1)S(1)}, bf16[256,768]{1,0:T(8,128)(2,1)}, u32[]{:S(2)}, u32[]{:S(2)}) collective-permute-start(bf16[256,768]{1,0:T(8,128)(2,1)S(1)} %slice.10), channel_id=1, source_target_pairs={{0,2},{2,4},{4,6},{6,0},{1,3},{3,5},{5,7},{7,1},{8,10},{10,12},{12... | collective-permute-start | bytes 1179656 | tf_op jit(solution)/shard_map/ppermute | solution.py:473
  96.2 22.2 %collective-permute-start.11 = (bf16[256,768]{1,0:T(8,128)(2,1)S(1)}, bf16[256,768]{1,0:T(8,128)(2,1)}, u32[]{:S(2)}, u32[]{:S(2)}) collective-permute-start(bf16[256,768]{1,0:T(8,128)(2,1)S(1)} %slice.9), channel_id=1, source_target_pairs={{0,6},{2,0},{4,2},{6,4},{1,7},{3,1},{5,3},{7,5},{8,14},{10,8},{12,... | collective-permute-start | bytes 1179656 | tf_op jit(solution)/shard_map/ppermute | solution.py:473
  104.9 13.3 %all-to-all-start.4 = ((bf16[32,16,128]{2,1,0:T(8,128)(2,1)}), bf16[32,16,128]{2,1,0:T(8,128)(2,1)S(1)}, u32[]{:S(2)}, u32[]{:S(2)}) async-start(bf16[32,16,128]{2,1,0:T(8,128)(2,1)} %shard_map.89), calls=%async_computation.4 | async-start | bytes 262144 | tf_op jit(solution)/shard_map/all_to_all | solution.py:481
  108.8 25.5 %collective-permute-start.18 = (bf16[512,768]{1,0:T(8,128)(2,1)S(1)}, bf16[512,768]{1,0:T(8,128)(2,1)}, u32[]{:S(2)}, u32[]{:S(2)}) collective-permute-start(bf16[512,768]{1,0:T(8,128)(2,1)S(1)} %collective-permute-done.12.rest_4_), channel_id=1, source_target_pairs={{0,1},{1,0},{2,3},{3,2},{4,5},{5,4},{6,7},{7,6},{8,9},{9,8},{10,11... | collective-permute-start | bytes 2359304 | tf_op jit(solution)/shard_map/ppermute | solution.py:477
  111.4 23.1 %collective-permute-start.14 = (bf16[512,768]{1,0:T(8,128)(2,1)S(1)}, bf16[512,768]{1,0:T(8,128)(2,1)}, u32[]{:S(2)}, u32[]{:S(2)}) collective-permute-start(bf16[512,768]{1,0:T(8,128)(2,1)S(1)} %copy-done), channel_id=1, source_target_pairs={{0,1},{1,0},{2,3},{3,2},{4,5},{5,4},{6,7},{7,6},{8,9},{9,8},{10,11... | collective-permute-start | bytes 2359304 | tf_op jit(solution)/shard_map/ppermute | solution.py:477
  111.5 23.4 %collective-permute-start.15 = (bf16[512,768]{1,0:T(8,128)(2,1)}, bf16[512,768]{1,0:T(8,128)(2,1)}, u32[]{:S(2)}, u32[]{:S(2)}) collective-permute-start(bf16[512,768]{1,0:T(8,128)(2,1)} %collective-permute-done.4.rest_1_), channel_id=1, source_target_pairs={{0,1},{1,0},{2,3},{3,2},{4,5},{5,4},{6,7},{7,6},{8,9},{9,8},{10,11... | collective-permute-start | bytes 2359304 | tf_op jit(solution)/shard_map/ppermute | solution.py:477
  118.2 3.5 %collective-permute-start.20 = (bf16[24,16,128]{2,1,0:T(8,128)(2,1)S(1)}, bf16[24,16,128]{2,1,0:T(8,128)(2,1)S(1)}, u32[]{:S(2)}, u32[]{:S(2)}) collective-permute-start(bf16[24,16,128]{2,1,0:T(8,128)(2,1)S(1)} %slice.12.b0), channel_id=1, source_target_pairs={{0,6},{2,0},{4,2},{6,4},{1,7},{3,1},{5,3},{7,5},{8,14},{10,8},{12,... | collective-permute-start | bytes 294920 | tf_op jit(solution)/shard_map/ppermute | solution.py:473
  118.3 5.1 %collective-permute-start.22 = (bf16[24,16,128]{2,1,0:T(8,128)(2,1)S(1)}, bf16[24,16,128]{2,1,0:T(8,128)(2,1)S(1)}, u32[]{:S(2)}, u32[]{:S(2)}) collective-permute-start(bf16[24,16,128]{2,1,0:T(8,128)(2,1)S(1)} %slice.12.b0), channel_id=1, source_target_pairs={{0,4},{2,6},{4,0},{6,2},{1,5},{3,7},{5,1},{7,3},{8,12},{10,14},{12... | collective-permute-start | bytes 294920 | tf_op jit(solution)/shard_map/ppermute | solution.py:473
  121.8 6.4 %collective-permute-start.24 = (bf16[24,16,128]{2,1,0:T(8,128)(2,1)S(1)}, bf16[24,16,128]{2,1,0:T(8,128)(2,1)S(1)}, u32[]{:S(2)}, u32[]{:S(2)}) collective-permute-start(bf16[24,16,128]{2,1,0:T(8,128)(2,1)S(1)} %slice.12.b0), channel_id=1, source_target_pairs={{0,2},{2,4},{4,6},{6,0},{1,3},{3,5},{5,7},{7,1},{8,10},{10,12},{12... | collective-permute-start | bytes 294920 | tf_op jit(solution)/shard_map/ppermute | solution.py:473
  123.4 9.0 %collective-permute-start.17 = (bf16[256,768]{1,0:T(8,128)(2,1)}, bf16[256,768]{1,0:T(8,128)(2,1)S(1)}, u32[]{:S(2)}, u32[]{:S(2)}) collective-permute-start(bf16[256,768]{1,0:T(8,128)(2,1)} %collective-permute-done.13.rest_3_), channel_id=1, source_target_pairs={{0,1},{1,0},{2,3},{3,2},{4,5},{5,4},{6,7},{7,6},{8,9},{9,8},{10,11... | collective-permute-start | bytes 1179656 | tf_op jit(solution)/shard_map/ppermute | solution.py:477
  128.2 5.8 %collective-permute-start.16 = (bf16[256,768]{1,0:T(8,128)(2,1)}, bf16[256,768]{1,0:T(8,128)(2,1)S(1)}, u32[]{:S(2)}, u32[]{:S(2)}) collective-permute-start(bf16[256,768]{1,0:T(8,128)(2,1)} %collective-permute-done.11.rest_2_), channel_id=1, source_target_pairs={{0,1},{1,0},{2,3},{3,2},{4,5},{5,4},{6,7},{7,6},{8,9},{9,8},{10,11... | collective-permute-start | bytes 1179656 | tf_op jit(solution)/shard_map/ppermute | solution.py:477
  132.4 2.5 %copy-start.4 = (bf16[256,768]{1,0:T(8,128)(2,1)}, bf16[256,768]{1,0:T(8,128)(2,1)S(1)}, u32[]{:S(2)}) copy-start(bf16[256,768]{1,0:T(8,128)(2,1)S(1)} %collective-permute-done.17.rest_8_) | copy-start | bytes 1179652
  132.4 13.7 %collective-permute-start.19 = (bf16[24,16,128]{2,1,0:T(8,128)(2,1)S(1)}, bf16[24,16,128]{2,1,0:T(8,128)(2,1)S(1)}, u32[]{:S(2)}, u32[]{:S(2)}) collective-permute-start(bf16[24,16,128]{2,1,0:T(8,128)(2,1)S(1)} %slice.12.b0), channel_id=1, source_target_pairs={{0,1},{1,0},{2,3},{3,2},{4,5},{5,4},{6,7},{7,6},{8,9},{9,8},{10,11... | collective-permute-start | bytes 294920 | tf_op jit(solution)/shard_map/ppermute | solution.py:477
  134.0 0.9 copy-start.5
  134.0 12.2 %collective-permute-start.21 = (bf16[24,16,128]{2,1,0:T(8,128)(2,1)S(1)}, bf16[24,16,128]{2,1,0:T(8,128)(2,1)S(1)}, u32[]{:S(2)}, u32[]{:S(2)}) collective-permute-start(bf16[24,16,128]{2,1,0:T(8,128)(2,1)S(1)} %collective-permute-done.20.b1), channel_id=1, source_target_pairs={{0,1},{1,0},{2,3},{3,2},{4,5},{5,4},{6,7},{7,6},{8,9},{9,8},{10,11... | collective-permute-start | bytes 294920 | tf_op jit(solution)/shard_map/ppermute | solution.py:477
  134.3 11.8 %collective-permute-start.23 = (bf16[24,16,128]{2,1,0:T(8,128)(2,1)S(1)}, bf16[24,16,128]{2,1,0:T(8,128)(2,1)S(1)}, u32[]{:S(2)}, u32[]{:S(2)}) collective-permute-start(bf16[24,16,128]{2,1,0:T(8,128)(2,1)S(1)} %collective-permute-done.22.b2), channel_id=1, source_target_pairs={{0,1},{1,0},{2,3},{3,2},{4,5},{5,4},{6,7},{7,6},{8,9},{9,8},{10,11... | collective-permute-start | bytes 294920 | tf_op jit(solution)/shard_map/ppermute | solution.py:477
  134.5 11.7 %collective-permute-start.25 = (bf16[24,16,128]{2,1,0:T(8,128)(2,1)S(1)}, bf16[24,16,128]{2,1,0:T(8,128)(2,1)S(1)}, u32[]{:S(2)}, u32[]{:S(2)}) collective-permute-start(bf16[24,16,128]{2,1,0:T(8,128)(2,1)S(1)} %collective-permute-done.24.b3), channel_id=1, source_target_pairs={{0,1},{1,0},{2,3},{3,2},{4,5},{5,4},{6,7},{7,6},{8,9},{9,8},{10,11... | collective-permute-start | bytes 294920 | tf_op jit(solution)/shard_map/ppermute | solution.py:477
  144.6 1.6 %copy-start.2 = (f32[384,192]{0,1:T(8,128)S(1)}, f32[384,192]{0,1:T(8,128)}, u32[]{:S(2)}) copy-start(f32[384,192]{0,1:T(8,128)} %param.9) | copy-start | bytes 884740
